TPU v7x, 16 devices: a 4x2x1 block of a 4x4x8 slice. The times are simulated.
16 devices in a mesh: dp: 2 (over y, z), tp: 8 (over x, core).
Axes of the slice: x: 4, y: 2, z: 1, core: 2. Of those that a mesh axis runs over, the one named last changes fastest.
The devices are a block of a 4x4x8 slice.
Arguments:
- x_in: bfloat16 [3072, 3072], P(('dp', 'tp')), parts along dimension 0
- grad_y: bfloat16 [3072, 3072], P(('dp', 'tp')), parts along dimension 0
- norm_gain: float32 [2, 3072], replicated
- w_qkv: bfloat16 [2, 3072, 5120], P(None, None, 'tp')
- w_out: bfloat16 [2, 3072, 3072], P(None, 'tp')
- w_gate: bfloat16 [2, 3072, 8192], P(None, None, 'tp')
- w_up: bfloat16 [2, 3072, 8192], P(None, None, 'tp')
- w_down: bfloat16 [2, 8192, 3072], P(None, 'tp')
Outputs:
- output 1: bfloat16 [3072, 3072], P(('dp', 'tp')), parts along dimension 0
- output 2: float32 [4, 3072], P('dp'), parts along dimension 0
- output 3: bfloat16 [4, 3072, 5120], P('dp', None, 'tp'), parts along dimension 0
- output 4: bfloat16 [4, 3072, 3072], P('dp', 'tp'), parts along dimension 0
- output 5: bfloat16 [4, 3072, 8192], P('dp', None, 'tp'), parts along dimension 0
- output 6: bfloat16 [4, 3072, 8192], P('dp', None, 'tp'), parts along dimension 0
- output 7: bfloat16 [4, 8192, 3072], P('dp', 'tp'), parts along dimension 0
There are 2 independent parts. A program takes and returns all parts, laid end to end along the dimension named above; an argument that names none is the same for every part.
All inputs are finite; a program needn't handle non-finite values.
Results may differ from a plain program's by a relative error of at most 0.0172757.
Values are sent between devices in bfloat16 or wider.
A program may use at most 768 MiB of HBM per device.

v0:
```python
import jax
import jax.numpy as jnp
from jax import lax
from jax.sharding import PartitionSpec as P

HEAD_DIM = 128
NORM_EPS = 1e-5
ROPE_BASE = 10000.0


def rope_tables(seq_len):
    half_dim = HEAD_DIM // 2
    freqs = ROPE_BASE ** (-2.0 * jnp.arange(half_dim, dtype=jnp.float32) / HEAD_DIM)
    angles = jnp.arange(seq_len, dtype=jnp.float32)[:, None] * freqs[None, :]
    return jnp.cos(angles)[:, None, None, :], jnp.sin(angles)[:, None, None, :]


def rotate(values, cos_tab, sin_tab):
    half_dim = values.shape[-1] // 2
    lower_half = values[..., :half_dim]
    upper_half = values[..., half_dim:]
    return jnp.concatenate([lower_half * cos_tab - upper_half * sin_tab, upper_half * cos_tab + lower_half * sin_tab], axis=-1)


def rms_scale(x_f32, gain_row):
    inv_rms = lax.rsqrt(jnp.mean(x_f32 * x_f32, axis=-1, keepdims=True) + NORM_EPS)
    return x_f32 * inv_rms * gain_row


def gated(gate_f32, up_f32):
    return jax.nn.silu(gate_f32) * up_f32


def causal_scores(query, keys_rot):
    seq_len = query.shape[0]
    causal = jnp.arange(seq_len)[:, None] >= jnp.arange(seq_len)[None, :]
    scores = jnp.einsum('skgd,tkd->kgst', query, keys_rot, preferred_element_type=jnp.float32) * HEAD_DIM ** -0.5
    return jnp.where(causal, scores, -1e30)


def block_forward(x_loc, gain_row, w_qkv_l, w_out_l, w_gate_l, w_up_l, w_down_l, cos_tab, sin_tab, with_output):
    seq_len = cos_tab.shape[0]
    heads_local = w_out_l.shape[0] // HEAD_DIM
    kv_local = (w_qkv_l.shape[1] // HEAD_DIM - heads_local) // 2
    group_size = heads_local // kv_local
    x_f32 = x_loc.astype(jnp.float32)
    u_loc = rms_scale(x_f32, gain_row).astype(jnp.bfloat16)
    u_full = lax.all_gather(u_loc, 'tp', axis=0, tiled=True)
    qkv_all = jnp.dot(u_full, w_qkv_l, preferred_element_type=jnp.float32).astype(jnp.bfloat16).reshape(seq_len, kv_local, group_size + 2, HEAD_DIM)
    rotated = rotate(qkv_all[:, :, :group_size + 1].astype(jnp.float32), cos_tab, sin_tab).astype(jnp.bfloat16)
    query = rotated[:, :, :group_size]
    keys_rot = rotated[:, :, group_size]
    values_v = qkv_all[:, :, group_size + 1]
    scores = causal_scores(query, keys_rot)
    row_max = jnp.max(scores, axis=-1, keepdims=True)
    log_norm = row_max + jnp.log(jnp.sum(jnp.exp(scores - row_max), axis=-1, keepdims=True))
    attn_prob = jnp.exp(scores - log_norm).astype(jnp.bfloat16)
    attn_out = jnp.einsum('kgst,tkd->skgd', attn_prob, values_v, preferred_element_type=jnp.float32).astype(jnp.bfloat16).reshape(seq_len, heads_local * HEAD_DIM)
    gate_act = jnp.dot(u_full, w_gate_l, preferred_element_type=jnp.float32).astype(jnp.bfloat16)
    up_act = jnp.dot(u_full, w_up_l, preferred_element_type=jnp.float32).astype(jnp.bfloat16)
    saved = {'x_loc': x_loc, 'u_loc': u_loc, 'query': query, 'keys_rot': keys_rot, 'values_v': values_v, 'attn_out': attn_out, 'log_norm': log_norm, 'gate_act': gate_act, 'up_act': up_act}
    if not with_output:
        return None, saved
    hidden = gated(gate_act.astype(jnp.float32), up_act.astype(jnp.float32)).astype(jnp.bfloat16)
    block_part = jnp.dot(attn_out, w_out_l, preferred_element_type=jnp.float32) + jnp.dot(hidden, w_down_l, preferred_element_type=jnp.float32)
    y_loc = (x_f32 + lax.psum_scatter(block_part, 'tp', scatter_dimension=0, tiled=True)).astype(jnp.bfloat16)
    return y_loc, saved


def block_backward(dy_loc, saved, gain_row, w_qkv_l, w_out_l, w_gate_l, w_up_l, w_down_l, cos_tab, sin_tab):
    saved, dy_loc = lax.optimization_barrier((saved, dy_loc))
    query = saved['query']
    keys_rot = saved['keys_rot']
    values_v = saved['values_v']
    seq_len, kv_local, group_size = query.shape[0], query.shape[1], query.shape[2]
    u_full = lax.all_gather(saved['u_loc'], 'tp', axis=0, tiled=True)
    dy_full = lax.all_gather(dy_loc, 'tp', axis=0, tiled=True)
    grad_out_l = jnp.einsum('sh,sd->hd', saved['attn_out'], dy_full, preferred_element_type=jnp.float32).astype(jnp.bfloat16)
    d_attn = jnp.einsum('sd,hd->sh', dy_full, w_out_l, preferred_element_type=jnp.float32).astype(jnp.bfloat16).reshape(seq_len, kv_local, group_size, HEAD_DIM)
    hidden_f32, gated_pull = jax.vjp(gated, saved['gate_act'].astype(jnp.float32), saved['up_act'].astype(jnp.float32))
    hidden = hidden_f32.astype(jnp.bfloat16)
    grad_down_l = jnp.einsum('sf,sd->fd', hidden, dy_full, preferred_element_type=jnp.float32).astype(jnp.bfloat16)
    d_hidden = jnp.einsum('sd,fd->sf', dy_full, w_down_l, preferred_element_type=jnp.float32).astype(jnp.bfloat16)
    d_gate_f32, d_up_f32 = gated_pull(d_hidden.astype(jnp.float32))
    d_gate = d_gate_f32.astype(jnp.bfloat16)
    d_up = d_up_f32.astype(jnp.bfloat16)
    grad_gate_l = jnp.einsum('sd,sf->df', u_full, d_gate, preferred_element_type=jnp.float32).astype(jnp.bfloat16)
    grad_up_l = jnp.einsum('sd,sf->df', u_full, d_up, preferred_element_type=jnp.float32).astype(jnp.bfloat16)
    attn_prob_f32 = jnp.exp(causal_scores(query, keys_rot) - saved['log_norm'])
    attn_prob = attn_prob_f32.astype(jnp.bfloat16)
    d_values = jnp.einsum('kgst,skgd->tkd', attn_prob, d_attn, preferred_element_type=jnp.float32).astype(jnp.bfloat16)
    d_prob = jnp.einsum('skgd,tkd->kgst', d_attn, values_v, preferred_element_type=jnp.float32).astype(jnp.bfloat16).astype(jnp.float32)
    d_scores = (attn_prob_f32 * (d_prob - jnp.sum(attn_prob_f32 * d_prob, axis=-1, keepdims=True)) * HEAD_DIM ** -0.5).astype(jnp.bfloat16)
    d_query = jnp.einsum('kgst,tkd->skgd', d_scores, keys_rot, preferred_element_type=jnp.float32).astype(jnp.bfloat16)
    d_keys = jnp.einsum('kgst,skgd->tkd', d_scores, query, preferred_element_type=jnp.float32).astype(jnp.bfloat16)
    d_rotated = jnp.concatenate([d_query, d_keys[:, :, None]], axis=2).astype(jnp.float32)
    d_unrotated = rotate(d_rotated, cos_tab, -sin_tab).astype(jnp.bfloat16)
    d_qkv = jnp.concatenate([d_unrotated, d_values[:, :, None]], axis=2).reshape(seq_len, w_qkv_l.shape[1])
    grad_qkv_l = jnp.einsum('sd,sc->dc', u_full, d_qkv, preferred_element_type=jnp.float32).astype(jnp.bfloat16)
    normed_part = jnp.einsum('sc,dc->sd', d_qkv, w_qkv_l, preferred_element_type=jnp.float32) + jnp.einsum('sf,df->sd', d_gate, w_gate_l, preferred_element_type=jnp.float32) + jnp.einsum('sf,df->sd', d_up, w_up_l, preferred_element_type=jnp.float32)
    d_normed = lax.psum_scatter(normed_part, 'tp', scatter_dimension=0, tiled=True).astype(jnp.bfloat16)
    norm_pull = jax.vjp(rms_scale, saved['x_loc'].astype(jnp.float32), gain_row)[1]
    d_x_norm, grad_gain_l = norm_pull(d_normed.astype(jnp.float32))
    grad_x_loc = (dy_loc.astype(jnp.float32) + d_x_norm).astype(jnp.bfloat16)
    return grad_x_loc, grad_gain_l, grad_qkv_l, grad_out_l, grad_gate_l, grad_up_l, grad_down_l


def solution(mesh):
    tp_size = mesh.shape['tp']
    row_spec = P(('dp', 'tp'), None)
    col_spec = P(None, None, 'tp')
    inner_spec = P(None, 'tp', None)

    def device_program(x_loc, dy_loc, norm_gain, w_qkv, w_out, w_gate, w_up, w_down):
        n_layers = w_qkv.shape[0]
        cos_tab, sin_tab = rope_tables(x_loc.shape[0] * tp_size)
        saved_all = []
        x_cur = x_loc
        for layer_idx in range(n_layers):
            x_cur, saved = block_forward(x_cur, norm_gain[layer_idx], w_qkv[layer_idx], w_out[layer_idx], w_gate[layer_idx], w_up[layer_idx], w_down[layer_idx], cos_tab, sin_tab, layer_idx < n_layers - 1)
            saved_all.append(saved)
        grad_cur = dy_loc
        layer_grads = []
        for layer_idx in reversed(range(n_layers)):
            results = block_backward(grad_cur, saved_all[layer_idx], norm_gain[layer_idx], w_qkv[layer_idx], w_out[layer_idx], w_gate[layer_idx], w_up[layer_idx], w_down[layer_idx], cos_tab, sin_tab)
            grad_cur = results[0]
            layer_grads.insert(0, results[1:])
        grad_gain = lax.psum(jnp.stack([item[0] for item in layer_grads]), 'tp')
        stacked = [jnp.stack([item[grad_idx] for item in layer_grads]) for grad_idx in range(1, 6)]
        return (grad_cur, grad_gain, stacked[0], stacked[1], stacked[2], stacked[3], stacked[4])

    return jax.shard_map(device_program, mesh=mesh, in_specs=(row_spec, row_spec, P(None, None), col_spec, inner_spec, col_spec, col_spec, inner_spec), out_specs=(row_spec, P('dp', None), P('dp', None, 'tp'), P('dp', 'tp', None), P('dp', None, 'tp'), P('dp', None, 'tp'), P('dp', 'tp', None)), check_vma=False)
```

profile of v0, /device:TPU:112, one launch (start us, length us, event | category | flops | bytes accessed | tf_op | source)
XLA Modules:
  0.0 1179.3 jit_solution(15559337251822555766)
XLA Ops:
  17.0 48.3 %all-gather.7.cloned.1.call-done = bf16[1536,3072]{1,0:T(8,128)(2,1)} async-done(((bf16[192,3072]{1,0:T(8,128)(2,1)}), bf16[1536,3072]{1,0:T(8,128)(2,1)}) %all-gather.7.cloned.1.call-update) | async-done | bytes 9437200 | tf_op jit(solution)/shard_map/all_gather | solution.py:48
  138.5 15.2 %fusion.101 = bf16[1536,1024]{1,0:T(8,128)(2,1)S(1)} fusion(bf16[1536,3072]{1,0:T(8,128)(2,1)} %all-gather.7.cloned.1.call-done, bf16[2,3072,1024]{2,1,0:T(8,128)(2,1)} %param.14), kind=kOutput, calls=%fused_computation.152 | convolution fusion | flops 9665249280 | bytes 18874368 | tf_op jit(solution)/shard_map/dot_general | solution.py:60
  153.7 18.0 %fusion.65 = f32[1536,3072]{1,0:T(8,128)} fusion(bf16[2,1024,3072]{2,1,0:T(8,128)(2,1)} %param.15, bf16[1536,1024]{1,0:T(8,128)(2,1)S(1)} %fusion.101, bf16[1536,1024]{1,0:T(8,128)(2,1)S(1)} %fusion.98), kind=kOutput, calls=%fused_computation.99 | convolution fusion | flops 9676259328 | bytes 31457280 | tf_op jit(solution)/shard_map/dot_general | solution.py:65
  184.8 98.0 %reduce-scatter.4.cloned.1.call-done = f32[192,3072]{1,0:T(8,128)} async-done(((f32[1536,3072]{1,0:T(8,128)}), f32[192,3072]{1,0:T(8,128)}) %reduce-scatter.4.cloned.1.call-update) | async-done | bytes 2359312 | tf_op jit(solution)/shard_map/reduce_scatter | solution.py:66
  287.4 49.6 %all-gather.9.cloned.1.call-done = bf16[1536,3072]{1,0:T(8,128)(2,1)} async-done(((bf16[192,3072]{1,0:T(8,128)(2,1)}), bf16[1536,3072]{1,0:T(8,128)(2,1)}) %all-gather.9.cloned.1.call-update) | async-done | bytes 9437200 | tf_op jit(solution)/shard_map/all_gather | solution.py:48
  399.0 15.4 %fusion.107 = bf16[1536,1024]{1,0:T(8,128)(2,1)} fusion(bf16[1536,3072]{1,0:T(8,128)(2,1)} %all-gather.9.cloned.1.call-done, bf16[2,3072,1024]{2,1,0:T(8,128)(2,1)} %param.13), kind=kOutput, calls=%fused_computation.154 | convolution fusion | flops 9665249280 | bytes 18874368 | tf_op jit(solution)/shard_map/dot_general | solution.py:59
  414.4 15.4 %fusion.110 = bf16[1536,1024]{1,0:T(8,128)(2,1)} fusion(bf16[1536,3072]{1,0:T(8,128)(2,1)} %all-gather.9.cloned.1.call-done, bf16[2,3072,1024]{2,1,0:T(8,128)(2,1)} %param.14), kind=kOutput, calls=%fused_computation.155 | convolution fusion | flops 9665249280 | bytes 18874368 | tf_op jit(solution)/shard_map/dot_general | solution.py:60
  430.0 50.2 %all-gather.11.cloned.1.call-done = bf16[1536,3072]{1,0:T(8,128)(2,1)} async-done(((bf16[192,3072]{1,0:T(8,128)(2,1)}), bf16[1536,3072]{1,0:T(8,128)(2,1)}) %all-gather.11.cloned.1.call-update) | async-done | bytes 9437200 | tf_op jit(solution)/shard_map/all_gather | solution.py:77
  495.9 19.6 %fusion.12 = (f32[3,1536]{1,0:T(4,128)}, f32[1,3,1536,1536]{2,3,1,0:T(8,128)}) fusion(bf16[1536,1536,3]{1,0,2:T(8,128)(2,1)} %convolution_convert_fusion.1, f32[3,1536]{1,0:T(4,128)} %copy-done.31, bf16[1536,1,3,128]{3,0,2,1:T(8,128)(2,1)} %copy-done.23, bf16[1536,1,128]{2,0,1:T(8,128)(2,1)S(1)} %bitcast.423, pred[1536,1536]{0,1:T(8,128)(4,1)S(1)} %iota_compare_fusion), kind=kOutput, calls=%fused_computation.18 | convolution fusion | flops 1854402048 | bytes 46436352 | tf_op jit(solution)/shard_map/skgd,tkd->kgst/dot_general | solution.py:37
  597.0 21.6 %fusion.59 = f32[1536,3072]{1,0:T(8,128)} fusion(bf16[2,3072,1024]{2,1,0:T(8,128)(2,1)} %param.13, bf16[1536,1024]{1,0:T(8,128)(2,1)} %fusion.107, bf16[1536,1024]{1,0:T(8,128)(2,1)} %fusion.110, bf16[1536,1024]{1,0:T(8,128)(2,1)} %fusion.113), kind=kOutput, calls=%fused_computation.93 | convolution fusion | flops 9685696512 | bytes 34603008 | tf_op jit(solution)/shard_map/sf,df->sd/dot_general | solution.py:100
  618.6 27.4 %add_add_fusion.1 = f32[1536,3072]{1,0:T(8,128)} fusion(f32[1536,3072]{1,0:T(8,128)} %fusion.88, f32[1536,3072]{1,0:T(8,128)} %fusion.59, bf16[2,3072,1024]{2,1,0:T(8,128)(2,1)} %param.14, bf16[1536,1024]{1,0:T(8,128)(2,1)} %fusion.113, bf16[1536,1024]{1,0:T(8,128)(2,1)} %fusion.107), kind=kOutput, calls=%fused_computation.29 | convolution fusion | flops 9685696512 | bytes 69206016 | tf_op jit(solution)/shard_map/sf,df->sd/dot_general | solution.py:100
  648.9 95.2 %reduce-scatter.6.cloned.1.call-done = f32[192,3072]{1,0:T(8,128)} async-done(((f32[1536,3072]{1,0:T(8,128)}), f32[192,3072]{1,0:T(8,128)}) %reduce-scatter.6.cloned.1.call-update) | async-done | bytes 2359312 | tf_op jit(solution)/shard_map/reduce_scatter | solution.py:101
  753.8 48.0 %all-gather.13.cloned.1.call-done = bf16[1536,3072]{1,0:T(8,128)(2,1)} async-done(((bf16[192,3072]{1,0:T(8,128)(2,1)}), bf16[1536,3072]{1,0:T(8,128)(2,1)}) %all-gather.13.cloned.1.call-update) | async-done | bytes 9437200 | tf_op jit(solution)/shard_map/all_gather | solution.py:77
  818.5 18.7 %fusion.6 = (f32[3,1536]{1,0:T(4,128)}, f32[1,3,1536,1536]{2,3,1,0:T(8,128)}) fusion(bf16[1536,1536,3]{1,0,2:T(8,128)(2,1)} %convolution_convert_fusion, f32[3,1536]{1,0:T(4,128)} %copy-done.30, bf16[1536,1,3,128]{3,0,2,1:T(8,128)(2,1)} %copy-done.21, bf16[1536,1,128]{2,0,1:T(8,128)(2,1)} %bitcast.421, pred[1536,1536]{0,1:T(8,128)(4,1)S(1)} %iota_compare_fusion), kind=kOutput, calls=%fused_computation.11 | convolution fusion | flops 1854402048 | bytes 46436352 | tf_op jit(solution)/shard_map/skgd,tkd->kgst/dot_general | solution.py:37
  837.2 20.2 %fusion.21 = bf16[3,1536,1536]{1,2,0:T(8,128)(2,1)} fusion(f32[1,3,1536,1536]{2,3,1,0:T(8,128)} %get-tuple-element.73, bf16[1536,1536,3]{1,0,2:T(8,128)(2,1)} %convolution_convert_fusion, f32[3,1536]{1,0:T(4,128)} %get-tuple-element.72), kind=kLoop, calls=%fused_computation.33 | loop fusion | flops 35389440 | bytes 56641536 | tf_op jit(solution)/shard_map/reshape.68
  908.9 15.8 %fusion.104 = bf16[1536,1024]{1,0:T(8,128)(2,1)} fusion(bf16[1536,3072]{1,0:T(8,128)(2,1)} %all-gather.13.cloned.1.call-done, bf16[2,1024,3072]{2,1,0:T(8,128)(2,1)} %param.15), kind=kOutput, calls=%fused_computation.153 | convolution fusion | flops 9665249280 | bytes 18874368 | tf_op jit(solution)/shard_map/sd,fd->sf/dot_general | solution.py:83
  924.7 17.8 %fusion.70 = f32[1536,3072]{1,0:T(8,128)} fusion(bf16[2,3072,1024]{2,1,0:T(8,128)(2,1)S(1)} %bitcast.436, bf16[1536,1024]{1,0:T(8,128)(2,1)} %copy-done.35, bf16[1536,1024]{1,0:T(8,128)(2,1)} %copy-done.38, bf16[1536,1024]{1,0:T(8,128)(2,1)} %fusion.104), kind=kOutput, calls=%fused_computation.104 | convolution fusion | flops 9685696512 | bytes 34603008 | tf_op jit(solution)/shard_map/sf,df->sd/dot_general | solution.py:100
  942.6 27.1 %add_add_fusion = f32[1536,3072]{1,0:T(8,128)} fusion(f32[1536,3072]{1,0:T(8,128)} %fusion.92, f32[1536,3072]{1,0:T(8,128)} %fusion.70, bf16[2,3072,1024]{2,1,0:T(8,128)(2,1)} %param.14, bf16[1536,1024]{1,0:T(8,128)(2,1)} %fusion.104, bf16[1536,1024]{1,0:T(8,128)(2,1)} %copy-done.35), kind=kOutput, calls=%fused_computation.28 | convolution fusion | flops 9685696512 | bytes 69206016 | tf_op jit(solution)/shard_map/sf,df->sd/dot_general | solution.py:100
  979.1 16.1 %convert_bitcast_fusion.2 = bf16[1,1024,3072]{2,1,0:T(8,128)(2,1)} fusion(bf16[1536,3072]{1,0:T(8,128)(2,1)} %all-gather.11.cloned.1.call-done, bf16[1536,1024]{1,0:T(8,128)(2,1)S(1)} %copy-done.39, bf16[1536,1024]{1,0:T(8,128)(2,1)S(1)} %copy-done.37), kind=kOutput, calls=%fused_computation.108 | convolution fusion | flops 9679405056 | bytes 22020096 | tf_op jit(solution)/shard_map/sf,sd->fd/dot_general | solution.py:82
  1007.4 16.0 %convert_bitcast_fusion.6 = bf16[1,3072,1024]{2,1,0:T(8,128)(2,1)} fusion(bf16[1536,3072]{1,0:T(8,128)(2,1)S(1)} %copy-done.33, bf16[1536,1024]{1,0:T(8,128)(2,1)} %fusion.107, bf16[1536,1024]{1,0:T(8,128)(2,1)} %fusion.110, bf16[1536,1024]{1,0:T(8,128)(2,1)} %fusion.113), kind=kOutput, calls=%fused_computation.112 | convolution fusion | flops 9688842240 | bytes 25165824 | tf_op jit(solution)/shard_map/sd,sf->df/dot_general | solution.py:87
  1065.0 17.5 %convert_bitcast_fusion.3 = bf16[1,1024,3072]{2,1,0:T(8,128)(2,1)} fusion(bf16[1536,3072]{1,0:T(8,128)(2,1)} %all-gather.13.cloned.1.call-done, bf16[1536,1024]{1,0:T(8,128)(2,1)} %copy-done.38, bf16[1536,1024]{1,0:T(8,128)(2,1)} %copy-done.35), kind=kOutput, calls=%fused_computation.109 | convolution fusion | flops 9679405056 | bytes 22020096 | tf_op jit(solution)/shard_map/sf,sd->fd/dot_general | solution.py:82
  1093.1 18.2 %convert_bitcast_fusion.7 = bf16[1,3072,1024]{2,1,0:T(8,128)(2,1)} fusion(bf16[1536,3072]{1,0:T(8,128)(2,1)} %all-gather.15.cloned.1.call-done, bf16[1536,1024]{1,0:T(8,128)(2,1)} %copy-done.35, bf16[1536,1024]{1,0:T(8,128)(2,1)} %copy-done.38, bf16[1536,1024]{1,0:T(8,128)(2,1)} %fusion.104), kind=kOutput, calls=%fused_computation.113 | convolution fusion | flops 9688842240 | bytes 25165824 | tf_op jit(solution)/shard_map/sd,sf->df/dot_general | solution.py:87
  1111.3 15.6 %convert_bitcast_fusion.5 = bf16[1,3072,1024]{2,1,0:T(8,128)(2,1)} fusion(bf16[1536,3072]{1,0:T(8,128)(2,1)} %all-gather.15.cloned.1.call-done, bf16[1536,1024]{1,0:T(8,128)(2,1)} %fusion.104, bf16[1536,1024]{1,0:T(8,128)(2,1)S(1)} %copy-done.36), kind=kOutput, calls=%fused_computation.111 | convolution fusion | flops 9679405056 | bytes 22020096 | tf_op jit(solution)/shard_map/sd,sf->df/dot_general | solution.py:88
  1144.1 24.8 %psum.7 = f32[2,3072]{1,0:T(2,128)} all-reduce(f32[2,3072]{1,0:T(2,128)S(1)} %pad_maximum_fusion.11), channel_id=1, replica_groups=mesh['dp'=2,'tp'=8] {'tp'}, use_global_device_ids=true, to_apply=%region_17.18 | all-reduce | flops 6144 | bytes 49152 | tf_op jit(solution)/shard_map/psum | solution.py:128
  (220 shorter events, 434.2 us)
Async XLA Ops:
  7.2 58.1 %all-gather.7.cloned.1.call-start = ((), (), s32[]{:S(2)}) async-start(), calls=%async_computation.3 | async-start | bytes 10616832 | tf_op jit(solution)/shard_map/all_gather | solution.py:48
  8.1 276.8 %copy-start.27 = (f32[1,3072]{1,0:T(1,128)}, f32[1,3072]{1,0:T(1,128)S(1)}, u32[]{:S(2)}) copy-start(f32[1,3072]{1,0:T(1,128)S(1)} %get-tuple-element.61) | copy-start | bytes 36868
  12.4 270.3 %reduce-scatter.4.cloned.1.call-start = ((), (), s32[]{:S(2)}) async-start(), calls=%async_computation.4 | async-start | bytes 21233664 | tf_op jit(solution)/shard_map/reduce_scatter | solution.py:66
  16.3 65.9 %copy-start.5 = (f32[1536,64]{1,0:T(8,128)}, f32[1536,64]{1,0:T(8,128)S(1)}, u32[]{:S(2)}) copy-start(f32[1536,64]{1,0:T(8,128)S(1)} %get-tuple-element.65) | copy-start | bytes 1179652
  124.0 47.7 %copy-start.12 = (bf16[128,3,1536]{2,0,1:T(8,128)(2,1)}, bf16[128,3,1536]{2,0,1:T(8,128)(2,1)S(1)}, u32[]{:S(2)}) copy-start(bf16[128,3,1536]{2,0,1:T(8,128)(2,1)S(1)} %fusion.132) | copy-start | bytes 3538948
  138.4 33.3 %slice-start.6 = ((s8[4718592]{0:T(1024)(128)(4,1)}), s8[4194304]{0:T(1024)(128)(4,1)S(1)}, s32[]{:S(2)}) async-start(s8[4718592]{0:T(1024)(128)(4,1)} %bitcast.425), calls=%async_computation.18 | async-start | bytes 8388608
  184.6 98.1 %copy-start.1 = (bf16[192,3072]{1,0:T(8,128)(2,1)S(1)}, bf16[192,3072]{1,0:T(8,128)(2,1)}, u32[]{:S(2)}) copy-start(bf16[192,3072]{1,0:T(8,128)(2,1)} %param.8) | copy-start | bytes 3538948
  184.7 152.4 %all-gather.9.cloned.1.call-start = ((), (), s32[]{:S(2)}) async-start(), calls=%async_computation.5 | async-start | bytes 10616832 | tf_op jit(solution)/shard_map/all_gather | solution.py:48
  287.4 192.8 %all-gather.11.cloned.1.call-start = ((), (), s32[]{:S(2)}) async-start(), calls=%async_computation.6 | async-start | bytes 10616832 | tf_op jit(solution)/shard_map/all_gather | solution.py:77
  357.3 138.6 %copy-start.18 = (bf16[1536,1,1,128]{3,0,2,1:T(8,128)(2,1)}, bf16[1536,1,1,128]{3,0,2,1:T(8,128)(2,1)S(1)}, u32[]{:S(2)}) copy-start(bf16[1536,1,1,128]{3,0,2,1:T(8,128)(2,1)S(1)} %pad_maximum_fusion.9) | copy-start | bytes 1179652
  429.9 314.2 %reduce-scatter.6.cloned.1.call-start = ((), (), s32[]{:S(2)}) async-start(), calls=%async_computation.7 | async-start | bytes 21233664 | tf_op jit(solution)/shard_map/reduce_scatter | solution.py:101
  646.0 98.1 %copy-start.28 = (f32[1,3072]{1,0:T(1,128)S(1)}, f32[1,3072]{1,0:T(1,128)}, u32[]{:S(2)}) copy-start(f32[1,3072]{1,0:T(1,128)} %copy-done.27) | copy-start | bytes 36868
  646.1 155.7 %all-gather.13.cloned.1.call-start = ((), (), s32[]{:S(2)}) async-start(), calls=%async_computation.8 | async-start | bytes 10616832 | tf_op jit(solution)/shard_map/all_gather | solution.py:77
  752.1 243.0 %all-gather.17.cloned.1.call-start = ((), (), s32[]{:S(2)}) async-start(), calls=%async_computation.11 | async-start | bytes 10616832 | tf_op jit(solution)/shard_map/all_gather | solution.py:76
  752.9 292.5 %all-gather.15.cloned.1.call-start = ((), (), s32[]{:S(2)}) async-start(), calls=%async_computation.10 | async-start | bytes 10616832 | tf_op jit(solution)/shard_map/all_gather | solution.py:76
  753.7 387.5 %reduce-scatter.8.cloned.1.call-start = ((), (), s32[]{:S(2)}) async-start(), calls=%async_computation.9 | async-start | bytes 21233664 | tf_op jit(solution)/shard_map/reduce_scatter | solution.py:101
  895.0 29.7 %slice-start.9 = ((s8[12582912]{0:T(1024)(128)(4,1)}), s8[4194304]{0:T(1024)(128)(4,1)S(1)}, s32[]{:S(2)}) async-start(s8[12582912]{0:T(1024)(128)(4,1)} %bitcast.435), calls=%async_computation.21 | async-start | bytes 8388608
  1007.4 31.2 %slice-start.14 = ((s8[9437184]{0:T(1024)(128)(4,1)}), s8[1048576]{0:T(1024)(128)(4,1)S(1)}, s32[]{:S(2)}) async-start(s8[9437184]{0:T(1024)(128)(4,1)} %bitcast.439), calls=%async_computation.26 | async-start | bytes 2097152
  1007.4 31.2 %slice-start.15 = ((s8[9437184]{0:T(1024)(128)(4,1)}), s8[4194304]{0:T(1024)(128)(4,1)S(1)}, s32[]{:S(2)}) async-start(s8[9437184]{0:T(1024)(128)(4,1)} %bitcast.439), calls=%async_computation.27 | async-start | bytes 8388608
  1082.6 44.3 %slice-start = ((s8[6291456]{0:T(1024)(128)(4,1)}), s8[4194304]{0:T(1024)(128)(4,1)S(1)}, s32[]{:S(2)}) async-start(s8[6291456]{0:T(1024)(128)(4,1)} %bitcast.403), calls=%async_computation.12 | async-start | bytes 8388608
  1082.6 44.3 %slice-start.2 = ((s8[6291456]{0:T(1024)(128)(4,1)}), s8[4194304]{0:T(1024)(128)(4,1)S(1)}, s32[]{:S(2)}) async-start(s8[6291456]{0:T(1024)(128)(4,1)} %bitcast.405), calls=%async_computation.14 | async-start | bytes 8388608
  1093.1 33.8 %slice-start.1 = ((s8[6291456]{0:T(1024)(128)(4,1)}), s8[2097152]{0:T(1024)(128)(4,1)S(1)}, s32[]{:S(2)}) async-start(s8[6291456]{0:T(1024)(128)(4,1)} %bitcast.403), calls=%async_computation.13 | async-start | bytes 4194304
  1093.1 33.8 %slice-start.3 = ((s8[6291456]{0:T(1024)(128)(4,1)}), s8[2097152]{0:T(1024)(128)(4,1)S(1)}, s32[]{:S(2)}) async-start(s8[6291456]{0:T(1024)(128)(4,1)} %bitcast.405), calls=%async_computation.15 | async-start | bytes 4194304
  1126.9 42.0 %copy-start.8 = (bf16[192,3072]{1,0:T(8,128)(2,1)S(1)}, bf16[192,3072]{1,0:T(8,128)(2,1)}, u32[]{:S(2)}) copy-start(bf16[192,3072]{1,0:T(8,128)(2,1)} %fusion.164) | copy-start | bytes 3538948
  (42 other events, 493.7 us)
Sparse Core Ops, SparseCore 0:
  12.6 52.7 all-gather.6
  184.8 97.8 reduce-scatter.3
  287.5 49.5 all-gather.8
  430.0 50.1 all-gather.10
  646.2 97.8 reduce-scatter.5
  752.2 49.5 all-gather.12
  803.4 50.1 all-gather.16
  855.7 50.1 all-gather.14
  969.9 97.8 reduce-scatter.7
where the time goes:
time: 1190 us; the launch traced here: 1180 us
  matrix products  578 us (49%)
  waiting for transfers between devices  391 us (33%)
  other arithmetic  140 us (12%)
  local copies, waits for them, and re-layouts  29.4 us (2%)
  blocking collectives  24.8 us (2%)
  between operations  15.1 us (1%)
    all_gather x2, waiting for transfers between devices, block_backward(): dy_full = lax.all_gather(dy_loc, 'tp', axis=0, tiled=True)  98.2 us
    all_gather x2, waiting for transfers between devices, block_forward(): u_full = lax.all_gather(u_loc, 'tp', axis=0, tiled=True)  98 us
    reduce_scatter x1, waiting for transfers between devices, block_forward(): lax.psum_scatter(block_part, 'tp', scatter_dimension=0, tiled=True)  98 us
    reduce_scatter x2, waiting for transfers between devices, block_backward(): lax.psum_scatter(normed_part, 'tp', scatter_dimension=0, tiled=True)  95.3 us
    dot_general x4, matrix products, causal_scores(): jnp.einsum('skgd,tkd->kgst', query, keys_rot, preferred_element_type=jnp....  62.6 us
    dot_general x2, matrix products, block_backward(): jnp.einsum('sf,df->sd', d_up, w_up_l, preferred_element_type=jnp.float32)  54.6 us
    another operation x6, other arithmetic  42.9 us
    dot_general x2, matrix products, block_backward(): jnp.einsum('sf,df->sd', d_gate, w_gate_l, preferred_element_type=jnp.floa...  39.4 us
  transfers between devices with their start and end apart: 9, of which 6 were waited for; matrix products, arithmetic and copies ran while one was open for 29% of the time, Pallas kernels for 0%

commit v1 on v0

v1 whole, which is shorter than its diff:
```python
import functools

import jax
import jax.numpy as jnp
from jax import lax
from jax.experimental import pallas as pl
from jax.experimental.pallas import tpu as pltpu
from jax.sharding import PartitionSpec as P

HEAD_DIM = 128
NORM_EPS = 1e-5
ROPE_BASE = 10000.0
Q_BLOCK = 256
VMEM_LIMIT = 60 * 1024 * 1024
F32 = jnp.float32
BF16 = jnp.bfloat16

CONTRACT_LAST = (((1,), (1,)), ((), ()))
CONTRACT_FIRST = (((0,), (0,)), ((), ()))
MATMUL = (((1,), (0,)), ((), ()))


def dot(lhs, rhs, dims):
    return lax.dot_general(lhs, rhs, dims, preferred_element_type=F32)


def params():
    return pltpu.CompilerParams(vmem_limit_bytes=VMEM_LIMIT)


def cost(flops, bytes_accessed, transcendentals=0):
    return pl.CostEstimate(flops=int(flops), bytes_accessed=int(bytes_accessed), transcendentals=int(transcendentals))


def rope_tables(seq_len):
    half_dim = HEAD_DIM // 2
    freqs = ROPE_BASE ** (-2.0 * jnp.arange(half_dim, dtype=F32) / HEAD_DIM)
    angles = jnp.arange(seq_len, dtype=F32)[:, None] * freqs[None, :]
    cos, sin = jnp.cos(angles), jnp.sin(angles)
    return jnp.concatenate([cos, cos], axis=-1), jnp.concatenate([-sin, sin], axis=-1)


def rms_scale(x_f32, gain_row):
    inv_rms = lax.rsqrt(jnp.mean(x_f32 * x_f32, axis=-1, keepdims=True) + NORM_EPS)
    return x_f32 * inv_rms * gain_row


def gated(gate_f32, up_f32):
    return jax.nn.silu(gate_f32) * up_f32


def head_cols(index):
    return pl.ds(pl.multiple_of(index * HEAD_DIM, HEAD_DIM), HEAD_DIM)


def diagonal_mask():
    return lax.broadcasted_iota(jnp.int32, (Q_BLOCK, Q_BLOCK), 0) >= lax.broadcasted_iota(jnp.int32, (Q_BLOCK, Q_BLOCK), 1)


def attn_fwd_kernel(group, qkv_ref, cos_ref, sin_ref, rot_ref, out_ref, lse_ref):
    seq_len = qkv_ref.shape[0]
    scale = HEAD_DIM ** -0.5
    key, val = pl.ds(group * HEAD_DIM, HEAD_DIM), pl.ds((group + 1) * HEAD_DIM, HEAD_DIM)

    def rotate_head(head, carry):
        values = qkv_ref[:, head_cols(head)].astype(F32)
        rot_ref[:, head_cols(head)] = (values * cos_ref[...] + pltpu.roll(values, HEAD_DIM // 2, 1) * sin_ref[...]).astype(BF16)
        return carry

    lax.fori_loop(0, group + 1, rotate_head, 0)
    rot_ref[:, val] = qkv_ref[:, val]
    for block in range(seq_len // Q_BLOCK):
        start = block * Q_BLOCK
        rows = pl.ds(start, Q_BLOCK)

        def one_head(head, carry):
            query = rot_ref[rows, head_cols(head)]
            diag = jnp.where(diagonal_mask(), dot(query, rot_ref[rows, key], CONTRACT_LAST) * scale, -1e30)
            row_max = jnp.max(diag, axis=-1, keepdims=True)
            if start:
                past = dot(query, rot_ref[pl.ds(0, start), key], CONTRACT_LAST) * scale
                row_max = jnp.maximum(row_max, jnp.max(past, axis=-1, keepdims=True))
            diag = jnp.exp(diag - row_max)
            total = jnp.sum(diag, axis=-1, keepdims=True)
            if start:
                past = jnp.exp(past - row_max)
                total = total + jnp.sum(past, axis=-1, keepdims=True)
            inverse = 1.0 / total
            acc = dot((diag * inverse).astype(BF16), rot_ref[rows, val], MATMUL)
            if start:
                acc = acc + dot((past * inverse).astype(BF16), rot_ref[pl.ds(0, start), val], MATMUL)
            out_ref[rows, head_cols(head)] = acc.astype(BF16)
            lse_ref[rows, head_cols(head)] = jnp.broadcast_to(row_max + jnp.log(total), (Q_BLOCK, HEAD_DIM))
            return carry

        lax.fori_loop(0, group, one_head, 0)


def attn_fwd(qkv, cos_tab, sin_tab, group):
    seq_len = qkv.shape[0]
    pairs = group * seq_len * seq_len
    return pl.pallas_call(
        functools.partial(attn_fwd_kernel, group),
        out_shape=(
            jax.ShapeDtypeStruct(qkv.shape, BF16),
            jax.ShapeDtypeStruct((seq_len, group * HEAD_DIM), BF16),
            jax.ShapeDtypeStruct((seq_len, group * HEAD_DIM), F32),
        ),
        compiler_params=params(),
        cost_estimate=cost(4 * pairs * HEAD_DIM, 8 * qkv.size, pairs // 2),
        name="attn_fwd",
    )(qkv, cos_tab, sin_tab)


def attn_bwd_kernel(group, rot_ref, lse_ref, dout_ref, cos_ref, sin_ref, dqkv_ref, dkey_ref, dval_ref):
    seq_len = rot_ref.shape[0]
    scale = HEAD_DIM ** -0.5
    key, val = pl.ds(group * HEAD_DIM, HEAD_DIM), pl.ds((group + 1) * HEAD_DIM, HEAD_DIM)
    dkey_ref[...] = jnp.zeros_like(dkey_ref)
    dval_ref[...] = jnp.zeros_like(dval_ref)

    def unrotate(values, rows):
        values = values.astype(BF16).astype(F32)
        return (values * cos_ref[rows, :] - pltpu.roll(values, HEAD_DIM // 2, 1) * sin_ref[rows, :]).astype(BF16)

    for block in range(seq_len // Q_BLOCK):
        start = block * Q_BLOCK
        rows = pl.ds(start, Q_BLOCK)

        def one_head(head, carry):
            query = rot_ref[rows, head_cols(head)]
            dout = dout_ref[rows, head_cols(head)]
            lse = lse_ref[rows, head_cols(head)][:, :1]

            def probs(cols, masked):
                scores = dot(query, rot_ref[cols, key], CONTRACT_LAST) * scale
                if masked:
                    scores = jnp.where(diagonal_mask(), scores, -1e30)
                prob = jnp.exp(scores - lse)
                dprob = dot(dout, rot_ref[cols, val], CONTRACT_LAST).astype(BF16).astype(F32)
                dval_ref[cols, :] += dot(prob.astype(BF16), dout, CONTRACT_FIRST)
                return prob, dprob, jnp.sum(prob * dprob, axis=-1, keepdims=True)

            def finish(cols, prob, dprob, delta):
                dscore = (prob * (dprob - delta) * scale).astype(BF16)
                dkey_ref[cols, :] += dot(dscore, query, CONTRACT_FIRST)
                return dot(dscore, rot_ref[cols, key], MATMUL)

            prob, dprob, delta = probs(rows, True)
            if start:
                past = pl.ds(0, start)
                past_prob, past_dprob, past_delta = probs(past, False)
                delta = delta + past_delta
            dquery = finish(rows, prob, dprob, delta)
            if start:
                dquery = dquery + finish(past, past_prob, past_dprob, delta)
            dqkv_ref[rows, head_cols(head)] = unrotate(dquery, rows)
            return carry

        lax.fori_loop(0, group, one_head, 0)
    dqkv_ref[:, key] = unrotate(dkey_ref[...], pl.ds(0, seq_len))
    dqkv_ref[:, val] = dval_ref[...].astype(BF16)


def attn_bwd(rot, lse, dout, cos_tab, sin_tab, group):
    seq_len = rot.shape[0]
    pairs = group * seq_len * seq_len
    return pl.pallas_call(
        functools.partial(attn_bwd_kernel, group),
        out_shape=jax.ShapeDtypeStruct(rot.shape, BF16),
        scratch_shapes=[pltpu.VMEM((seq_len, HEAD_DIM), F32)] * 2,
        compiler_params=params(),
        cost_estimate=cost(10 * pairs * HEAD_DIM, 8 * rot.size, pairs // 2),
        name="attn_bwd",
    )(rot, lse, dout, cos_tab, sin_tab)


def sum_of_dots_kernel(dims, n_terms, *refs):
    out_ref = refs[-1]
    total = dot(refs[0][...], refs[n_terms][...], dims)
    for term in range(1, n_terms):
        total = total + dot(refs[term][...], refs[n_terms + term][...], dims)
    out_ref[...] = total


def sum_of_dots(terms, layer, dims, first_col, n_cols, tile, name):
    seq_len = terms[0][0].shape[0]
    flops = sum(2 * seq_len * lhs.shape[1] * n_cols for lhs, _ in terms)
    n_bytes = sum(2 * lhs.shape[1] * (seq_len + n_cols) for lhs, _ in terms) + 4 * seq_len * n_cols
    first_tile = first_col // tile
    lhs_specs = [pl.BlockSpec(lhs.shape, lambda step: (0, 0)) for lhs, _ in terms]
    if dims is MATMUL:
        rhs_specs = [pl.BlockSpec((None, rhs.shape[1], tile), lambda step: (layer, 0, first_tile + step)) for _, rhs in terms]
    else:
        rhs_specs = [pl.BlockSpec((None, tile, rhs.shape[2]), lambda step: (layer, first_tile + step, 0)) for _, rhs in terms]
    return pl.pallas_call(
        functools.partial(sum_of_dots_kernel, dims, len(terms)),
        out_shape=jax.ShapeDtypeStruct((seq_len, n_cols), F32),
        grid=(n_cols // tile,),
        in_specs=lhs_specs + rhs_specs,
        out_specs=pl.BlockSpec((seq_len, tile), lambda step: (0, step)),
        compiler_params=params(),
        cost_estimate=cost(flops, n_bytes),
        name=name,
    )(*[lhs for lhs, _ in terms], *[rhs for _, rhs in terms])


def grad_in_kernel(n_rhs, *refs):
    lhs = refs[0][...]
    rhs_refs, out_refs = refs[1:1 + n_rhs], refs[-n_rhs:]
    for rhs_ref, out_ref in zip(rhs_refs, out_refs):
        out_ref[...] = dot(lhs, rhs_ref[...], CONTRACT_FIRST).astype(BF16)


def grad_in(lhs, rhs_list, layer, n_layers, previous, tile=512):
    seq_len, depth = lhs.shape
    n_rhs = len(rhs_list)
    shapes = tuple(jax.ShapeDtypeStruct((n_layers, depth, rhs.shape[1]), BF16) for rhs in rhs_list)
    width = sum(rhs.shape[1] for rhs in rhs_list)
    aliases = {1 + n_rhs + idx: idx for idx in range(n_rhs)} if previous else {}
    return pl.pallas_call(
        functools.partial(grad_in_kernel, n_rhs),
        out_shape=shapes,
        grid=(depth // tile,),
        in_specs=[pl.BlockSpec((seq_len, tile), lambda step: (0, step))]
        + [pl.BlockSpec(rhs.shape, lambda step: (0, 0)) for rhs in rhs_list]
        + [pl.BlockSpec(memory_space=pl.ANY) for _ in previous],
        out_specs=[pl.BlockSpec((None, tile, rhs.shape[1]), lambda step: (layer, step, 0)) for rhs in rhs_list],
        input_output_aliases=aliases,
        compiler_params=params(),
        cost_estimate=cost(2 * seq_len * depth * width, 2 * (seq_len * depth + seq_len * width + depth * width)),
        name="grad_in",
    )(lhs, *rhs_list, *previous)


def grad_out_kernel(attn_ref, hidden_ref, dy_ref, *refs):
    out_ref, down_ref = refs[-2:]

    @pl.when(pl.program_id(0) == 0)
    def _():
        out_ref[...] = dot(attn_ref[...], dy_ref[...], CONTRACT_FIRST).astype(BF16)

    down_ref[...] = dot(hidden_ref[...], dy_ref[...], CONTRACT_FIRST).astype(BF16)


def grad_out(attn_out, hidden, dy_full, layer, n_layers, previous, tile=512):
    seq_len, depth = dy_full.shape
    heads, ff = attn_out.shape[1], hidden.shape[1]
    return pl.pallas_call(
        grad_out_kernel,
        out_shape=(jax.ShapeDtypeStruct((n_layers, heads, depth), BF16), jax.ShapeDtypeStruct((n_layers, ff, depth), BF16)),
        grid=(ff // tile,),
        in_specs=[
            pl.BlockSpec((seq_len, heads), lambda step: (0, 0)),
            pl.BlockSpec((seq_len, tile), lambda step: (0, step)),
            pl.BlockSpec((seq_len, depth), lambda step: (0, 0), pipeline_mode=pl.Buffered(1)),
        ]
        + [pl.BlockSpec(memory_space=pl.ANY) for _ in previous],
        out_specs=[
            pl.BlockSpec((None, heads, depth), lambda step: (layer, 0, 0)),
            pl.BlockSpec((None, tile, depth), lambda step: (layer, step, 0)),
        ],
        input_output_aliases={3: 0, 4: 1} if previous else {},
        compiler_params=params(),
        cost_estimate=cost(2 * seq_len * depth * (heads + ff), 2 * (seq_len * depth + (seq_len + depth) * (heads + ff))),
        name="grad_out",
    )(attn_out, hidden, dy_full, *previous)


def gather_rows(rows_loc):
    return lax.all_gather(rows_loc, 'tp', axis=0, tiled=True)


def after(value, *others):
    return lax.optimization_barrier((value,) + others)[0]


def reduce_rows(chunks):
    return jnp.concatenate([lax.psum_scatter(chunk, 'tp', scatter_dimension=0, tiled=True) for chunk in chunks], axis=1)


def solution(mesh):
    tp_size = mesh.shape['tp']
    row_spec = P(('dp', 'tp'), None)
    col_spec = P(None, None, 'tp')
    inner_spec = P(None, 'tp', None)

    def sum_over_tp(value):
        stride = 1
        while stride < tp_size:
            value = value + lax.ppermute(value, 'tp', [(idx, idx ^ stride) for idx in range(tp_size)])
            stride *= 2
        return value

    def device_program(x_loc, dy_loc, norm_gain, w_qkv, w_out, w_gate, w_up, w_down):
        n_layers, depth = w_qkv.shape[0], w_qkv.shape[1]
        group = w_out.shape[1] // HEAD_DIM
        seq_len = x_loc.shape[0] * tp_size
        n_chunks = 2
        chunk_cols = depth // n_chunks
        cos_tab, sin_tab = rope_tables(seq_len)
        saved_all = []
        x_cur = x_loc
        dy_full = None
        for layer in range(n_layers):
            last = layer == n_layers - 1
            x_f32 = x_cur.astype(F32)
            u_loc = rms_scale(x_f32, norm_gain[layer]).astype(BF16)
            u_full = gather_rows(u_loc)
            if dy_full is None:
                dy_full = gather_rows(after(dy_loc, u_full))
            qkv = jnp.dot(u_full, w_qkv[layer], preferred_element_type=F32).astype(BF16)
            rot, attn_out, lse = attn_fwd(qkv, cos_tab, sin_tab, group)
            gate = jnp.dot(u_full, w_gate[layer], preferred_element_type=F32).astype(BF16)
            up = jnp.dot(u_full, w_up[layer], preferred_element_type=F32).astype(BF16)
            saved_all.append((x_cur, u_loc, rot, attn_out, lse, gate, up))
            if not last:
                hidden = gated(gate.astype(F32), up.astype(F32)).astype(BF16)
                parts = [
                    sum_of_dots([(attn_out, w_out), (hidden, w_down)], layer, MATMUL, idx * chunk_cols, chunk_cols, 512, "block_out")
                    for idx in range(n_chunks)
                ]
                x_cur = (x_f32 + reduce_rows(parts)).astype(BF16)

        in_grads, out_grads, gain_grads = (), (), []
        for layer in reversed(range(n_layers)):
            x_in, u_loc, rot, attn_out, lse, gate, up = saved_all[layer]
            if layer < n_layers - 1:
                dy_full, in_grads, out_grads = lax.optimization_barrier((gather_rows(dy_loc), in_grads, out_grads))
            d_attn = lax.dot_general(dy_full, w_out[layer], CONTRACT_LAST, preferred_element_type=F32).astype(BF16)
            d_hidden = lax.dot_general(dy_full, w_down[layer], CONTRACT_LAST, preferred_element_type=F32).astype(BF16)
            hidden_f32, gated_pull = jax.vjp(gated, gate.astype(F32), up.astype(F32))
            hidden = hidden_f32.astype(BF16)
            d_gate, d_up = [item.astype(BF16) for item in gated_pull(d_hidden.astype(F32))]
            u_full = gather_rows(after(u_loc, attn_out, d_attn))
            d_qkv = attn_bwd(rot, lse, d_attn, cos_tab, sin_tab, group)
            d_qkv, d_gate, d_up, hidden, u_full = lax.optimization_barrier((d_qkv, d_gate, d_up, hidden, u_full))
            parts = [
                sum_of_dots([(d_qkv, w_qkv), (d_gate, w_gate), (d_up, w_up)], layer, CONTRACT_LAST, idx * chunk_cols, chunk_cols, 512, "block_in_back")
                for idx in range(n_chunks)
            ]
            held = lax.optimization_barrier((parts[-1], d_qkv, d_gate, d_up, hidden, attn_out))
            parts[-1] = held[0]
            in_grads = grad_in(u_full, held[1:4], layer, n_layers, in_grads)
            out_grads = grad_out(held[5], held[4], dy_full, layer, n_layers, out_grads)
            d_normed = reduce_rows(parts).astype(BF16)
            norm_pull = jax.vjp(rms_scale, x_in.astype(F32), norm_gain[layer])[1]
            d_x_norm, gain_grad = norm_pull(d_normed.astype(F32))
            dy_loc = (dy_loc.astype(F32) + d_x_norm).astype(BF16)
            gain_grads.insert(0, gain_grad)
        grad_gain = sum_over_tp(jnp.stack(gain_grads))
        return (dy_loc, grad_gain, in_grads[0], out_grads[0], in_grads[1], in_grads[2], out_grads[1])

    return jax.shard_map(device_program, mesh=mesh, in_specs=(row_spec, row_spec, P(None, None), col_spec, inner_spec, col_spec, col_spec, inner_spec), out_specs=(row_spec, P('dp', None), P('dp', None, 'tp'), P('dp', 'tp', None), P('dp', None, 'tp'), P('dp', None, 'tp'), P('dp', 'tp', None)), check_vma=False)
```

time: 1190 us -> 885 us (0.74)
  matrix products: 578 us -> 142 us
  Pallas kernels: 0 us -> 306 us
  other arithmetic: 140 us -> 26.2 us
  local copies, waits for them, and re-layouts: 29.4 us -> 2.04 us
  blocking collectives: 24.8 us -> 0 us
    dot_general x42 -> x10, matrix products: 578 us -> 142 us  [the longest x2 34.6 us: device_program(): lax.dot_general(dy_full, w_down[layer], CONTRACT_LAST, preferred_element_...]
    pallas_call x0 -> x14, Pallas kernels: none -> 306 us  [the longest x6 107 us: sum_of_dots(): pl.pallas_call(functools.partial(sum_of_dots_kernel, dims, len(terms)), o...]
    another operation x11 -> x5, other arithmetic: 77.8 us -> 5.44 us
    all_gather x6, waiting for transfers between devices: 196 us -> 141 us  [gather_rows(): return lax.all_gather(rows_loc, 'tp', axis=0, tiled=True)]
    reduce_scatter x3 -> x6, waiting for transfers between devices: 193 us -> 238 us  [reduce_rows(): lax.psum_scatter(chunk, 'tp', scatter_dimension=0, tiled=True)]
    reduce_sum x2 -> x0, other arithmetic: 25.5 us -> none  [block_forward(): jnp.sum(jnp.exp(scores - row_max), axis=-1, keepdims=True)]
    psum x1 -> x0, blocking collectives: 24.8 us -> none  [device_program(): grad_gain = lax.psum(jnp.stack([item[0] for item in layer_grads]), 'tp')]
    unnamed x116 -> x44, local copies, waits for them, and re-layouts: 15.7 us -> 1.2 us
  transfers between devices with their start and end apart: 9 -> 15, of which waited for: 6 -> 11; matrix products, arithmetic and copies ran while one was open for 29% -> 10% of each run, Pallas kernels for 0% -> 24%
where the time goes in v1:
time: 885 us; the launch traced here: 881 us
  waiting for transfers between devices  386 us (44%)
  Pallas kernels  306 us (35%)
  matrix products  142 us (16%)
  other arithmetic  26.2 us (3%)
  between operations  14.8 us (2%)
    reduce_scatter x6, waiting for transfers between devices, reduce_rows(): lax.psum_scatter(chunk, 'tp', scatter_dimension=0, tiled=True)  238 us
    all_gather x6, waiting for transfers between devices, gather_rows(): return lax.all_gather(rows_loc, 'tp', axis=0, tiled=True)  141 us
    pallas_call x6, Pallas kernels, sum_of_dots(): pl.pallas_call(functools.partial(sum_of_dots_kernel, dims, len(terms)), o...  107 us
    pallas_call x2, Pallas kernels, grad_in(): pl.pallas_call(functools.partial(grad_in_kernel, n_rhs), out_shape=shapes...  66.2 us
    pallas_call x2, Pallas kernels, attn_bwd(): pl.pallas_call(functools.partial(attn_bwd_kernel, group), out_shape=jax.S...  55 us
    pallas_call x2, Pallas kernels, grad_out(): pl.pallas_call(grad_out_kernel, out_shape=(jax.ShapeDtypeStruct((n_layers...  40.7 us
    pallas_call x2, Pallas kernels, attn_fwd(): pl.pallas_call(functools.partial(attn_fwd_kernel, group), out_shape=(jax....  37.8 us
    dot_general x2, matrix products, device_program(): lax.dot_general(dy_full, w_down[layer], CONTRACT_LAST, preferred_element_...  34.6 us
  transfers between devices with their start and end apart: 15, of which 11 were waited for; matrix products, arithmetic and copies ran while one was open for 10% of the time, Pallas kernels for 24%

profile of v1, /device:TPU:112, one launch (start us, length us, event | category | flops | bytes accessed | tf_op | source)
XLA Modules:
  0.0 880.6 jit_solution(17725807669931659343)
XLA Ops:
  18.2 48.2 %all-gather.7.cloned.1.call-done = bf16[1536,3072]{1,0:T(8,128)(2,1)} async-done(((bf16[192,3072]{1,0:T(8,128)(2,1)}), bf16[1536,3072]{1,0:T(8,128)(2,1)}) %all-gather.7.cloned.1.call-update) | async-done | bytes 9437200 | tf_op jit(solution)/shard_map/all_gather | solution.py:271
  78.8 19.0 %attn_fwd.2 = (bf16[1536,640]{1,0:T(8,128)(2,1)}, bf16[1536,384]{1,0:T(8,128)(2,1)}, f32[1536,384]{1,0:T(8,128)}) custom-call(bf16[1536,640]{1,0:T(8,128)(2,1)} %fusion.58.qkv_ref, f32[1536,128]{1,0:T(8,128)} %get-tuple-element.119.cos_ref, f32[1536,128]{1,0:T(8,128)} %get-tuple-element.120.sin_ref), custom_call_target="tpu_custom_call" | custom-call | flops 3623878656 | bytes 7864320 | tf_op jit(solution)/shard_map/attn_fwd/pallas_call | solution.py:102
  112.0 16.2 %fusion = (bf16[1536,1024]{1,0:T(8,128)(2,1)}, bf16[1536,1024]{1,0:T(8,128)(2,1)}) fusion(bf16[1536,1024]{1,0:T(8,128)(2,1)S(1)} %fusion.40, bf16[1536,3072]{1,0:T(8,128)(2,1)S(1)} %bitcast.81, bf16[2,3072,1024]{2,1,0:T(8,128)(2,1)} %refs_5_.7), kind=kOutput, calls=%fused_computation.14 | convolution fusion | flops 9677832192 | bytes 25165824 | tf_op jit(solution)/shard_map/dot_general | solution.py:315
  153.7 40.7 %reduce-scatter.9.cloned.1.call-done = f32[192,1536]{1,0:T(8,128)} async-done(((f32[1536,1536]{1,0:T(8,128)}), f32[192,1536]{1,0:T(8,128)}) %reduce-scatter.9.cloned.1.call-update) | async-done | bytes 1179664 | tf_op jit(solution)/shard_map/reduce_scatter | solution.py:279
  194.4 56.0 %reduce-scatter.7.cloned.1.call-done = f32[192,1536]{1,0:T(8,128)} async-done(((f32[1536,1536]{1,0:T(8,128)}), f32[192,1536]{1,0:T(8,128)}) %reduce-scatter.7.cloned.1.call-update) | async-done | bytes 1179664 | tf_op jit(solution)/shard_map/reduce_scatter | solution.py:279
  254.0 47.4 %all-gather.11.cloned.1.call-done.dy_ref = bf16[1536,3072]{1,0:T(8,128)(2,1)} async-done(((bf16[192,3072]{1,0:T(8,128)(2,1)}), bf16[1536,3072]{1,0:T(8,128)(2,1)}) %all-gather.11.cloned.1.call-update) | async-done | bytes 9437200 | tf_op jit(solution)/shard_map/all_gather | solution.py:271
  310.7 42.8 %all-gather.9.cloned.1.call-done = bf16[1536,3072]{1,0:T(8,128)(2,1)} async-done(((bf16[192,3072]{1,0:T(8,128)(2,1)}), bf16[1536,3072]{1,0:T(8,128)(2,1)}) %all-gather.9.cloned.1.call-update) | async-done | bytes 9437200 | tf_op jit(solution)/shard_map/all_gather | solution.py:271
  365.7 18.8 %attn_fwd.3 = (bf16[1536,640]{1,0:T(8,128)(2,1)}, bf16[1536,384]{1,0:T(8,128)(2,1)}, f32[1536,384]{1,0:T(8,128)}) custom-call(bf16[1536,640]{1,0:T(8,128)(2,1)} %fusion.61.qkv_ref, f32[1536,128]{1,0:T(8,128)} %get-tuple-element.119.cos_ref, f32[1536,128]{1,0:T(8,128)} %get-tuple-element.120.sin_ref), custom_call_target="tpu_custom_call" | custom-call | flops 3623878656 | bytes 7864320 | tf_op jit(solution)/shard_map/attn_fwd/pallas_call | solution.py:102
  400.4 27.3 %attn_bwd.2.refs_0_.refs_1_ = bf16[1536,640]{1,0:T(8,128)(2,1)} custom-call(bf16[1536,640]{1,0:T(8,128)(2,1)} %get-tuple-element.55.rot_ref, f32[1536,384]{1,0:T(8,128)} %get-tuple-element.56.lse_ref, bf16[1536,384]{1,0:T(8,128)(2,1)} %convolution_convert_fusion.1.dout_ref, f32[1536,128]{1,0:T(8,128)} %get-tuple-element.119.cos_ref, ...), custom_call_target="tpu_custom_call" | custom-call | flops 9059696640 | bytes 7864320 | tf_op jit(solution)/shard_map/attn_bwd/pallas_call | solution.py:168
  427.7 16.0 %fusion.52 = bf16[1536,1024]{1,0:T(8,128)(2,1)} fusion(bf16[1536,3072]{1,0:T(8,128)(2,1)} %all-gather.9.cloned.1.call-done, bf16[2,3072,1024]{2,1,0:T(8,128)(2,1)} %refs_4_.7), kind=kOutput, calls=%fused_computation.67 | convolution fusion | flops 9665249280 | bytes 18874368 | tf_op jit(solution)/shard_map/dot_general | solution.py:314
  443.7 18.2 %fusion.2 = (bf16[1536,1024]{1,0:T(8,128)(2,1)}, bf16[1536,1024]{1,0:T(8,128)(2,1)}, bf16[1536,1024]{1,0:T(8,128)(2,1)}) fusion(bf16[1536,1024]{1,0:T(8,128)(2,1)} %fusion.52, bf16[1536,1024]{1,0:T(8,128)(2,1)S(1)} %copy-done.15, bf16[1536,3072]{1,0:T(8,128)(2,1)S(1)} %bitcast.79, bf16[2,3072,1024]{2,1,0:T(8,128)(2,1)} %refs_5_.7), kind=kOutput, calls=%fused_computation.16 | convolution fusion | flops 9695133696 | bytes 31457280 | tf_op jit(solution)/shard_map/dot_general | solution.py:315
  461.9 20.5 %block_in_back.5 = f32[1536,1536]{1,0:T(8,128)} custom-call(bf16[1536,640]{1,0:T(8,128)(2,1)} %attn_bwd.2.refs_0_.refs_1_, bf16[1536,1024]{1,0:T(8,128)(2,1)} %get-tuple-element.69.refs_1_.refs_2_, bf16[1536,1024]{1,0:T(8,128)(2,1)} %get-tuple-element.70.refs_2_.refs_3_, bf16[2,3072,640]{2,1,0:T(8,128)(2,1)} %refs_3_.11, bf16[2,3072,1024]{2,1,0:T(8,128)(2,1)} %refs_4_.7, ...), custom_call_target="tpu_custom_call" | custom-call | flops 12683575296 | bytes 25952256 | tf_op jit(solution)/shard_map/block_in_back/pallas_call | solution.py:196
  482.6 20.4 %block_in_back.4 = f32[1536,1536]{1,0:T(8,128)} custom-call(bf16[1536,640]{1,0:T(8,128)(2,1)} %attn_bwd.2.refs_0_.refs_1_, bf16[1536,1024]{1,0:T(8,128)(2,1)} %get-tuple-element.69.refs_1_.refs_2_, bf16[1536,1024]{1,0:T(8,128)(2,1)} %get-tuple-element.70.refs_2_.refs_3_, bf16[2,3072,640]{2,1,0:T(8,128)(2,1)} %refs_3_.11, bf16[2,3072,1024]{2,1,0:T(8,128)(2,1)} %refs_4_.7, ...), custom_call_target="tpu_custom_call" | custom-call | flops 12683575296 | bytes 25952256 | tf_op jit(solution)/shard_map/block_in_back/pallas_call | solution.py:196
  503.1 33.2 %reduce-scatter.13.cloned.1.call-done = f32[192,1536]{1,0:T(8,128)} async-done(((f32[1536,1536]{1,0:T(8,128)}), f32[192,1536]{1,0:T(8,128)}) %reduce-scatter.13.cloned.1.call-update) | async-done | bytes 1179664 | tf_op jit(solution)/shard_map/reduce_scatter | solution.py:279
  537.7 54.6 %reduce-scatter.11.cloned.1.call-done = f32[192,1536]{1,0:T(8,128)} async-done(((f32[1536,1536]{1,0:T(8,128)}), f32[192,1536]{1,0:T(8,128)}) %reduce-scatter.11.cloned.1.call-update) | async-done | bytes 1179664 | tf_op jit(solution)/shard_map/reduce_scatter | solution.py:279
  598.3 20.4 %grad_out.2 = (bf16[2,384,3072]{2,1,0:T(8,128)(2,1)}, bf16[2,1024,3072]{2,1,0:T(8,128)(2,1)}) custom-call(bf16[1536,384]{1,0:T(8,128)(2,1)} %get-tuple-element.74.attn_ref, bf16[1536,1024]{1,0:T(8,128)(2,1)} %get-tuple-element.75.hidden_ref, bf16[1536,3072]{1,0:T(8,128)(2,1)} %all-gather.11.cloned.1.call-done.dy_ref), custom_call_target="tpu_custom_call" | custom-call | flops 13287555072 | bytes 22413312 | tf_op jit(solution)/shard_map/grad_out/pallas_call | solution.py:249
  618.6 33.1 %grad_in.2 = (bf16[2,3072,640]{2,1,0:T(8,128)(2,1)}, bf16[2,3072,1024]{2,1,0:T(8,128)(2,1)}, bf16[2,3072,1024]{2,1,0:T(8,128)(2,1)}) custom-call(bf16[1536,3072]{1,0:T(8,128)(2,1)} %all-gather.13.cloned.1.call-done.refs_0_, bf16[1536,640]{1,0:T(8,128)(2,1)} %attn_bwd.2.refs_0_.refs_1_, bf16[1536,1024]{1,0:T(8,128)(2,1)} %get-tuple-element.69.refs_1_.refs_2_, ...), custom_call_target="tpu_custom_call" | custom-call | flops 25367150592 | bytes 34209792 | tf_op jit(solution)/shard_map/grad_in/pallas_call | solution.py:221
  661.1 27.7 %attn_bwd.3.refs_0_.refs_1_ = bf16[1536,640]{1,0:T(8,128)(2,1)} custom-call(bf16[1536,640]{1,0:T(8,128)(2,1)} %get-tuple-element.65.rot_ref, f32[1536,384]{1,0:T(8,128)} %get-tuple-element.66.lse_ref, bf16[1536,384]{1,0:T(8,128)(2,1)} %convolution_convert_fusion.dout_ref, f32[1536,128]{1,0:T(8,128)} %get-tuple-element.119.cos_ref, ...), custom_call_target="tpu_custom_call" | custom-call | flops 9059696640 | bytes 7864320 | tf_op jit(solution)/shard_map/attn_bwd/pallas_call | solution.py:168
  688.8 18.9 %fusion.3 = (bf16[1536,1024]{1,0:T(8,128)(2,1)}, bf16[1536,1024]{1,0:T(8,128)(2,1)}) fusion(bf16[1536,1024]{1,0:T(8,128)(2,1)S(1)} %copy-done.14, bf16[1536,1024]{1,0:T(8,128)(2,1)} %get-tuple-element.118, bf16[1536,3072]{1,0:T(8,128)(2,1)} %all-gather.15.cloned.1.call-done.dy_ref, bf16[2,1024,3072]{2,1,0:T(8,128)(2,1)} %refs_3_.7), kind=kOutput, calls=%fused_computation.17 | convolution fusion | flops 9691987968 | bytes 28311552 | tf_op jit(solution)/shard_map/dot_general | solution.py:331
  710.7 20.4 %block_in_back.7 = f32[1536,1536]{1,0:T(8,128)} custom-call(bf16[1536,640]{1,0:T(8,128)(2,1)} %attn_bwd.3.refs_0_.refs_1_, bf16[1536,1024]{1,0:T(8,128)(2,1)} %get-tuple-element.87.refs_1_.refs_2_, bf16[1536,1024]{1,0:T(8,128)(2,1)} %get-tuple-element.88.refs_2_.refs_3_, bf16[2,3072,640]{2,1,0:T(8,128)(2,1)} %refs_3_.11, bf16[2,3072,1024]{2,1,0:T(8,128)(2,1)} %refs_4_.7, ...), custom_call_target="tpu_custom_call" | custom-call | flops 12683575296 | bytes 25952256 | tf_op jit(solution)/shard_map/block_in_back/pallas_call | solution.py:196
  731.3 20.8 %block_in_back.6 = f32[1536,1536]{1,0:T(8,128)} custom-call(bf16[1536,640]{1,0:T(8,128)(2,1)} %attn_bwd.3.refs_0_.refs_1_, bf16[1536,1024]{1,0:T(8,128)(2,1)} %get-tuple-element.87.refs_1_.refs_2_, bf16[1536,1024]{1,0:T(8,128)(2,1)} %get-tuple-element.88.refs_2_.refs_3_, bf16[2,3072,640]{2,1,0:T(8,128)(2,1)} %refs_3_.11, bf16[2,3072,1024]{2,1,0:T(8,128)(2,1)} %refs_4_.7, ...), custom_call_target="tpu_custom_call" | custom-call | flops 12683575296 | bytes 25952256 | tf_op jit(solution)/shard_map/block_in_back/pallas_call | solution.py:196
  752.1 33.1 %grad_in.3 = (bf16[2,3072,640]{2,1,0:T(8,128)(2,1)}, bf16[2,3072,1024]{2,1,0:T(8,128)(2,1)}, bf16[2,3072,1024]{2,1,0:T(8,128)(2,1)}) custom-call(bf16[1536,3072]{1,0:T(8,128)(2,1)} %all-gather.17.cloned.1.call-done.refs_0_, bf16[1536,640]{1,0:T(8,128)(2,1)} %attn_bwd.3.refs_0_.refs_1_, ...), custom_call_target="tpu_custom_call", output_to_operand_aliasing={{0}: (4, {}), {1}: (5, {}), {2}: (6, {})} | custom-call | flops 25367150592 | bytes 34209792 | tf_op jit(solution)/shard_map/grad_in/pallas_call | solution.py:221
  786.7 53.6 %reduce-scatter.15.cloned.1.call-done = f32[192,1536]{1,0:T(8,128)} async-done(((f32[1536,1536]{1,0:T(8,128)}), f32[192,1536]{1,0:T(8,128)}) %reduce-scatter.15.cloned.1.call-update) | async-done | bytes 1179664 | tf_op jit(solution)/shard_map/reduce_scatter | solution.py:279
  843.1 20.4 %grad_out.3 = (bf16[2,384,3072]{2,1,0:T(8,128)(2,1)}, bf16[2,1024,3072]{2,1,0:T(8,128)(2,1)}) custom-call(bf16[1536,384]{1,0:T(8,128)(2,1)} %get-tuple-element.93.refs_0_.attn_ref, bf16[1536,1024]{1,0:T(8,128)(2,1)} %get-tuple-element.94.refs_1_.hidden_ref, ...), custom_call_target="tpu_custom_call", output_to_operand_aliasing={{0}: (3, {}), {1}: (4, {})} | custom-call | flops 13287555072 | bytes 22413312 | tf_op jit(solution)/shard_map/grad_out/pallas_call | solution.py:249
  (112 shorter events, 138.3 us)
Async XLA Ops:
  7.2 59.3 %all-gather.7.cloned.1.call-start = ((), (), s32[]{:S(2)}) async-start(), calls=%async_computation.6 | async-start | bytes 10616832 | tf_op jit(solution)/shard_map/all_gather | solution.py:271
  13.5 180.9 %reduce-scatter.9.cloned.1.call-start = ((), (), s32[]{:S(2)}) async-start(), calls=%async_computation.8 | async-start | bytes 10616832 | tf_op jit(solution)/shard_map/reduce_scatter | solution.py:279
  78.8 33.2 %slice-start.3 = ((s8[9437184]{0:T(1024)(128)(4,1)}), s8[1048576]{0:T(1024)(128)(4,1)S(1)}, s32[]{:S(2)}) async-start(s8[9437184]{0:T(1024)(128)(4,1)} %bitcast.80), calls=%async_computation.21 | async-start | bytes 2097152
  140.6 109.8 %reduce-scatter.7.cloned.1.call-start = ((), (), s32[]{:S(2)}) async-start(), calls=%async_computation.7 | async-start | bytes 10616832 | tf_op jit(solution)/shard_map/reduce_scatter | solution.py:279
  152.9 97.5 %copy-start = (bf16[192,3072]{1,0:T(8,128)(2,1)S(1)}, bf16[192,3072]{1,0:T(8,128)(2,1)}, u32[]{:S(2)}) copy-start(bf16[192,3072]{1,0:T(8,128)(2,1)} %param.8) | copy-start | bytes 3538948
  153.0 148.4 %all-gather.11.cloned.1.call-start = ((), (), s32[]{:S(2)}) async-start(), calls=%async_computation.10 | async-start | bytes 10616832 | tf_op jit(solution)/shard_map/all_gather | solution.py:271
  153.6 199.9 %all-gather.9.cloned.1.call-start = ((), (), s32[]{:S(2)}) async-start(), calls=%async_computation.9 | async-start | bytes 10616832 | tf_op jit(solution)/shard_map/all_gather | solution.py:271
  252.5 58.3 %copy-start.10 = (f32[192]{0:T(256)}, f32[192]{0:T(256)S(1)}, u32[]{:S(2)}) copy-start(f32[192]{0:T(256)S(1)} %get-tuple-element.105) | copy-start | bytes 2308
  254.0 208.0 %all-gather.13.cloned.1.call-start = ((), (), s32[]{:S(2)}) async-start(), calls=%async_computation.11 | async-start | bytes 10616832 | tf_op jit(solution)/shard_map/all_gather | solution.py:271
  384.6 151.7 %reduce-scatter.13.cloned.1.call-start = ((), (), s32[]{:S(2)}) async-start(), calls=%async_computation.13 | async-start | bytes 10616832 | tf_op jit(solution)/shard_map/reduce_scatter | solution.py:279
  400.4 43.3 %slice-start = ((s8[9437184]{0:T(1024)(128)(4,1)}), s8[1048576]{0:T(1024)(128)(4,1)S(1)}, s32[]{:S(2)}) async-start(s8[9437184]{0:T(1024)(128)(4,1)} %bitcast.78), calls=%async_computation.18 | async-start | bytes 2097152
  482.5 109.8 %reduce-scatter.11.cloned.1.call-start = ((), (), s32[]{:S(2)}) async-start(), calls=%async_computation.12 | async-start | bytes 10616832 | tf_op jit(solution)/shard_map/reduce_scatter | solution.py:279
  503.0 93.2 %copy-start.3 = (bf16[192,3072]{1,0:T(8,128)(2,1)S(1)}, bf16[192,3072]{1,0:T(8,128)(2,1)}, u32[]{:S(2)}) copy-start(bf16[192,3072]{1,0:T(8,128)(2,1)} %param.9) | copy-start | bytes 3538948
  503.1 148.7 %all-gather.15.cloned.1.call-start = ((), (), s32[]{:S(2)}) async-start(), calls=%async_computation.14 | async-start | bytes 10616832 | tf_op jit(solution)/shard_map/all_gather | solution.py:271
  598.2 112.5 %all-gather.17.cloned.1.call-start = ((), (), s32[]{:S(2)}) async-start(), calls=%async_computation.15 | async-start | bytes 10616832 | tf_op jit(solution)/shard_map/all_gather | solution.py:271
  661.0 124.3 %reduce-scatter.17.cloned.1.call-start = ((), (), s32[]{:S(2)}) async-start(), calls=%async_computation.17 | async-start | bytes 10616832 | tf_op jit(solution)/shard_map/reduce_scatter | solution.py:279
  731.2 109.1 %reduce-scatter.15.cloned.1.call-start = ((), (), s32[]{:S(2)}) async-start(), calls=%async_computation.16 | async-start | bytes 10616832 | tf_op jit(solution)/shard_map/reduce_scatter | solution.py:279
  785.2 56.4 %copy-start.1 = (bf16[192,3072]{1,0:T(8,128)(2,1)S(1)}, bf16[192,3072]{1,0:T(8,128)(2,1)}, u32[]{:S(2)}) copy-start(bf16[192,3072]{1,0:T(8,128)(2,1)} %param.8) | copy-start | bytes 3538948
  785.2 56.4 %copy-start.5 = (f32[1,3072]{1,0:T(1,128)S(1)}, f32[1,3072]{1,0:T(1,128)}, u32[]{:S(2)}) copy-start(f32[1,3072]{1,0:T(1,128)} %copy-done.4) | copy-start | bytes 36868
  785.2 56.4 %copy-start.9 = (f32[192]{0:T(256)S(1)}, f32[192]{0:T(256)}, u32[]{:S(2)}) copy-start(f32[192]{0:T(256)} %copy-done.8) | copy-start | bytes 2308
  785.2 57.8 %copy-start.6 = (f32[3072]{0:T(1024)S(1)}, f32[3072]{0:T(1024)}, u32[]{:S(2)}) copy-start(f32[3072]{0:T(1024)} %get-tuple-element.103) | copy-start | bytes 36868
  843.0 20.5 %collective-permute-start = (f32[2,3072]{1,0:T(2,128)S(1)}, f32[2,3072]{1,0:T(2,128)S(1)}, u32[]{:S(2)}, u32[]{:S(2)}) collective-permute-start(f32[2,3072]{1,0:T(2,128)S(1)} %pad_maximum_fusion.4), channel_id=1, source_target_pairs={{0,1},{1,0},{2,3},{3,2},{4,5},{5,4},{6,7},{7,6},{8,9},{9,8},{10,11... | collective-permute-start | bytes 73736 | tf_op jit(solution)/shard_map/ppermute | solution.py:291
  863.6 3.9 collective-permute-start.1
  867.5 5.4 collective-permute-start.2
  (13 other events, 190.3 us)
Sparse Core Ops, SparseCore 0:
  13.7 52.7 all-gather.6
  140.7 53.6 reduce-scatter.8
  197.3 53.0 reduce-scatter.6
  251.8 49.5 all-gather.10
  303.4 50.1 all-gather.8
  384.7 50.1 all-gather.12
  482.6 53.6 reduce-scatter.12
  539.2 53.0 reduce-scatter.10
  598.3 49.5 all-gather.14
  661.1 49.5 all-gather.16
  731.3 53.6 reduce-scatter.16
  787.2 53.0 reduce-scatter.14

commit v2 on v1

--- a/solution.py
+++ b/solution.py
@@ -267,6 +267,282 @@
     )(attn_out, hidden, dy_full, *previous)
 
 
+MESH = pl.DeviceIdType.MESH
+CORES = 2
+
+
+def ring_place(chips):
+    me = lax.axis_index('tp')
+    chip, core = me // CORES, lax.rem(me, CORES)
+    left, right = lax.rem(chip + chips - 1, chips), lax.rem(chip + 1, chips)
+    return chip, core, (chip * CORES + 1 - core, left * CORES + core, right * CORES + core)
+
+
+def enter_ring(peers):
+    barrier = pltpu.get_barrier_semaphore()
+    for peer in peers:
+        pl.semaphore_signal(barrier, inc=1, device_id={'tp': peer}, device_id_type=MESH)
+    pl.semaphore_wait(barrier, len(peers))
+
+
+def remote(src, dst, send, recv, index, peer):
+    return pltpu.make_async_remote_copy(src_ref=src, dst_ref=dst, send_sem=send.at[index], recv_sem=recv.at[index], device_id={'tp': peer}, device_id_type=MESH)
+
+
+def ring_gather(chips, loc_ref, full, send, recv, consume):
+    n_rows = loc_ref.shape[0]
+    half = n_rows // 2
+    chip, core, (partner, left, right) = ring_place(chips)
+    left_chip, right_chip, far_chip = lax.rem(chip + chips - 1, chips), lax.rem(chip + 1, chips), lax.rem(chip + 2, chips)
+
+    def rows(chip_idx, core_idx, first=0, count=n_rows):
+        return full.at[pl.ds(pl.multiple_of((chip_idx * CORES + core_idx) * n_rows + first, half), count)]
+
+    low, high = (0, half), (half, half)
+    own_low, own_high = loc_ref.at[pl.ds(0, half)], loc_ref.at[pl.ds(half, half)]
+    sends = [
+        remote(own_low, rows(chip, core, *low), send, recv, 0, right),
+        remote(own_high, rows(chip, core, *high), send, recv, 1, left),
+        remote(own_high, rows(chip, core, *high), send, recv, 2, right),
+        remote(own_low, rows(chip, core, *low), send, recv, 3, left),
+        remote(rows(left_chip, core, *low), rows(left_chip, core, *low), send, recv, 4, right),
+        remote(rows(right_chip, core, *high), rows(right_chip, core, *high), send, recv, 5, left),
+        remote(loc_ref, rows(chip, core), send, recv, 6, partner),
+        remote(rows(left_chip, core), rows(left_chip, core), send, recv, 7, partner),
+        remote(rows(right_chip, core), rows(right_chip, core), send, recv, 8, partner),
+        remote(rows(far_chip, core), rows(far_chip, core), send, recv, 9, partner),
+    ]
+    landing = [
+        rows(left_chip, core, *low), rows(right_chip, core, *high), rows(left_chip, core, *high), rows(right_chip, core, *low),
+        rows(far_chip, core, *low), rows(far_chip, core, *high), rows(chip, 1 - core), rows(left_chip, 1 - core), rows(right_chip, 1 - core),
+        rows(far_chip, 1 - core),
+    ]
+
+    def arrived(index):
+        remote(landing[index], landing[index], send, recv, index, partner).wait_recv()
+
+    enter_ring((partner, left, right))
+    for index in (0, 1, 2, 3, 6):
+        sends[index].start()
+    full[pl.ds(pl.multiple_of((chip * CORES + core) * n_rows, n_rows), n_rows), :] = loc_ref[...]
+    arrived(6)
+    consume(0, chip)
+    arrived(0)
+    sends[4].start()
+    arrived(1)
+    sends[5].start()
+    arrived(2)
+    sends[7].start()
+    arrived(3)
+    sends[8].start()
+    arrived(7)
+    consume(1, left_chip)
+    arrived(8)
+    consume(2, right_chip)
+    arrived(4)
+    arrived(5)
+    sends[9].start()
+    arrived(9)
+    consume(3, far_chip)
+    for copy in sends:
+        copy.wait_send()
+
+
+def gather_dots_kernel(chips, layer, forward, n_outs, tile, loc_ref, *refs):
+    n_weights = 3 if forward else 2
+    n_inputs = 3 if forward else 4
+    inputs, outs = refs[:n_inputs], refs[n_inputs:n_inputs + n_outs]
+    full, scratch = refs[n_inputs + n_outs], refs[n_inputs + n_outs + 1:]
+    held, staged = scratch[:n_inputs], scratch[n_inputs:-4]
+    load_sem, store_sem, send, recv = scratch[-4:]
+    chip_rows = CORES * loc_ref.shape[0]
+    loads = [pltpu.make_async_copy(src.at[layer] if idx < n_weights else src, dst, load_sem.at[idx]) for idx, (src, dst) in enumerate(zip(inputs, held))]
+    for load in loads:
+        load.start()
+    stores = []
+
+    def consume(step, chip_idx):
+        rows = pl.ds(pl.multiple_of(chip_idx * chip_rows, chip_rows), chip_rows)
+        if not step:
+            loads[0].wait()
+        first = staged[0]
+        first[rows, :] = dot(full[rows, :], held[0][...], MATMUL if forward else CONTRACT_LAST).astype(BF16)
+        if not step:
+            for load in loads[1:]:
+                load.wait()
+
+        def one_tile(idx, carry):
+            cols = pl.ds(pl.multiple_of(idx * tile, tile), tile)
+            if forward:
+                gate = dot(full[rows, :], held[1][:, cols], MATMUL).astype(BF16)
+                up = dot(full[rows, :], held[2][:, cols], MATMUL).astype(BF16)
+                staged[1][rows, cols] = gate
+                staged[2][rows, cols] = up
+                if n_outs > 3:
+                    staged[3][rows, cols] = gated(gate.astype(F32), up.astype(F32)).astype(BF16)
+            else:
+                d_hidden = dot(full[rows, :], held[1][cols, :], CONTRACT_LAST).astype(BF16).astype(F32)
+                hidden, pull = jax.vjp(gated, held[2][rows, cols].astype(F32), held[3][rows, cols].astype(F32))
+                d_gate, d_up = pull(d_hidden)
+                staged[1][rows, cols] = hidden.astype(BF16)
+                staged[2][rows, cols] = d_gate.astype(BF16)
+                staged[3][rows, cols] = d_up.astype(BF16)
+            return carry
+
+        lax.fori_loop(0, staged[1].shape[1] // tile, one_tile, 0)
+        for idx, out in enumerate(outs):
+            source = full if idx == len(staged) else staged[idx]
+            copy = pltpu.make_async_copy(source.at[rows], out.at[rows], store_sem.at[step, idx])
+            copy.start()
+            stores.append(copy)
+
+    ring_gather(chips, loc_ref, full, send, recv, consume)
+    for copy in stores:
+        copy.wait()
+
+
+def gather_dots(loc, inputs, layer, forward, with_hidden, tp_size, collective_id, name, tile=256):
+    n_rows, depth = loc.shape
+    seq_len, chips = n_rows * tp_size, tp_size // CORES
+    n_weights = 3 if forward else 2
+    weights, saved = inputs[:n_weights], inputs[n_weights:]
+    if forward:
+        widths = [weight.shape[2] for weight in weights] + ([weights[1].shape[2]] if with_hidden else [])
+    else:
+        widths = [weights[0].shape[1]] + [weights[1].shape[1]] * 3
+    staged = [pltpu.VMEM((seq_len, width), BF16) for width in widths]
+    outs = [jax.ShapeDtypeStruct((seq_len, width), BF16) for width in widths + ([] if forward else [depth])]
+    n_cols = sum(weight.size // (weight.shape[0] * depth) for weight in weights)
+    return pl.pallas_call(
+        functools.partial(gather_dots_kernel, chips, layer, forward, len(outs), tile),
+        out_shape=outs,
+        in_specs=[pl.BlockSpec(memory_space=pltpu.VMEM)] + [pl.BlockSpec(memory_space=pl.ANY)] * len(inputs),
+        out_specs=[pl.BlockSpec(memory_space=pl.ANY)] * len(outs),
+        scratch_shapes=[pltpu.VMEM((seq_len, depth), BF16)]
+        + [pltpu.VMEM(weight.shape[1:], BF16) for weight in weights]
+        + [pltpu.VMEM(item.shape, BF16) for item in saved]
+        + staged
+        + [pltpu.SemaphoreType.DMA((len(inputs),)), pltpu.SemaphoreType.DMA((4, len(outs))), pltpu.SemaphoreType.DMA((10,)), pltpu.SemaphoreType.DMA((10,))],
+        compiler_params=pltpu.CompilerParams(vmem_limit_bytes=VMEM_LIMIT, collective_id=collective_id, has_side_effects=True),
+        cost_estimate=cost(2 * seq_len * depth * n_cols, 2 * (seq_len * depth + depth * n_cols + seq_len * n_cols)),
+        name=name,
+    )(loc, *inputs)
+
+
+SCATTER_ORDER = ((0, 0), (0, 1), (1, 0), (2, 1), (1, 1), (2, 0), (3, 0), (3, 1))
+
+
+def dots_scatter_kernel(chips, layer, dims, n_terms, tile, *refs):
+    lhs_refs, rhs_refs, out_ref = refs[:n_terms], refs[n_terms:2 * n_terms], refs[2 * n_terms]
+    held, scratch = refs[2 * n_terms + 1:3 * n_terms + 1], refs[3 * n_terms + 1:]
+    part, from_core, acc, from_far, from_side, load_sem, core_send, core_recv, send, recv = scratch
+    n_rows, n_cols = out_ref.shape
+    half = n_cols // 2
+    chip, core, (partner, left, right) = ring_place(chips)
+    dest_chips = [lax.rem(chip + offset, chips) for offset in (2, chips - 1, 1, 0)]
+
+    def half_of(ref, which):
+        cols = pl.ds(which * half, half)
+        return ref.at[:, cols] if dims is MATMUL else ref.at[cols, :]
+
+    loads = [
+        [pltpu.make_async_copy(half_of(src.at[layer], which), half_of(dst, which), load_sem.at[idx, which]) for idx, (src, dst) in enumerate(zip(rhs_refs, held))]
+        for which in range(2)
+    ]
+    for group in loads:
+        for load in group:
+            load.start()
+    enter_ring((partner, left, right))
+    to_core = [remote(part.at[item % 2, 1 - core], from_core.at[item], core_send, core_recv, item, partner) for item in range(len(SCATTER_ORDER))]
+    hops = {
+        (0, 0): remote(acc.at[0, 0], from_far.at[0], send, recv, 0, right),
+        (0, 1): remote(acc.at[0, 1], from_far.at[1], send, recv, 1, left),
+        (1, 0): remote(acc.at[1, 0], from_side.at[1, 0], send, recv, 2, left),
+        (2, 1): remote(acc.at[2, 1], from_side.at[0, 1], send, recv, 3, right),
+        (1, 1): remote(acc.at[1, 1], from_side.at[1, 1], send, recv, 4, left),
+        (2, 0): remote(acc.at[2, 0], from_side.at[0, 0], send, recv, 5, right),
+    }
+
+    def compute(item):
+        step, which = SCATTER_ORDER[item]
+        rows = pl.ds(pl.multiple_of(dest_chips[step] * (CORES * n_rows), CORES * n_rows), CORES * n_rows)
+        if item < 2:
+            for load in loads[which]:
+                load.wait()
+        if item >= 2:
+            to_core[item - 2].wait_send()
+
+        def one_tile(idx, carry):
+            first = pl.multiple_of(idx * tile, tile)
+            rhs_cols = pl.ds(which * half + first, tile)
+            total = None
+            for lhs_ref, rhs_ref in zip(lhs_refs, held):
+                rhs = rhs_ref[:, rhs_cols] if dims is MATMUL else rhs_ref[rhs_cols, :]
+                product = dot(lhs_ref[rows, :], rhs, dims)
+                total = product if total is None else total + product
+            for idx_core in range(CORES):
+                part[item % 2, idx_core, :, pl.ds(first, tile)] = total[idx_core * n_rows:(idx_core + 1) * n_rows]
+            return carry
+
+        lax.fori_loop(0, half // tile, one_tile, 0)
+        to_core[item].start()
+
+    def add_core(item):
+        step, which = SCATTER_ORDER[item]
+        to_core[item].wait_recv()
+        acc[step, which] = part[item % 2, core] + from_core[item]
+        if item < 4:
+            hops[step, which].start()
+
+    n_items = len(SCATTER_ORDER)
+    for item in range(n_items):
+        compute(item)
+        if item:
+            add_core(item - 1)
+    add_core(n_items - 1)
+    for which, step in ((0, 2), (1, 1)):
+        hops[0, which].wait_recv()
+        acc[step, which] = acc[step, which] + from_far[which]
+        hops[step, which].start()
+    for key in ((1, 0), (2, 1), (1, 1), (2, 0)):
+        hops[key].wait_recv()
+    for which in range(2):
+        out_ref[:, pl.ds(which * half, half)] = acc[3, which] + from_side[0, which] + from_side[1, which]
+    for copy in to_core[-2:]:
+        copy.wait_send()
+    for copy in hops.values():
+        copy.wait_send()
+
+
+def dots_scatter(terms, layer, dims, tp_size, collective_id, name, tile=512):
+    seq_len = terms[0][0].shape[0]
+    n_cols = terms[0][1].shape[2] if dims is MATMUL else terms[0][1].shape[1]
+    n_rows, half = seq_len // tp_size, n_cols // 2
+    depth = sum(lhs.shape[1] for lhs, _ in terms)
+    return pl.pallas_call(
+        functools.partial(dots_scatter_kernel, tp_size // CORES, layer, dims, len(terms), tile),
+        out_shape=jax.ShapeDtypeStruct((n_rows, n_cols), F32),
+        in_specs=[pl.BlockSpec(memory_space=pltpu.VMEM)] * len(terms) + [pl.BlockSpec(memory_space=pl.ANY)] * len(terms),
+        out_specs=pl.BlockSpec(memory_space=pltpu.VMEM),
+        scratch_shapes=[pltpu.VMEM(rhs.shape[1:], BF16) for _, rhs in terms]
+        + [
+            pltpu.VMEM((2, CORES, n_rows, half), F32),
+            pltpu.VMEM((len(SCATTER_ORDER), n_rows, half), F32),
+            pltpu.VMEM((4, 2, n_rows, half), F32),
+            pltpu.VMEM((2, n_rows, half), F32),
+            pltpu.VMEM((2, 2, n_rows, half), F32),
+            pltpu.SemaphoreType.DMA((len(terms), 2)),
+            pltpu.SemaphoreType.DMA((len(SCATTER_ORDER),)),
+            pltpu.SemaphoreType.DMA((len(SCATTER_ORDER),)),
+            pltpu.SemaphoreType.DMA((6,)),
+            pltpu.SemaphoreType.DMA((6,)),
+        ],
+        compiler_params=pltpu.CompilerParams(vmem_limit_bytes=VMEM_LIMIT, collective_id=collective_id, has_side_effects=True),
+        cost_estimate=cost(2 * seq_len * depth * n_cols, 2 * depth * (seq_len + n_cols) + 4 * n_rows * n_cols),
+        name=name,
+    )(*[lhs for lhs, _ in terms], *[rhs for _, rhs in terms])
+
+
 def gather_rows(rows_loc):
     return lax.all_gather(rows_loc, 'tp', axis=0, tiled=True)
 
@@ -301,40 +577,26 @@
         cos_tab, sin_tab = rope_tables(seq_len)
         saved_all = []
         x_cur = x_loc
-        dy_full = None
         for layer in range(n_layers):
             last = layer == n_layers - 1
             x_f32 = x_cur.astype(F32)
             u_loc = rms_scale(x_f32, norm_gain[layer]).astype(BF16)
-            u_full = gather_rows(u_loc)
-            if dy_full is None:
-                dy_full = gather_rows(after(dy_loc, u_full))
-            qkv = jnp.dot(u_full, w_qkv[layer], preferred_element_type=F32).astype(BF16)
+            outs = gather_dots(u_loc, (w_qkv, w_gate, w_up), layer, True, not last, tp_size, layer, "gather_in")
+            qkv, gate, up = outs[:3]
             rot, attn_out, lse = attn_fwd(qkv, cos_tab, sin_tab, group)
-            gate = jnp.dot(u_full, w_gate[layer], preferred_element_type=F32).astype(BF16)
-            up = jnp.dot(u_full, w_up[layer], preferred_element_type=F32).astype(BF16)
             saved_all.append((x_cur, u_loc, rot, attn_out, lse, gate, up))
             if not last:
-                hidden = gated(gate.astype(F32), up.astype(F32)).astype(BF16)
-                parts = [
-                    sum_of_dots([(attn_out, w_out), (hidden, w_down)], layer, MATMUL, idx * chunk_cols, chunk_cols, 512, "block_out")
-                    for idx in range(n_chunks)
-                ]
-                x_cur = (x_f32 + reduce_rows(parts)).astype(BF16)
+                block_sum = dots_scatter([(attn_out, w_out), (outs[3], w_down)], layer, MATMUL, tp_size, n_layers + layer, "scatter_out")
+                x_cur = (x_f32 + block_sum).astype(BF16)
 
         in_grads, out_grads, gain_grads = (), (), []
         for layer in reversed(range(n_layers)):
             x_in, u_loc, rot, attn_out, lse, gate, up = saved_all[layer]
-            if layer < n_layers - 1:
-                dy_full, in_grads, out_grads = lax.optimization_barrier((gather_rows(dy_loc), in_grads, out_grads))
-            d_attn = lax.dot_general(dy_full, w_out[layer], CONTRACT_LAST, preferred_element_type=F32).astype(BF16)
-            d_hidden = lax.dot_general(dy_full, w_down[layer], CONTRACT_LAST, preferred_element_type=F32).astype(BF16)
-            hidden_f32, gated_pull = jax.vjp(gated, gate.astype(F32), up.astype(F32))
-            hidden = hidden_f32.astype(BF16)
-            d_gate, d_up = [item.astype(BF16) for item in gated_pull(d_hidden.astype(F32))]
+            dy_send, rot = lax.optimization_barrier((dy_loc, rot))
+            d_attn, hidden, d_gate, d_up, dy_full = gather_dots(dy_send, (w_out, w_down, gate, up), layer, False, True, tp_size, 2 * n_layers + layer, "gather_back")
             u_full = gather_rows(after(u_loc, attn_out, d_attn))
             d_qkv = attn_bwd(rot, lse, d_attn, cos_tab, sin_tab, group)
-            d_qkv, d_gate, d_up, hidden, u_full = lax.optimization_barrier((d_qkv, d_gate, d_up, hidden, u_full))
+            d_qkv, u_full = lax.optimization_barrier((d_qkv, u_full))
             parts = [
                 sum_of_dots([(d_qkv, w_qkv), (d_gate, w_gate), (d_up, w_up)], layer, CONTRACT_LAST, idx * chunk_cols, chunk_cols, 512, "block_in_back")
                 for idx in range(n_chunks)
@@ -343,7 +605,8 @@
             parts[-1] = held[0]
             in_grads = grad_in(u_full, held[1:4], layer, n_layers, in_grads)
             out_grads = grad_out(held[5], held[4], dy_full, layer, n_layers, out_grads)
-            d_normed = reduce_rows(parts).astype(BF16)
+            d_normed, in_grads, out_grads = lax.optimization_barrier((reduce_rows(parts), in_grads, out_grads))
+            d_normed = d_normed.astype(BF16)
             norm_pull = jax.vjp(rms_scale, x_in.astype(F32), norm_gain[layer])[1]
             d_x_norm, gain_grad = norm_pull(d_normed.astype(F32))
             dy_loc = (dy_loc.astype(F32) + d_x_norm).astype(BF16)

time: 885 us -> 774 us (0.87)
  Pallas kernels: 306 us -> 607 us
  waiting for transfers between devices: 386 us -> 121 us
  matrix products: 142 us -> 0 us
    pallas_call x0 -> x5, Pallas kernels: none -> 326 us  [the longest x4 233 us: gather_dots(): pl.pallas_call(functools.partial(gather_dots_kernel, chips, layer, forwar...]
    reduce_scatter x6 -> x4, waiting for transfers between devices: 238 us -> 69.9 us  [reduce_rows(): lax.psum_scatter(chunk, 'tp', scatter_dimension=0, tiled=True)]
    dot_general x10 -> x0, matrix products: 142 us -> none  [the longest x2 34.6 us: device_program(): lax.dot_general(dy_full, w_down[layer], CONTRACT_LAST, preferred_element_...]
    all_gather x6 -> x2, waiting for transfers between devices: 141 us -> 44.3 us  [gather_rows(): return lax.all_gather(rows_loc, 'tp', axis=0, tiled=True)]
    pallas_call x6 -> x4, Pallas kernels: 107 us -> 82.5 us  [sum_of_dots(): pl.pallas_call(functools.partial(sum_of_dots_kernel, dims, len(terms)), o...]
  transfers between devices with their start and end apart: 15 -> 9, of which waited for: 11 -> 7; matrix products, arithmetic and copies ran while one was open for 10% -> 0% of each run, Pallas kernels for 24% -> 26%
where the time goes in v2:
time: 774 us; the launch traced here: 769 us
  Pallas kernels  607 us (78%)
  waiting for transfers between devices  121 us (16%)
  other arithmetic  22.1 us (3%)
  between operations  14.8 us (2%)
    pallas_call x4, Pallas kernels, gather_dots(): pl.pallas_call(functools.partial(gather_dots_kernel, chips, layer, forwar...  233 us
    pallas_call x1, Pallas kernels, dots_scatter(): pl.pallas_call(functools.partial(dots_scatter_kernel, tp_size // CORES, l...  92.5 us
    pallas_call x4, Pallas kernels, sum_of_dots(): pl.pallas_call(functools.partial(sum_of_dots_kernel, dims, len(terms)), o...  82.5 us
    reduce_scatter x4, waiting for transfers between devices, reduce_rows(): lax.psum_scatter(chunk, 'tp', scatter_dimension=0, tiled=True)  69.9 us
    pallas_call x2, Pallas kernels, grad_in(): pl.pallas_call(functools.partial(grad_in_kernel, n_rhs), out_shape=shapes...  66.4 us
    pallas_call x2, Pallas kernels, attn_bwd(): pl.pallas_call(functools.partial(attn_bwd_kernel, group), out_shape=jax.S...  54.3 us
    all_gather x2, waiting for transfers between devices, gather_rows(): return lax.all_gather(rows_loc, 'tp', axis=0, tiled=True)  44.3 us
    pallas_call x2, Pallas kernels, grad_out(): pl.pallas_call(grad_out_kernel, out_shape=(jax.ShapeDtypeStruct((n_layers...  40.2 us
  transfers between devices with their start and end apart: 9, of which 7 were waited for; matrix products, arithmetic and copies ran while one was open for 0% of the time, Pallas kernels for 26%

profile of v2, /device:TPU:112, one launch (start us, length us, event | category | flops | bytes accessed | tf_op | source)
XLA Modules:
  0.0 768.6 jit_solution(15392957811737090941)
XLA Ops:
  10.4 2.9 fusion.19
  16.4 62.9 %gather_in.2 = (bf16[1536,640]{1,0:T(8,128)(2,1)}, bf16[1536,1024]{1,0:T(8,128)(2,1)}, bf16[1536,1024]{1,0:T(8,128)(2,1)}, bf16[1536,1024]{1,0:T(8,128)(2,1)}) custom-call(bf16[192,3072]{1,0:T(8,128)(2,1)} %fusion.4.loc_ref, bf16[2,3072,640]{2,1,0:T(8,128)(2,1)} %refs_3_.9, bf16[2,3072,1024]{2,1,0:T(8,128)(2,1)} %refs_4_.7, bf16[2,3072,1024]{2,1,0:T(8,128)(2,1)} %refs_5_.7), custom_call_target="tpu_custom_call" | custom-call | flops 25367150592 | bytes 34209792 | tf_op jit(solution)/shard_map/gather_in/pallas_call | solution.py:416
  79.3 18.9 %attn_fwd.2 = (bf16[1536,640]{1,0:T(8,128)(2,1)}, bf16[1536,384]{1,0:T(8,128)(2,1)}, f32[1536,384]{1,0:T(8,128)}) custom-call(bf16[1536,640]{1,0:T(8,128)(2,1)} %get-tuple-element.74.qkv_ref, f32[1536,128]{1,0:T(8,128)} %get-tuple-element.152.cos_ref, f32[1536,128]{1,0:T(8,128)} %get-tuple-element.153.sin_ref), custom_call_target="tpu_custom_call" | custom-call | flops 3623878656 | bytes 7864320 | tf_op jit(solution)/shard_map/attn_fwd/pallas_call | solution.py:102
  98.2 92.5 %scatter_out.1 = f32[192,3072]{1,0:T(8,128)} custom-call(bf16[1536,384]{1,0:T(8,128)(2,1)} %get-tuple-element.128.refs_0_.attn_ref, bf16[1536,1024]{1,0:T(8,128)(2,1)} %get-tuple-element.76.refs_1_, bf16[2,384,3072]{2,1,0:T(8,128)(2,1)} %refs_0_.7, bf16[2,1024,3072]{2,1,0:T(8,128)(2,1)} %refs_1_.7), custom_call_target="tpu_custom_call" | custom-call | flops 13287555072 | bytes 15335424 | tf_op jit(solution)/shard_map/scatter_out/pallas_call | solution.py:522
  190.7 2.1 fusion.12
  194.2 61.4 %gather_in.3 = (bf16[1536,640]{1,0:T(8,128)(2,1)}, bf16[1536,1024]{1,0:T(8,128)(2,1)}, bf16[1536,1024]{1,0:T(8,128)(2,1)}) custom-call(bf16[192,3072]{1,0:T(8,128)(2,1)} %fusion.5.loc_ref, bf16[2,3072,640]{2,1,0:T(8,128)(2,1)} %refs_3_.9, bf16[2,3072,1024]{2,1,0:T(8,128)(2,1)} %refs_4_.7, bf16[2,3072,1024]{2,1,0:T(8,128)(2,1)} %refs_5_.7), custom_call_target="tpu_custom_call" | custom-call | flops 25367150592 | bytes 34209792 | tf_op jit(solution)/shard_map/gather_in/pallas_call | solution.py:416
  255.7 18.8 %attn_fwd.3 = (bf16[1536,640]{1,0:T(8,128)(2,1)}, bf16[1536,384]{1,0:T(8,128)(2,1)}, f32[1536,384]{1,0:T(8,128)}) custom-call(bf16[1536,640]{1,0:T(8,128)(2,1)} %get-tuple-element.77.qkv_ref, f32[1536,128]{1,0:T(8,128)} %get-tuple-element.152.cos_ref, f32[1536,128]{1,0:T(8,128)} %get-tuple-element.153.sin_ref), custom_call_target="tpu_custom_call" | custom-call | flops 3623878656 | bytes 7864320 | tf_op jit(solution)/shard_map/attn_fwd/pallas_call | solution.py:102
  274.5 54.5 %gather_back.2 = (bf16[1536,384]{1,0:T(8,128)(2,1)}, bf16[1536,1024]{1,0:T(8,128)(2,1)}, bf16[1536,1024]{1,0:T(8,128)(2,1)}, bf16[1536,1024]{1,0:T(8,128)(2,1)}, bf16[1536,3072]{1,0:T(8,128)(2,1)}) custom-call(bf16[192,3072]{1,0:T(8,128)(2,1)} %loc_ref, bf16[2,384,3072]{2,1,0:T(8,128)(2,1)} %refs_0_.7, bf16[2,1024,3072]{2,1,0:T(8,128)(2,1)} %refs_1_.7, ...), custom_call_target="tpu_custom_call" | custom-call | flops 13287555072 | bytes 22413312 | tf_op jit(solution)/shard_map/gather_back/pallas_call | solution.py:416
  329.2 27.2 %attn_bwd.2.refs_0_.refs_1_ = bf16[1536,640]{1,0:T(8,128)(2,1)} custom-call(bf16[1536,640]{1,0:T(8,128)(2,1)} %get-tuple-element.79.rot_ref, f32[1536,384]{1,0:T(8,128)} %get-tuple-element.80.lse_ref, bf16[1536,384]{1,0:T(8,128)(2,1)} %get-tuple-element.84.dout_ref, f32[1536,128]{1,0:T(8,128)} %get-tuple-element.152.cos_ref, ...), custom_call_target="tpu_custom_call" | custom-call | flops 9059696640 | bytes 7864320 | tf_op jit(solution)/shard_map/attn_bwd/pallas_call | solution.py:168
  356.3 22.4 %all-gather.3.cloned.1.call-done.refs_0_ = bf16[1536,3072]{1,0:T(8,128)(2,1)} async-done(((bf16[192,3072]{1,0:T(8,128)(2,1)}), bf16[1536,3072]{1,0:T(8,128)(2,1)}) %all-gather.3.cloned.1.call-update) | async-done | bytes 9437200 | tf_op jit(solution)/shard_map/all_gather | solution.py:547
  378.7 20.6 %block_in_back.5 = f32[1536,1536]{1,0:T(8,128)} custom-call(bf16[1536,640]{1,0:T(8,128)(2,1)} %attn_bwd.2.refs_0_.refs_1_, bf16[1536,1024]{1,0:T(8,128)(2,1)} %get-tuple-element.94.refs_1_.refs_2_, bf16[1536,1024]{1,0:T(8,128)(2,1)} %get-tuple-element.95.refs_2_.refs_3_, bf16[2,3072,640]{2,1,0:T(8,128)(2,1)} %refs_3_.9, bf16[2,3072,1024]{2,1,0:T(8,128)(2,1)} %refs_4_.7, ...), custom_call_target="tpu_custom_call" | custom-call | flops 12683575296 | bytes 25952256 | tf_op jit(solution)/shard_map/block_in_back/pallas_call | solution.py:196
  399.4 20.8 %block_in_back.4 = f32[1536,1536]{1,0:T(8,128)} custom-call(bf16[1536,640]{1,0:T(8,128)(2,1)} %attn_bwd.2.refs_0_.refs_1_, bf16[1536,1024]{1,0:T(8,128)(2,1)} %get-tuple-element.94.refs_1_.refs_2_, bf16[1536,1024]{1,0:T(8,128)(2,1)} %get-tuple-element.95.refs_2_.refs_3_, bf16[2,3072,640]{2,1,0:T(8,128)(2,1)} %refs_3_.9, bf16[2,3072,1024]{2,1,0:T(8,128)(2,1)} %refs_4_.7, ...), custom_call_target="tpu_custom_call" | custom-call | flops 12683575296 | bytes 25952256 | tf_op jit(solution)/shard_map/block_in_back/pallas_call | solution.py:196
  420.3 20.1 %grad_out.2 = (bf16[2,384,3072]{2,1,0:T(8,128)(2,1)}, bf16[2,1024,3072]{2,1,0:T(8,128)(2,1)}) custom-call(bf16[1536,384]{1,0:T(8,128)(2,1)} %get-tuple-element.99.attn_ref, bf16[1536,1024]{1,0:T(8,128)(2,1)} %get-tuple-element.100.hidden_ref, bf16[1536,3072]{1,0:T(8,128)(2,1)} %get-tuple-element.101.dy_ref), custom_call_target="tpu_custom_call" | custom-call | flops 13287555072 | bytes 22413312 | tf_op jit(solution)/shard_map/grad_out/pallas_call | solution.py:249
  440.5 33.1 %grad_in.2 = (bf16[2,3072,640]{2,1,0:T(8,128)(2,1)}, bf16[2,3072,1024]{2,1,0:T(8,128)(2,1)}, bf16[2,3072,1024]{2,1,0:T(8,128)(2,1)}) custom-call(bf16[1536,3072]{1,0:T(8,128)(2,1)} %all-gather.3.cloned.1.call-done.refs_0_, bf16[1536,640]{1,0:T(8,128)(2,1)} %attn_bwd.2.refs_0_.refs_1_, bf16[1536,1024]{1,0:T(8,128)(2,1)} %get-tuple-element.94.refs_1_.refs_2_, ...), custom_call_target="tpu_custom_call" | custom-call | flops 25367150592 | bytes 34209792 | tf_op jit(solution)/shard_map/grad_in/pallas_call | solution.py:221
  473.6 35.0 %reduce-scatter.5.cloned.1.call-done = f32[192,1536]{1,0:T(8,128)} async-done(((f32[1536,1536]{1,0:T(8,128)}), f32[192,1536]{1,0:T(8,128)}) %reduce-scatter.5.cloned.1.call-update) | async-done | bytes 1179664 | tf_op jit(solution)/shard_map/reduce_scatter | solution.py:555
  513.7 54.3 %gather_back.3 = (bf16[1536,384]{1,0:T(8,128)(2,1)}, bf16[1536,1024]{1,0:T(8,128)(2,1)}, bf16[1536,1024]{1,0:T(8,128)(2,1)}, bf16[1536,1024]{1,0:T(8,128)(2,1)}, bf16[1536,3072]{1,0:T(8,128)(2,1)}) custom-call(bf16[192,3072]{1,0:T(8,128)(2,1)} %fusion.9.loc_ref, bf16[2,384,3072]{2,1,0:T(8,128)(2,1)} %refs_0_.7, bf16[2,1024,3072]{2,1,0:T(8,128)(2,1)} %refs_1_.7, ...), custom_call_target="tpu_custom_call" | custom-call | flops 13287555072 | bytes 22413312 | tf_op jit(solution)/shard_map/gather_back/pallas_call | solution.py:416
  568.2 27.1 %attn_bwd.3.refs_0_.refs_1_ = bf16[1536,640]{1,0:T(8,128)(2,1)} custom-call(bf16[1536,640]{1,0:T(8,128)(2,1)} %get-tuple-element.106.rot_ref, f32[1536,384]{1,0:T(8,128)} %get-tuple-element.107.lse_ref, bf16[1536,384]{1,0:T(8,128)(2,1)} %get-tuple-element.111.dout_ref, f32[1536,128]{1,0:T(8,128)} %get-tuple-element.152.cos_ref, ...), custom_call_target="tpu_custom_call" | custom-call | flops 9059696640 | bytes 7864320 | tf_op jit(solution)/shard_map/attn_bwd/pallas_call | solution.py:168
  595.3 21.9 %all-gather.5.cloned.1.call-done.refs_0_ = bf16[1536,3072]{1,0:T(8,128)(2,1)} async-done(((bf16[192,3072]{1,0:T(8,128)(2,1)}), bf16[1536,3072]{1,0:T(8,128)(2,1)}) %all-gather.5.cloned.1.call-update) | async-done | bytes 9437200 | tf_op jit(solution)/shard_map/all_gather | solution.py:547
  617.2 20.6 %block_in_back.7 = f32[1536,1536]{1,0:T(8,128)} custom-call(bf16[1536,640]{1,0:T(8,128)(2,1)} %attn_bwd.3.refs_0_.refs_1_, bf16[1536,1024]{1,0:T(8,128)(2,1)} %get-tuple-element.120.refs_1_.refs_2_, bf16[1536,1024]{1,0:T(8,128)(2,1)} %get-tuple-element.121.refs_2_.refs_3_, bf16[2,3072,640]{2,1,0:T(8,128)(2,1)} %refs_3_.9, bf16[2,3072,1024]{2,1,0:T(8,128)(2,1)} %refs_4_.7, ...), custom_call_target="tpu_custom_call" | custom-call | flops 12683575296 | bytes 25952256 | tf_op jit(solution)/shard_map/block_in_back/pallas_call | solution.py:196
  637.9 20.6 %block_in_back.6 = f32[1536,1536]{1,0:T(8,128)} custom-call(bf16[1536,640]{1,0:T(8,128)(2,1)} %attn_bwd.3.refs_0_.refs_1_, bf16[1536,1024]{1,0:T(8,128)(2,1)} %get-tuple-element.120.refs_1_.refs_2_, bf16[1536,1024]{1,0:T(8,128)(2,1)} %get-tuple-element.121.refs_2_.refs_3_, bf16[2,3072,640]{2,1,0:T(8,128)(2,1)} %refs_3_.9, bf16[2,3072,1024]{2,1,0:T(8,128)(2,1)} %refs_4_.7, ...), custom_call_target="tpu_custom_call" | custom-call | flops 12683575296 | bytes 25952256 | tf_op jit(solution)/shard_map/block_in_back/pallas_call | solution.py:196
  658.5 20.1 %grad_out.3 = (bf16[2,384,3072]{2,1,0:T(8,128)(2,1)}, bf16[2,1024,3072]{2,1,0:T(8,128)(2,1)}) custom-call(bf16[1536,384]{1,0:T(8,128)(2,1)} %get-tuple-element.128.refs_0_.attn_ref, bf16[1536,1024]{1,0:T(8,128)(2,1)} %get-tuple-element.129.hidden_ref, bf16[1536,3072]{1,0:T(8,128)(2,1)} %get-tuple-element.130.dy_ref, ...), custom_call_target="tpu_custom_call", output_to_operand_aliasing={{0}: (3, {}), {1}: (4, {})} | custom-call | flops 13287555072 | bytes 22413312 | tf_op jit(solution)/shard_map/grad_out/pallas_call | solution.py:249
  678.6 33.3 %grad_in.3 = (bf16[2,3072,640]{2,1,0:T(8,128)(2,1)}, bf16[2,3072,1024]{2,1,0:T(8,128)(2,1)}, bf16[2,3072,1024]{2,1,0:T(8,128)(2,1)}) custom-call(bf16[1536,3072]{1,0:T(8,128)(2,1)} %all-gather.5.cloned.1.call-done.refs_0_, bf16[1536,640]{1,0:T(8,128)(2,1)} %attn_bwd.3.refs_0_.refs_1_, ...), custom_call_target="tpu_custom_call", output_to_operand_aliasing={{0}: (4, {}), {1}: (5, {}), {2}: (6, {})} | custom-call | flops 25367150592 | bytes 34209792 | tf_op jit(solution)/shard_map/grad_in/pallas_call | solution.py:221
  712.0 34.8 %reduce-scatter.9.cloned.1.call-done = f32[192,1536]{1,0:T(8,128)} async-done(((f32[1536,1536]{1,0:T(8,128)}), f32[192,1536]{1,0:T(8,128)}) %reduce-scatter.9.cloned.1.call-update) | async-done | bytes 1179664 | tf_op jit(solution)/shard_map/reduce_scatter | solution.py:555
  751.7 3.6 collective-permute-done.1
  (59 shorter events, 24.2 us)
Async XLA Ops:
  7.2 6.2 copy-start
  7.2 371.5 %all-gather.3.cloned.1.call-start = ((), (), s32[]{:S(2)}) async-start(), calls=%async_computation.4 | async-start | bytes 10616832 | tf_op jit(solution)/shard_map/all_gather | solution.py:547
  8.9 0.6 copy-start.8
  9.5 3.8 copy-start.6
  10.4 3.0 copy-start.4
  329.1 144.5 %reduce-scatter.7.cloned.1.call-start = ((), (), s32[]{:S(2)}) async-start(), calls=%async_computation.6 | async-start | bytes 10616832 | tf_op jit(solution)/shard_map/reduce_scatter | solution.py:555
  399.4 109.2 %reduce-scatter.5.cloned.1.call-start = ((), (), s32[]{:S(2)}) async-start(), calls=%async_computation.5 | async-start | bytes 10616832 | tf_op jit(solution)/shard_map/reduce_scatter | solution.py:555
  420.3 196.9 %all-gather.5.cloned.1.call-start = ((), (), s32[]{:S(2)}) async-start(), calls=%async_computation.7 | async-start | bytes 10616832 | tf_op jit(solution)/shard_map/all_gather | solution.py:547
  473.6 38.2 %copy-start.3 = (bf16[192,3072]{1,0:T(8,128)(2,1)S(1)}, bf16[192,3072]{1,0:T(8,128)(2,1)}, u32[]{:S(2)}) copy-start(bf16[192,3072]{1,0:T(8,128)(2,1)} %loc_ref) | copy-start | bytes 3538948
  568.1 143.9 %reduce-scatter.11.cloned.1.call-start = ((), (), s32[]{:S(2)}) async-start(), calls=%async_computation.9 | async-start | bytes 10616832 | tf_op jit(solution)/shard_map/reduce_scatter | solution.py:555
  637.8 109.1 %reduce-scatter.9.cloned.1.call-start = ((), (), s32[]{:S(2)}) async-start(), calls=%async_computation.8 | async-start | bytes 10616832 | tf_op jit(solution)/shard_map/reduce_scatter | solution.py:555
  712.0 36.7 %copy-start.1 = (bf16[192,3072]{1,0:T(8,128)(2,1)S(1)}, bf16[192,3072]{1,0:T(8,128)(2,1)}, u32[]{:S(2)}) copy-start(bf16[192,3072]{1,0:T(8,128)(2,1)} %param.8) | copy-start | bytes 3538948
  712.0 36.7 %copy-start.5 = (f32[1,3072]{1,0:T(1,128)S(1)}, f32[1,3072]{1,0:T(1,128)}, u32[]{:S(2)}) copy-start(f32[1,3072]{1,0:T(1,128)} %copy-done.4) | copy-start | bytes 36868
  712.0 36.7 %copy-start.7 = (f32[192]{0:T(256)S(1)}, f32[192]{0:T(256)}, u32[]{:S(2)}) copy-start(f32[192]{0:T(256)} %copy-done.6) | copy-start | bytes 2308
  712.0 39.7 %copy-start.9 = (f32[192]{0:T(256)S(1)}, f32[192]{0:T(256)}, u32[]{:S(2)}) copy-start(f32[192]{0:T(256)} %copy-done.8) | copy-start | bytes 2308
  712.0 44.8 %copy-start.2 = (bf16[192,3072]{1,0:T(8,128)(2,1)S(1)}, bf16[192,3072]{1,0:T(8,128)(2,1)}, u32[]{:S(2)}) copy-start(bf16[192,3072]{1,0:T(8,128)(2,1)} %fusion.9.loc_ref) | copy-start | bytes 3538948
  750.1 1.3 collective-permute-start
  751.4 3.9 collective-permute-start.1
  755.3 5.4 collective-permute-start.2
Sparse Core Ops, SparseCore 0:
  329.2 49.4 all-gather.2
  399.5 53.6 reduce-scatter.6
  455.5 53.0 reduce-scatter.4
  568.2 48.8 all-gather.4
  637.9 53.6 reduce-scatter.10
  693.8 53.0 reduce-scatter.8

commit v3 on v2

--- a/solution.py
+++ b/solution.py
@@ -2,6 +2,7 @@
 
 import jax
 import jax.numpy as jnp
+import numpy as np
 from jax import lax
 from jax.experimental import pallas as pl
 from jax.experimental.pallas import tpu as pltpu
@@ -11,7 +12,7 @@
 NORM_EPS = 1e-5
 ROPE_BASE = 10000.0
 Q_BLOCK = 256
-VMEM_LIMIT = 60 * 1024 * 1024
+VMEM_LIMIT = 63 * 1024 * 1024
 F32 = jnp.float32
 BF16 = jnp.bfloat16
 
@@ -34,10 +35,10 @@
 
 def rope_tables(seq_len):
     half_dim = HEAD_DIM // 2
-    freqs = ROPE_BASE ** (-2.0 * jnp.arange(half_dim, dtype=F32) / HEAD_DIM)
-    angles = jnp.arange(seq_len, dtype=F32)[:, None] * freqs[None, :]
-    cos, sin = jnp.cos(angles), jnp.sin(angles)
-    return jnp.concatenate([cos, cos], axis=-1), jnp.concatenate([-sin, sin], axis=-1)
+    freqs = (ROPE_BASE ** (-2.0 * np.arange(half_dim) / HEAD_DIM)).astype(np.float32)
+    angles = (np.arange(seq_len, dtype=np.float32)[:, None] * freqs[None, :]).astype(np.float64)
+    cos, sin = np.cos(angles).astype(np.float32), np.sin(angles).astype(np.float32)
+    return jnp.asarray(np.concatenate([cos, cos], axis=-1)), jnp.asarray(np.concatenate([-sin, sin], axis=-1))
 
 
 def rms_scale(x_f32, gain_row):
@@ -175,62 +176,31 @@
     )(rot, lse, dout, cos_tab, sin_tab)
 
 
-def sum_of_dots_kernel(dims, n_terms, *refs):
-    out_ref = refs[-1]
-    total = dot(refs[0][...], refs[n_terms][...], dims)
-    for term in range(1, n_terms):
-        total = total + dot(refs[term][...], refs[n_terms + term][...], dims)
-    out_ref[...] = total
-
-
-def sum_of_dots(terms, layer, dims, first_col, n_cols, tile, name):
-    seq_len = terms[0][0].shape[0]
-    flops = sum(2 * seq_len * lhs.shape[1] * n_cols for lhs, _ in terms)
-    n_bytes = sum(2 * lhs.shape[1] * (seq_len + n_cols) for lhs, _ in terms) + 4 * seq_len * n_cols
-    first_tile = first_col // tile
-    lhs_specs = [pl.BlockSpec(lhs.shape, lambda step: (0, 0)) for lhs, _ in terms]
-    if dims is MATMUL:
-        rhs_specs = [pl.BlockSpec((None, rhs.shape[1], tile), lambda step: (layer, 0, first_tile + step)) for _, rhs in terms]
-    else:
-        rhs_specs = [pl.BlockSpec((None, tile, rhs.shape[2]), lambda step: (layer, first_tile + step, 0)) for _, rhs in terms]
-    return pl.pallas_call(
-        functools.partial(sum_of_dots_kernel, dims, len(terms)),
-        out_shape=jax.ShapeDtypeStruct((seq_len, n_cols), F32),
-        grid=(n_cols // tile,),
-        in_specs=lhs_specs + rhs_specs,
-        out_specs=pl.BlockSpec((seq_len, tile), lambda step: (0, step)),
-        compiler_params=params(),
-        cost_estimate=cost(flops, n_bytes),
-        name=name,
-    )(*[lhs for lhs, _ in terms], *[rhs for _, rhs in terms])
-
-
 def grad_in_kernel(n_rhs, *refs):
     lhs = refs[0][...]
-    rhs_refs, out_refs = refs[1:1 + n_rhs], refs[-n_rhs:]
-    for rhs_ref, out_ref in zip(rhs_refs, out_refs):
-        out_ref[...] = dot(lhs, rhs_ref[...], CONTRACT_FIRST).astype(BF16)
-
-
-def grad_in(lhs, rhs_list, layer, n_layers, previous, tile=512):
+    rhs_refs, done_refs, out_refs = refs[1:1 + n_rhs], refs[1 + n_rhs:-n_rhs], refs[-n_rhs:]
+    for idx, (rhs_ref, out_ref) in enumerate(zip(rhs_refs, out_refs)):
+        out_ref[0] = dot(lhs, rhs_ref[...], CONTRACT_FIRST).astype(BF16)
+        for place, done_ref in enumerate(done_refs[idx::n_rhs]):
+            out_ref[1 + place] = done_ref[...]
+
+
+def grad_in(lhs, rhs_list, done, tile=512):
     seq_len, depth = lhs.shape
-    n_rhs = len(rhs_list)
-    shapes = tuple(jax.ShapeDtypeStruct((n_layers, depth, rhs.shape[1]), BF16) for rhs in rhs_list)
+    n_rhs, n_layers = len(rhs_list), 1 + len(done)
     width = sum(rhs.shape[1] for rhs in rhs_list)
-    aliases = {1 + n_rhs + idx: idx for idx in range(n_rhs)} if previous else {}
     return pl.pallas_call(
         functools.partial(grad_in_kernel, n_rhs),
-        out_shape=shapes,
+        out_shape=[jax.ShapeDtypeStruct((n_layers, depth, rhs.shape[1]), BF16) for rhs in rhs_list],
         grid=(depth // tile,),
         in_specs=[pl.BlockSpec((seq_len, tile), lambda step: (0, step))]
-        + [pl.BlockSpec(rhs.shape, lambda step: (0, 0)) for rhs in rhs_list]
-        + [pl.BlockSpec(memory_space=pl.ANY) for _ in previous],
-        out_specs=[pl.BlockSpec((None, tile, rhs.shape[1]), lambda step: (layer, step, 0)) for rhs in rhs_list],
-        input_output_aliases=aliases,
+        + [pl.BlockSpec(rhs.shape, lambda step: (0, 0), pipeline_mode=pl.Buffered(1)) for rhs in rhs_list]
+        + [pl.BlockSpec((tile, item.shape[1]), lambda step: (step, 0)) for layer_done in done for item in layer_done],
+        out_specs=[pl.BlockSpec((n_layers, tile, rhs.shape[1]), lambda step: (0, step, 0)) for rhs in rhs_list],
         compiler_params=params(),
-        cost_estimate=cost(2 * seq_len * depth * width, 2 * (seq_len * depth + seq_len * width + depth * width)),
+        cost_estimate=cost(2 * seq_len * depth * width, 2 * (seq_len * depth + seq_len * width + (2 * n_layers - 1) * depth * width)),
         name="grad_in",
-    )(lhs, *rhs_list, *previous)
+    )(lhs, *rhs_list, *[item for layer_done in done for item in layer_done])
 
 
 def grad_out_kernel(attn_ref, hidden_ref, dy_ref, *refs):
@@ -295,55 +265,64 @@
     chip, core, (partner, left, right) = ring_place(chips)
     left_chip, right_chip, far_chip = lax.rem(chip + chips - 1, chips), lax.rem(chip + 1, chips), lax.rem(chip + 2, chips)
 
-    def rows(chip_idx, core_idx, first=0, count=n_rows):
-        return full.at[pl.ds(pl.multiple_of((chip_idx * CORES + core_idx) * n_rows + first, half), count)]
-
-    low, high = (0, half), (half, half)
-    own_low, own_high = loc_ref.at[pl.ds(0, half)], loc_ref.at[pl.ds(half, half)]
+    def first_row(chip_idx, core_idx, which):
+        return pl.multiple_of((chip_idx * CORES + core_idx) * n_rows + which * half, half)
+
+    def piece(chip_idx, core_idx, which):
+        return full.at[pl.ds(first_row(chip_idx, core_idx, which), half)]
+
+    def own(which):
+        return loc_ref.at[pl.ds(which * half, half)]
+
+    received = [(left_chip, 0), (right_chip, 1), (left_chip, 1), (right_chip, 0), (far_chip, 0), (far_chip, 1)]
     sends = [
-        remote(own_low, rows(chip, core, *low), send, recv, 0, right),
-        remote(own_high, rows(chip, core, *high), send, recv, 1, left),
-        remote(own_high, rows(chip, core, *high), send, recv, 2, right),
-        remote(own_low, rows(chip, core, *low), send, recv, 3, left),
-        remote(rows(left_chip, core, *low), rows(left_chip, core, *low), send, recv, 4, right),
-        remote(rows(right_chip, core, *high), rows(right_chip, core, *high), send, recv, 5, left),
-        remote(loc_ref, rows(chip, core), send, recv, 6, partner),
-        remote(rows(left_chip, core), rows(left_chip, core), send, recv, 7, partner),
-        remote(rows(right_chip, core), rows(right_chip, core), send, recv, 8, partner),
-        remote(rows(far_chip, core), rows(far_chip, core), send, recv, 9, partner),
+        remote(own(0), piece(chip, core, 0), send, recv, 0, right),
+        remote(own(1), piece(chip, core, 1), send, recv, 1, left),
+        remote(own(1), piece(chip, core, 1), send, recv, 2, right),
+        remote(own(0), piece(chip, core, 0), send, recv, 3, left),
+        remote(piece(left_chip, core, 0), piece(left_chip, core, 0), send, recv, 4, right),
+        remote(piece(right_chip, core, 1), piece(right_chip, core, 1), send, recv, 5, left),
     ]
-    landing = [
-        rows(left_chip, core, *low), rows(right_chip, core, *high), rows(left_chip, core, *high), rows(right_chip, core, *low),
-        rows(far_chip, core, *low), rows(far_chip, core, *high), rows(chip, 1 - core), rows(left_chip, 1 - core), rows(right_chip, 1 - core),
-        rows(far_chip, 1 - core),
-    ]
+    landing = [piece(item[0], core, item[1]) for item in received]
+    for idx, item in enumerate(received):
+        sends.append(remote(piece(item[0], core, item[1]), piece(item[0], core, item[1]), send, recv, 6 + idx, partner))
+        landing.append(piece(item[0], 1 - core, item[1]))
+    for which in range(2):
+        sends.append(remote(own(which), piece(chip, core, which), send, recv, 12 + which, partner))
+        landing.append(piece(chip, 1 - core, which))
 
     def arrived(index):
         remote(landing[index], landing[index], send, recv, index, partner).wait_recv()
 
+    def hand_over(*indices):
+        for index in indices:
+            arrived(index)
+            if index < 2:
+                sends[4 + index].start()
+            sends[6 + index].start()
+
+    def group_rows(*items):
+        return [first_row(item[0], idx, item[1]) for item in items for idx in range(CORES)]
+
     enter_ring((partner, left, right))
-    for index in (0, 1, 2, 3, 6):
+    for index in (0, 1, 2, 3, 12, 13):
         sends[index].start()
     full[pl.ds(pl.multiple_of((chip * CORES + core) * n_rows, n_rows), n_rows), :] = loc_ref[...]
+    arrived(12)
+    arrived(13)
+    consume(0, group_rows((chip, 0), (chip, 1)))
+    hand_over(0, 1)
     arrived(6)
-    consume(0, chip)
-    arrived(0)
-    sends[4].start()
-    arrived(1)
-    sends[5].start()
-    arrived(2)
-    sends[7].start()
-    arrived(3)
-    sends[8].start()
     arrived(7)
-    consume(1, left_chip)
+    consume(1, group_rows(received[0], received[1]))
+    hand_over(2, 3)
     arrived(8)
-    consume(2, right_chip)
-    arrived(4)
-    arrived(5)
-    sends[9].start()
     arrived(9)
-    consume(3, far_chip)
+    consume(2, group_rows(received[2], received[3]))
+    hand_over(4, 5)
+    arrived(10)
+    arrived(11)
+    consume(3, group_rows(received[4], received[5]))
     for copy in sends:
         copy.wait_send()
 
@@ -355,46 +334,54 @@
     full, scratch = refs[n_inputs + n_outs], refs[n_inputs + n_outs + 1:]
     held, staged = scratch[:n_inputs], scratch[n_inputs:-4]
     load_sem, store_sem, send, recv = scratch[-4:]
-    chip_rows = CORES * loc_ref.shape[0]
+    half = loc_ref.shape[0] // 2
     loads = [pltpu.make_async_copy(src.at[layer] if idx < n_weights else src, dst, load_sem.at[idx]) for idx, (src, dst) in enumerate(zip(inputs, held))]
     for load in loads:
         load.start()
     stores = []
 
-    def consume(step, chip_idx):
-        rows = pl.ds(pl.multiple_of(chip_idx * chip_rows, chip_rows), chip_rows)
-        if not step:
+    def consume(group, first_rows):
+        pieces = [pl.ds(first, half) for first in first_rows]
+
+        def rows_of(ref, cols=slice(None)):
+            return jnp.concatenate([ref[rows, cols] for rows in pieces], axis=0)
+
+        def put(ref, cols, value):
+            for idx, rows in enumerate(pieces):
+                ref[rows, cols] = value[idx * half:(idx + 1) * half]
+
+        if not group:
             loads[0].wait()
-        first = staged[0]
-        first[rows, :] = dot(full[rows, :], held[0][...], MATMUL if forward else CONTRACT_LAST).astype(BF16)
-        if not step:
+        put(staged[0], slice(None), dot(rows_of(full), held[0][...], MATMUL if forward else CONTRACT_LAST).astype(BF16))
+        if not group:
             for load in loads[1:]:
                 load.wait()
 
         def one_tile(idx, carry):
             cols = pl.ds(pl.multiple_of(idx * tile, tile), tile)
             if forward:
-                gate = dot(full[rows, :], held[1][:, cols], MATMUL).astype(BF16)
-                up = dot(full[rows, :], held[2][:, cols], MATMUL).astype(BF16)
-                staged[1][rows, cols] = gate
-                staged[2][rows, cols] = up
+                gate = dot(rows_of(full), held[1][:, cols], MATMUL).astype(BF16)
+                up = dot(rows_of(full), held[2][:, cols], MATMUL).astype(BF16)
+                put(staged[1], cols, gate)
+                put(staged[2], cols, up)
                 if n_outs > 3:
-                    staged[3][rows, cols] = gated(gate.astype(F32), up.astype(F32)).astype(BF16)
+                    put(staged[3], cols, gated(gate.astype(F32), up.astype(F32)).astype(BF16))
             else:
-                d_hidden = dot(full[rows, :], held[1][cols, :], CONTRACT_LAST).astype(BF16).astype(F32)
-                hidden, pull = jax.vjp(gated, held[2][rows, cols].astype(F32), held[3][rows, cols].astype(F32))
+                d_hidden = dot(rows_of(full), held[1][cols, :], CONTRACT_LAST).astype(BF16).astype(F32)
+                hidden, pull = jax.vjp(gated, rows_of(held[2], cols).astype(F32), rows_of(held[3], cols).astype(F32))
                 d_gate, d_up = pull(d_hidden)
-                staged[1][rows, cols] = hidden.astype(BF16)
-                staged[2][rows, cols] = d_gate.astype(BF16)
-                staged[3][rows, cols] = d_up.astype(BF16)
+                put(staged[1], cols, hidden.astype(BF16))
+                put(staged[2], cols, d_gate.astype(BF16))
+                put(staged[3], cols, d_up.astype(BF16))
             return carry
 
         lax.fori_loop(0, staged[1].shape[1] // tile, one_tile, 0)
         for idx, out in enumerate(outs):
             source = full if idx == len(staged) else staged[idx]
-            copy = pltpu.make_async_copy(source.at[rows], out.at[rows], store_sem.at[step, idx])
-            copy.start()
-            stores.append(copy)
+            for place, rows in enumerate(pieces):
+                copy = pltpu.make_async_copy(source.at[rows], out.at[rows], store_sem.at[group, place, idx])
+                copy.start()
+                stores.append(copy)
 
     ring_gather(chips, loc_ref, full, send, recv, consume)
     for copy in stores:
@@ -422,7 +409,7 @@
         + [pltpu.VMEM(weight.shape[1:], BF16) for weight in weights]
         + [pltpu.VMEM(item.shape, BF16) for item in saved]
         + staged
-        + [pltpu.SemaphoreType.DMA((len(inputs),)), pltpu.SemaphoreType.DMA((4, len(outs))), pltpu.SemaphoreType.DMA((10,)), pltpu.SemaphoreType.DMA((10,))],
+        + [pltpu.SemaphoreType.DMA((len(inputs),)), pltpu.SemaphoreType.DMA((4, 2 * CORES, len(outs))), pltpu.SemaphoreType.DMA((14,)), pltpu.SemaphoreType.DMA((14,))],
         compiler_params=pltpu.CompilerParams(vmem_limit_bytes=VMEM_LIMIT, collective_id=collective_id, has_side_effects=True),
         cost_estimate=cost(2 * seq_len * depth * n_cols, 2 * (seq_len * depth + depth * n_cols + seq_len * n_cols)),
         name=name,
@@ -432,10 +419,58 @@
 SCATTER_ORDER = ((0, 0), (0, 1), (1, 0), (2, 1), (1, 1), (2, 0), (3, 0), (3, 1))
 
 
-def dots_scatter_kernel(chips, layer, dims, n_terms, tile, *refs):
-    lhs_refs, rhs_refs, out_ref = refs[:n_terms], refs[n_terms:2 * n_terms], refs[2 * n_terms]
-    held, scratch = refs[2 * n_terms + 1:3 * n_terms + 1], refs[3 * n_terms + 1:]
-    part, from_core, acc, from_far, from_side, load_sem, core_send, core_recv, send, recv = scratch
+def weight_grads(u_ref, rhs_refs, grad_refs, u_held, grads_held, u_sem, grad_sem):
+    tile = u_held.shape[2]
+    n_tiles = u_ref.shape[1] // tile
+    starts = [sum(rhs.shape[1] for rhs in rhs_refs[:idx]) for idx in range(len(rhs_refs))]
+
+    def load(idx, slot):
+        return pltpu.make_async_copy(u_ref.at[:, pl.ds(pl.multiple_of(idx * tile, tile), tile)], u_held.at[slot], u_sem.at[slot])
+
+    def stores(idx, slot):
+        rows = pl.ds(pl.multiple_of(idx * tile, tile), tile)
+        return [
+            pltpu.make_async_copy(grads_held.at[slot, :, pl.ds(start, rhs.shape[1])], grad.at[rows, :], grad_sem.at[slot, place])
+            for place, (start, rhs, grad) in enumerate(zip(starts, rhs_refs, grad_refs))
+        ]
+
+    load(0, 0).start()
+
+    def one_tile(idx, carry):
+        slot = lax.rem(idx, 2)
+
+        @pl.when(idx + 1 < n_tiles)
+        def _():
+            load(idx + 1, 1 - slot).start()
+
+        @pl.when(idx >= 2)
+        def _():
+            for store in stores(idx - 2, slot):
+                store.wait()
+
+        load(idx, slot).wait()
+        lhs = u_held[slot]
+        for start, rhs in zip(starts, rhs_refs):
+            grads_held[slot, :, pl.ds(start, rhs.shape[1])] = dot(lhs, rhs[...], CONTRACT_FIRST).astype(BF16)
+        for store in stores(idx, slot):
+            store.start()
+        return carry
+
+    lax.fori_loop(0, n_tiles, one_tile, 0)
+    for idx in range(max(n_tiles - 2, 0), n_tiles):
+        for store in stores(idx, idx % 2):
+            store.wait()
+
+
+def dots_scatter_kernel(chips, layer, dims, n_terms, tile, with_grads, *refs):
+    lhs_refs, rhs_refs, refs = refs[:n_terms], refs[n_terms:2 * n_terms], refs[2 * n_terms:]
+    if with_grads:
+        u_ref, refs = refs[0], refs[1:]
+    out_ref, refs = refs[0], refs[1:]
+    if with_grads:
+        grad_refs, refs = refs[:n_terms], refs[n_terms:]
+    held, scratch = refs[:n_terms], refs[n_terms:]
+    part, acc, from_far, from_side, load_sem, core_send, core_recv, send, recv = scratch[:9]
     n_rows, n_cols = out_ref.shape
     half = n_cols // 2
     chip, core, (partner, left, right) = ring_place(chips)
@@ -453,7 +488,9 @@
         for load in group:
             load.start()
     enter_ring((partner, left, right))
-    to_core = [remote(part.at[item % 2, 1 - core], from_core.at[item], core_send, core_recv, item, partner) for item in range(len(SCATTER_ORDER))]
+    to_core = [
+        remote(part.at[item % 2, 1 - core], acc.at[step, which], core_send, core_recv, item, partner) for item, (step, which) in enumerate(SCATTER_ORDER)
+    ]
     hops = {
         (0, 0): remote(acc.at[0, 0], from_far.at[0], send, recv, 0, right),
         (0, 1): remote(acc.at[0, 1], from_far.at[1], send, recv, 1, left),
@@ -490,7 +527,7 @@
     def add_core(item):
         step, which = SCATTER_ORDER[item]
         to_core[item].wait_recv()
-        acc[step, which] = part[item % 2, core] + from_core[item]
+        acc[step, which] = acc[step, which] + part[item % 2, core]
         if item < 4:
             hops[step, which].start()
 
@@ -504,6 +541,8 @@
         hops[0, which].wait_recv()
         acc[step, which] = acc[step, which] + from_far[which]
         hops[step, which].start()
+    if with_grads:
+        weight_grads(u_ref, lhs_refs, grad_refs, *scratch[9:])
     for key in ((1, 0), (2, 1), (1, 1), (2, 0)):
         hops[key].wait_recv()
     for which in range(2):
@@ -514,33 +553,47 @@
         copy.wait_send()
 
 
-def dots_scatter(terms, layer, dims, tp_size, collective_id, name, tile=512):
+def dots_scatter(terms, layer, dims, tp_size, collective_id, name, u_full=None, tile=512, grad_tile=512):
     seq_len = terms[0][0].shape[0]
     n_cols = terms[0][1].shape[2] if dims is MATMUL else terms[0][1].shape[1]
     n_rows, half = seq_len // tp_size, n_cols // 2
     depth = sum(lhs.shape[1] for lhs, _ in terms)
-    return pl.pallas_call(
-        functools.partial(dots_scatter_kernel, tp_size // CORES, layer, dims, len(terms), tile),
-        out_shape=jax.ShapeDtypeStruct((n_rows, n_cols), F32),
-        in_specs=[pl.BlockSpec(memory_space=pltpu.VMEM)] * len(terms) + [pl.BlockSpec(memory_space=pl.ANY)] * len(terms),
-        out_specs=pl.BlockSpec(memory_space=pltpu.VMEM),
+    with_grads = u_full is not None
+    n_terms = len(terms)
+    any_spec, vmem_spec = pl.BlockSpec(memory_space=pl.ANY), pl.BlockSpec(memory_space=pltpu.VMEM)
+    outs, extra_inputs, extra_scratch = [jax.ShapeDtypeStruct((n_rows, n_cols), F32)], (), []
+    if with_grads:
+        outs += [jax.ShapeDtypeStruct((n_cols, lhs.shape[1]), BF16) for lhs, _ in terms]
+        extra_inputs = (u_full,)
+        extra_scratch = [
+            pltpu.VMEM((2, seq_len, grad_tile), BF16),
+            pltpu.VMEM((2, grad_tile, depth), BF16),
+            pltpu.SemaphoreType.DMA((2,)),
+            pltpu.SemaphoreType.DMA((2, n_terms)),
+        ]
+    results = pl.pallas_call(
+        functools.partial(dots_scatter_kernel, tp_size // CORES, layer, dims, n_terms, tile, with_grads),
+        out_shape=outs,
+        in_specs=[vmem_spec] * n_terms + [any_spec] * (n_terms + len(extra_inputs)),
+        out_specs=[vmem_spec] + [any_spec] * (len(outs) - 1),
         scratch_shapes=[pltpu.VMEM(rhs.shape[1:], BF16) for _, rhs in terms]
         + [
             pltpu.VMEM((2, CORES, n_rows, half), F32),
-            pltpu.VMEM((len(SCATTER_ORDER), n_rows, half), F32),
             pltpu.VMEM((4, 2, n_rows, half), F32),
             pltpu.VMEM((2, n_rows, half), F32),
             pltpu.VMEM((2, 2, n_rows, half), F32),
-            pltpu.SemaphoreType.DMA((len(terms), 2)),
+            pltpu.SemaphoreType.DMA((n_terms, 2)),
             pltpu.SemaphoreType.DMA((len(SCATTER_ORDER),)),
             pltpu.SemaphoreType.DMA((len(SCATTER_ORDER),)),
             pltpu.SemaphoreType.DMA((6,)),
             pltpu.SemaphoreType.DMA((6,)),
-        ],
+        ]
+        + extra_scratch,
         compiler_params=pltpu.CompilerParams(vmem_limit_bytes=VMEM_LIMIT, collective_id=collective_id, has_side_effects=True),
-        cost_estimate=cost(2 * seq_len * depth * n_cols, 2 * depth * (seq_len + n_cols) + 4 * n_rows * n_cols),
+        cost_estimate=cost(2 * seq_len * depth * n_cols * (2 if with_grads else 1), 2 * depth * (seq_len + n_cols) + 4 * n_rows * n_cols),
         name=name,
-    )(*[lhs for lhs, _ in terms], *[rhs for _, rhs in terms])
+    )(*[lhs for lhs, _ in terms], *[rhs for _, rhs in terms], *extra_inputs)
+    return (results[0], tuple(results[1:])) if with_grads else results[0]
 
 
 def gather_rows(rows_loc):
@@ -549,10 +602,6 @@
 
 def after(value, *others):
     return lax.optimization_barrier((value,) + others)[0]
-
-
-def reduce_rows(chunks):
-    return jnp.concatenate([lax.psum_scatter(chunk, 'tp', scatter_dimension=0, tiled=True) for chunk in chunks], axis=1)
 
 
 def solution(mesh):
@@ -572,8 +621,6 @@
         n_layers, depth = w_qkv.shape[0], w_qkv.shape[1]
         group = w_out.shape[1] // HEAD_DIM
         seq_len = x_loc.shape[0] * tp_size
-        n_chunks = 2
-        chunk_cols = depth // n_chunks
         cos_tab, sin_tab = rope_tables(seq_len)
         saved_all = []
         x_cur = x_loc
@@ -589,23 +636,23 @@
                 block_sum = dots_scatter([(attn_out, w_out), (outs[3], w_down)], layer, MATMUL, tp_size, n_layers + layer, "scatter_out")
                 x_cur = (x_f32 + block_sum).astype(BF16)
 
-        in_grads, out_grads, gain_grads = (), (), []
+        out_grads, gain_grads, done_grads = (), [], []
         for layer in reversed(range(n_layers)):
             x_in, u_loc, rot, attn_out, lse, gate, up = saved_all[layer]
             dy_send, rot = lax.optimization_barrier((dy_loc, rot))
             d_attn, hidden, d_gate, d_up, dy_full = gather_dots(dy_send, (w_out, w_down, gate, up), layer, False, True, tp_size, 2 * n_layers + layer, "gather_back")
             u_full = gather_rows(after(u_loc, attn_out, d_attn))
             d_qkv = attn_bwd(rot, lse, d_attn, cos_tab, sin_tab, group)
-            d_qkv, u_full = lax.optimization_barrier((d_qkv, u_full))
-            parts = [
-                sum_of_dots([(d_qkv, w_qkv), (d_gate, w_gate), (d_up, w_up)], layer, CONTRACT_LAST, idx * chunk_cols, chunk_cols, 512, "block_in_back")
-                for idx in range(n_chunks)
-            ]
-            held = lax.optimization_barrier((parts[-1], d_qkv, d_gate, d_up, hidden, attn_out))
-            parts[-1] = held[0]
-            in_grads = grad_in(u_full, held[1:4], layer, n_layers, in_grads)
-            out_grads = grad_out(held[5], held[4], dy_full, layer, n_layers, out_grads)
-            d_normed, in_grads, out_grads = lax.optimization_barrier((reduce_rows(parts), in_grads, out_grads))
+            out_grads = grad_out(attn_out, hidden, dy_full, layer, n_layers, out_grads)
+            d_qkv, u_full, out_grads = lax.optimization_barrier((d_qkv, u_full, out_grads))
+            terms = [(d_qkv, w_qkv), (d_gate, w_gate), (d_up, w_up)]
+            if layer:
+                d_normed, done = dots_scatter(terms, layer, CONTRACT_LAST, tp_size, 3 * n_layers + layer, "scatter_back", u_full)
+                done_grads.insert(0, done)
+            else:
+                d_normed = dots_scatter(terms, layer, CONTRACT_LAST, tp_size, 3 * n_layers + layer, "scatter_back")
+                d_normed, u_full, d_qkv, d_gate, d_up = lax.optimization_barrier((d_normed, u_full, d_qkv, d_gate, d_up))
+                in_grads = grad_in(u_full, (d_qkv, d_gate, d_up), done_grads)
             d_normed = d_normed.astype(BF16)
             norm_pull = jax.vjp(rms_scale, x_in.astype(F32), norm_gain[layer])[1]
             d_x_norm, gain_grad = norm_pull(d_normed.astype(F32))

time: 774 us -> 733 us (0.947)
  waiting for transfers between devices: 121 us -> 8.09 us
  Pallas kernels: 607 us -> 678 us
    pallas_call x1 -> x3, Pallas kernels: 92.5 us -> 291 us  [dots_scatter(): pl.pallas_call(functools.partial(dots_scatter_kernel, tp_size // CORES, l...]
    pallas_call x6 -> x1, Pallas kernels: 149 us -> 36.8 us  [grad_in(): pl.pallas_call(functools.partial(grad_in_kernel, n_rhs), out_shape=[jax.S...]
    reduce_scatter x4 -> x0, waiting for transfers between devices: 69.9 us -> none  [reduce_rows(): lax.psum_scatter(chunk, 'tp', scatter_dimension=0, tiled=True)]
    all_gather x2, waiting for transfers between devices: 44.3 us -> 5.34 us  [gather_rows(): return lax.all_gather(rows_loc, 'tp', axis=0, tiled=True)]
    pallas_call x4, Pallas kernels: 233 us -> 217 us  [gather_dots(): pl.pallas_call(functools.partial(gather_dots_kernel, chips, layer, forwar...]
  transfers between devices with their start and end apart: 9 -> 5, of which waited for: 7 -> 3; matrix products, arithmetic and copies ran while one was open for 0% -> 1% of each run, Pallas kernels for 26% -> 18%
where the time goes in v3:
time: 733 us; the launch traced here: 730 us
  Pallas kernels  678 us (92%)
  other arithmetic  22.5 us (3%)
  between operations  14.4 us (2%)
  waiting for transfers between devices  8.09 us (1%)
    pallas_call x3, Pallas kernels, dots_scatter(): pl.pallas_call(functools.partial(dots_scatter_kernel, tp_size // CORES, l...  291 us
    pallas_call x4, Pallas kernels, gather_dots(): pl.pallas_call(functools.partial(gather_dots_kernel, chips, layer, forwar...  217 us
    pallas_call x2, Pallas kernels, attn_bwd(): pl.pallas_call(functools.partial(attn_bwd_kernel, group), out_shape=jax.S...  54.3 us
    pallas_call x2, Pallas kernels, grad_out(): pl.pallas_call(grad_out_kernel, out_shape=(jax.ShapeDtypeStruct((n_layers...  41 us
    pallas_call x2, Pallas kernels, attn_fwd(): pl.pallas_call(functools.partial(attn_fwd_kernel, group), out_shape=(jax....  38.2 us
    pallas_call x1, Pallas kernels, grad_in(): pl.pallas_call(functools.partial(grad_in_kernel, n_rhs), out_shape=[jax.S...  36.8 us
  transfers between devices with their start and end apart: 5, of which 3 were waited for; matrix products, arithmetic and copies ran while one was open for 1% of the time, Pallas kernels for 18%

profile of v3, /device:TPU:112, one launch (start us, length us, event | category | flops | bytes accessed | tf_op | source)
XLA Modules:
  0.0 729.7 jit_solution(15359183478274020399)
XLA Ops:
  10.8 2.7 fusion.4.loc_ref
  13.5 56.1 %gather_in.2 = (bf16[1536,640]{1,0:T(8,128)(2,1)}, bf16[1536,1024]{1,0:T(8,128)(2,1)}, bf16[1536,1024]{1,0:T(8,128)(2,1)}, bf16[1536,1024]{1,0:T(8,128)(2,1)}) custom-call(bf16[192,3072]{1,0:T(8,128)(2,1)} %fusion.4.loc_ref, bf16[2,3072,640]{2,1,0:T(8,128)(2,1)} %refs_3_.5, bf16[2,3072,1024]{2,1,0:T(8,128)(2,1)} %refs_4_.3, bf16[2,3072,1024]{2,1,0:T(8,128)(2,1)} %refs_5_.3), custom_call_target="tpu_custom_call" | custom-call | flops 25367150592 | bytes 34209792 | tf_op jit(solution)/shard_map/gather_in/pallas_call | solution.py:403
  69.6 19.4 %attn_fwd.2 = (bf16[1536,640]{1,0:T(8,128)(2,1)}, bf16[1536,384]{1,0:T(8,128)(2,1)}, f32[1536,384]{1,0:T(8,128)}) custom-call(bf16[1536,640]{1,0:T(8,128)(2,1)} %get-tuple-element.60.qkv_ref, f32[1536,128]{1,0:T(8,128)} %constant.16.clone.cos_ref, f32[1536,128]{1,0:T(8,128)} %constant.17.clone.sin_ref), custom_call_target="tpu_custom_call" | custom-call | flops 3623878656 | bytes 7864320 | tf_op jit(solution)/shard_map/attn_fwd/pallas_call | solution.py:103
  89.0 93.0 %scatter_out.1 = f32[192,3072]{1,0:T(8,128)} custom-call(bf16[1536,384]{1,0:T(8,128)(2,1)} %get-tuple-element.61.refs_0_.attn_ref, bf16[1536,1024]{1,0:T(8,128)(2,1)} %get-tuple-element.62.refs_1_, bf16[2,384,3072]{2,1,0:T(8,128)(2,1)} %refs_0_.7, bf16[2,1024,3072]{2,1,0:T(8,128)(2,1)} %refs_1_.7), custom_call_target="tpu_custom_call" | custom-call | flops 13287555072 | bytes 15335424 | tf_op jit(solution)/shard_map/scatter_out/pallas_call | solution.py:574
  182.0 2.5 fusion.12
  186.9 53.8 %gather_in.3 = (bf16[1536,640]{1,0:T(8,128)(2,1)}, bf16[1536,1024]{1,0:T(8,128)(2,1)}, bf16[1536,1024]{1,0:T(8,128)(2,1)}) custom-call(bf16[192,3072]{1,0:T(8,128)(2,1)} %fusion.5.loc_ref, bf16[2,3072,640]{2,1,0:T(8,128)(2,1)} %refs_3_.5, bf16[2,3072,1024]{2,1,0:T(8,128)(2,1)} %refs_4_.3, bf16[2,3072,1024]{2,1,0:T(8,128)(2,1)} %refs_5_.3), custom_call_target="tpu_custom_call" | custom-call | flops 25367150592 | bytes 34209792 | tf_op jit(solution)/shard_map/gather_in/pallas_call | solution.py:403
  240.7 18.8 %attn_fwd.3 = (bf16[1536,640]{1,0:T(8,128)(2,1)}, bf16[1536,384]{1,0:T(8,128)(2,1)}, f32[1536,384]{1,0:T(8,128)}) custom-call(bf16[1536,640]{1,0:T(8,128)(2,1)} %get-tuple-element.63.qkv_ref, f32[1536,128]{1,0:T(8,128)} %constant.16.clone.cos_ref, f32[1536,128]{1,0:T(8,128)} %constant.17.clone.sin_ref), custom_call_target="tpu_custom_call" | custom-call | flops 3623878656 | bytes 7864320 | tf_op jit(solution)/shard_map/attn_fwd/pallas_call | solution.py:103
  259.6 54.5 %gather_back.2 = (bf16[1536,384]{1,0:T(8,128)(2,1)}, bf16[1536,1024]{1,0:T(8,128)(2,1)}, bf16[1536,1024]{1,0:T(8,128)(2,1)}, bf16[1536,1024]{1,0:T(8,128)(2,1)}, bf16[1536,3072]{1,0:T(8,128)(2,1)}) custom-call(bf16[192,3072]{1,0:T(8,128)(2,1)} %loc_ref, bf16[2,384,3072]{2,1,0:T(8,128)(2,1)} %refs_0_.7, bf16[2,1024,3072]{2,1,0:T(8,128)(2,1)} %refs_1_.7, ...), custom_call_target="tpu_custom_call" | custom-call | flops 13287555072 | bytes 22413312 | tf_op jit(solution)/shard_map/gather_back/pallas_call | solution.py:403
  314.2 27.1 %attn_bwd.2.refs_0_ = bf16[1536,640]{1,0:T(8,128)(2,1)} custom-call(bf16[1536,640]{1,0:T(8,128)(2,1)} %get-tuple-element.65.rot_ref, f32[1536,384]{1,0:T(8,128)} %get-tuple-element.66.lse_ref, bf16[1536,384]{1,0:T(8,128)(2,1)} %get-tuple-element.70.dout_ref, f32[1536,128]{1,0:T(8,128)} %constant.16.clone.cos_ref, f32[1536,128]{1,0:T(8,128)} %constant.17.clone.sin_ref), custom_call_target="tpu_custom_call" | custom-call | flops 9059696640 | bytes 7864320 | tf_op jit(solution)/shard_map/attn_bwd/pallas_call | solution.py:169
  341.3 20.5 %grad_out.2 = (bf16[2,384,3072]{2,1,0:T(8,128)(2,1)}, bf16[2,1024,3072]{2,1,0:T(8,128)(2,1)}) custom-call(bf16[1536,384]{1,0:T(8,128)(2,1)} %get-tuple-element.71.attn_ref, bf16[1536,1024]{1,0:T(8,128)(2,1)} %get-tuple-element.73.hidden_ref, bf16[1536,3072]{1,0:T(8,128)(2,1)} %get-tuple-element.74.dy_ref), custom_call_target="tpu_custom_call" | custom-call | flops 13287555072 | bytes 22413312 | tf_op jit(solution)/shard_map/grad_out/pallas_call | solution.py:219
  361.8 2.3 all-gather.3.cloned.1.call-done.refs_6_
  364.2 98.8 %scatter_back.2 = (f32[192,3072]{1,0:T(8,128)}, bf16[3072,640]{1,0:T(8,128)(2,1)}, bf16[3072,1024]{1,0:T(8,128)(2,1)}, bf16[3072,1024]{1,0:T(8,128)(2,1)}) custom-call(bf16[1536,640]{1,0:T(8,128)(2,1)} %attn_bwd.2.refs_0_, bf16[1536,1024]{1,0:T(8,128)(2,1)} %get-tuple-element.78.refs_1_, bf16[1536,1024]{1,0:T(8,128)(2,1)} %get-tuple-element.79.refs_2_, ...), custom_call_target="tpu_custom_call" | custom-call | flops 50734301184 | bytes 27131904 | tf_op jit(solution)/shard_map/scatter_back/pallas_call | solution.py:574
  463.1 3.3 fusion.6
  466.4 3.1 fusion.9.loc_ref
  469.5 52.8 %gather_back.3 = (bf16[1536,384]{1,0:T(8,128)(2,1)}, bf16[1536,1024]{1,0:T(8,128)(2,1)}, bf16[1536,1024]{1,0:T(8,128)(2,1)}, bf16[1536,1024]{1,0:T(8,128)(2,1)}, bf16[1536,3072]{1,0:T(8,128)(2,1)}) custom-call(bf16[192,3072]{1,0:T(8,128)(2,1)} %fusion.9.loc_ref, bf16[2,384,3072]{2,1,0:T(8,128)(2,1)} %refs_0_.7, bf16[2,1024,3072]{2,1,0:T(8,128)(2,1)} %refs_1_.7, ...), custom_call_target="tpu_custom_call" | custom-call | flops 13287555072 | bytes 22413312 | tf_op jit(solution)/shard_map/gather_back/pallas_call | solution.py:403
  522.3 27.1 %attn_bwd.3.refs_0_.refs_1_ = bf16[1536,640]{1,0:T(8,128)(2,1)} custom-call(bf16[1536,640]{1,0:T(8,128)(2,1)} %get-tuple-element.83.rot_ref, f32[1536,384]{1,0:T(8,128)} %get-tuple-element.84.lse_ref, bf16[1536,384]{1,0:T(8,128)(2,1)} %get-tuple-element.88.dout_ref, f32[1536,128]{1,0:T(8,128)} %constant.16.clone.cos_ref, f32[1536,128]{1,0:T(8,128)} %constant.17.clone.sin_ref), custom_call_target="tpu_custom_call" | custom-call | flops 9059696640 | bytes 7864320 | tf_op jit(solution)/shard_map/attn_bwd/pallas_call | solution.py:169
  549.4 20.5 %grad_out.3 = (bf16[2,384,3072]{2,1,0:T(8,128)(2,1)}, bf16[2,1024,3072]{2,1,0:T(8,128)(2,1)}) custom-call(bf16[1536,384]{1,0:T(8,128)(2,1)} %get-tuple-element.61.refs_0_.attn_ref, bf16[1536,1024]{1,0:T(8,128)(2,1)} %get-tuple-element.90.hidden_ref, bf16[1536,3072]{1,0:T(8,128)(2,1)} %get-tuple-element.91.dy_ref, ...), custom_call_target="tpu_custom_call", output_to_operand_aliasing={{0}: (3, {}), {1}: (4, {})} | custom-call | flops 13287555072 | bytes 22413312 | tf_op jit(solution)/shard_map/grad_out/pallas_call | solution.py:219
  569.9 3.0 all-gather.5.cloned.1.call-done.refs_0_
  572.9 98.9 %scatter_back.3 = f32[192,3072]{1,0:T(8,128)} custom-call(bf16[1536,640]{1,0:T(8,128)(2,1)} %attn_bwd.3.refs_0_.refs_1_, bf16[1536,1024]{1,0:T(8,128)(2,1)} %get-tuple-element.103.refs_1_.refs_2_, bf16[1536,1024]{1,0:T(8,128)(2,1)} %get-tuple-element.104.refs_2_.refs_3_, bf16[2,3072,640]{2,1,0:T(8,128)(2,1)} %refs_3_.5, bf16[2,3072,1024]{2,1,0:T(8,128)(2,1)} %refs_4_.3, ...), custom_call_target="tpu_custom_call" | custom-call | flops 25367150592 | bytes 27131904 | tf_op jit(solution)/shard_map/scatter_back/pallas_call | solution.py:574
  671.8 3.1 fusion.7
  675.1 36.8 %grad_in.1 = (bf16[2,3072,640]{2,1,0:T(8,128)(2,1)}, bf16[2,3072,1024]{2,1,0:T(8,128)(2,1)}, bf16[2,3072,1024]{2,1,0:T(8,128)(2,1)}) custom-call(bf16[1536,3072]{1,0:T(8,128)(2,1)} %all-gather.5.cloned.1.call-done.refs_0_, bf16[1536,640]{1,0:T(8,128)(2,1)} %attn_bwd.3.refs_0_.refs_1_, bf16[1536,1024]{1,0:T(8,128)(2,1)} %get-tuple-element.103.refs_1_.refs_2_, ...), custom_call_target="tpu_custom_call" | custom-call | flops 25367150592 | bytes 67239936 | tf_op jit(solution)/shard_map/grad_in/pallas_call | solution.py:192
  713.2 2.6 collective-permute-done.1
  715.9 2.0 collective-permute-start.2
  717.9 4.2 fusion.11
  (37 shorter events, 8.3 us)
Async XLA Ops:
  7.2 357.0 %all-gather.3.cloned.1.call-start = ((), (), s32[]{:S(2)}) async-start(), calls=%async_computation | async-start | bytes 10616832 | tf_op jit(solution)/shard_map/all_gather | solution.py:600
  8.1 2.2 copy-start.3
  9.7 0.6 copy-start.7
  10.3 0.5 copy-start.5
  184.4 1.1 copy-start
  314.1 258.8 %all-gather.5.cloned.1.call-start = ((), (), s32[]{:S(2)}) async-start(), calls=%async_computation.1 | async-start | bytes 10616832 | tf_op jit(solution)/shard_map/all_gather | solution.py:600
  463.0 3.3 copy-start.1
  463.0 3.3 copy-start.2
  572.9 98.9 %copy-start.4 = (f32[1,3072]{1,0:T(1,128)S(1)}, f32[1,3072]{1,0:T(1,128)}, u32[]{:S(2)}) copy-start(f32[1,3072]{1,0:T(1,128)} %copy-done.3) | copy-start | bytes 36868
  572.9 98.9 %copy-start.6 = (f32[192]{0:T(256)S(1)}, f32[192]{0:T(256)}, u32[]{:S(2)}) copy-start(f32[192]{0:T(256)} %copy-done.5) | copy-start | bytes 2308
  675.0 37.0 %collective-permute-start = (f32[2,3072]{1,0:T(2,128)S(1)}, f32[2,3072]{1,0:T(2,128)S(1)}, u32[]{:S(2)}, u32[]{:S(2)}) collective-permute-start(f32[2,3072]{1,0:T(2,128)S(1)} %pad_maximum_fusion), channel_id=1, source_target_pairs={{0,1},{1,0},{2,3},{3,2},{4,5},{5,4},{6,7},{7,6},{8,9},{9,8},{10,11... | collective-permute-start | bytes 73736 | tf_op jit(solution)/shard_map/ppermute | solution.py:616
  675.1 38.2 %copy-start.8 = (f32[192]{0:T(256)S(1)}, f32[192]{0:T(256)}, u32[]{:S(2)}) copy-start(f32[192]{0:T(256)} %copy-done.7) | copy-start | bytes 2308
  712.0 3.9 collective-permute-start.1
  715.9 6.2 collective-permute-start.2
Sparse Core Ops, SparseCore 0:
  314.2 49.8 all-gather.2
  522.4 50.4 all-gather.4

commit v4 on v3

--- a/solution.py
+++ b/solution.py
@@ -259,37 +259,34 @@
     return pltpu.make_async_remote_copy(src_ref=src, dst_ref=dst, send_sem=send.at[index], recv_sem=recv.at[index], device_id={'tp': peer}, device_id_type=MESH)
 
 
-def ring_gather(chips, loc_ref, full, send, recv, consume):
+def ring_gather(chips, loc_ref, full, send, recv, consume, meanwhile=None):
     n_rows = loc_ref.shape[0]
-    half = n_rows // 2
+    half, quarter = n_rows // 2, n_rows // 4
     chip, core, (partner, left, right) = ring_place(chips)
     left_chip, right_chip, far_chip = lax.rem(chip + chips - 1, chips), lax.rem(chip + 1, chips), lax.rem(chip + 2, chips)
 
-    def first_row(chip_idx, core_idx, which):
-        return pl.multiple_of((chip_idx * CORES + core_idx) * n_rows + which * half, half)
-
-    def piece(chip_idx, core_idx, which):
-        return full.at[pl.ds(first_row(chip_idx, core_idx, which), half)]
-
-    def own(which):
-        return loc_ref.at[pl.ds(which * half, half)]
-
-    received = [(left_chip, 0), (right_chip, 1), (left_chip, 1), (right_chip, 0), (far_chip, 0), (far_chip, 1)]
+    def first_row(core_idx, item):
+        return pl.multiple_of((item[0] * CORES + core_idx) * n_rows + item[1], item[2])
+
+    def piece(core_idx, item):
+        return full.at[pl.ds(first_row(core_idx, item), item[2])]
+
+    low, high = (chip, 0, half), (chip, half, half)
+    received = [
+        (left_chip, 0, half), (right_chip, half, half), (left_chip, half, half), (right_chip, 0, half),
+        (far_chip, 0, quarter), (far_chip, half, quarter), (far_chip, quarter, quarter), (far_chip, half + quarter, quarter),
+    ]
+    passed_on = [(left_chip, 0, quarter), (right_chip, half, quarter), (left_chip, quarter, quarter), (right_chip, half + quarter, quarter)]
     sends = [
-        remote(own(0), piece(chip, core, 0), send, recv, 0, right),
-        remote(own(1), piece(chip, core, 1), send, recv, 1, left),
-        remote(own(1), piece(chip, core, 1), send, recv, 2, right),
-        remote(own(0), piece(chip, core, 0), send, recv, 3, left),
-        remote(piece(left_chip, core, 0), piece(left_chip, core, 0), send, recv, 4, right),
-        remote(piece(right_chip, core, 1), piece(right_chip, core, 1), send, recv, 5, left),
+        remote(loc_ref.at[pl.ds(item[1], half)], piece(core, item), send, recv, idx, peer)
+        for idx, (item, peer) in enumerate([(low, right), (high, left), (high, right), (low, left)])
     ]
-    landing = [piece(item[0], core, item[1]) for item in received]
-    for idx, item in enumerate(received):
-        sends.append(remote(piece(item[0], core, item[1]), piece(item[0], core, item[1]), send, recv, 6 + idx, partner))
-        landing.append(piece(item[0], 1 - core, item[1]))
-    for which in range(2):
-        sends.append(remote(own(which), piece(chip, core, which), send, recv, 12 + which, partner))
-        landing.append(piece(chip, 1 - core, which))
+    sends += [remote(piece(core, item), piece(core, item), send, recv, 4 + idx, (right, left)[idx % 2]) for idx, item in enumerate(passed_on)]
+    sends += [remote(piece(core, item), piece(core, item), send, recv, 8 + idx, partner) for idx, item in enumerate(received)]
+    own = full.at[pl.ds(pl.multiple_of((chip * CORES + core) * n_rows, n_rows), n_rows)]
+    other = full.at[pl.ds(pl.multiple_of((chip * CORES + 1 - core) * n_rows, n_rows), n_rows)]
+    sends.append(remote(loc_ref, own, send, recv, 16, partner))
+    landing = [piece(core, item) for item in received] + [piece(1 - core, item) for item in received] + [other]
 
     def arrived(index):
         remote(landing[index], landing[index], send, recv, index, partner).wait_recv()
@@ -299,62 +296,72 @@
             arrived(index)
             if index < 2:
                 sends[4 + index].start()
-            sends[6 + index].start()
-
-    def group_rows(*items):
-        return [first_row(item[0], idx, item[1]) for item in items for idx in range(CORES)]
+                sends[6 + index].start()
+            sends[8 + index].start()
+
+    def use(group, items):
+        consume(group, [first_row(idx, item) for item in items for idx in range(CORES)], items[0][2])
 
     enter_ring((partner, left, right))
-    for index in (0, 1, 2, 3, 12, 13):
+    for index in (0, 1, 2, 3, 16):
         sends[index].start()
-    full[pl.ds(pl.multiple_of((chip * CORES + core) * n_rows, n_rows), n_rows), :] = loc_ref[...]
-    arrived(12)
-    arrived(13)
-    consume(0, group_rows((chip, 0), (chip, 1)))
-    hand_over(0, 1)
-    arrived(6)
-    arrived(7)
-    consume(1, group_rows(received[0], received[1]))
-    hand_over(2, 3)
-    arrived(8)
-    arrived(9)
-    consume(2, group_rows(received[2], received[3]))
-    hand_over(4, 5)
-    arrived(10)
-    arrived(11)
-    consume(3, group_rows(received[4], received[5]))
+    own[...] = loc_ref[...]
+    if meanwhile is not None:
+        meanwhile()
+        hand_over(0, 1)
+    arrived(16)
+    use(0, (low, high))
+    if meanwhile is None:
+        hand_over(0, 1)
+    for group in range(1, 5):
+        pair = (2 * group - 2, 2 * group - 1)
+        if group > 1:
+            hand_over(*pair)
+        for index in pair:
+            arrived(8 + index)
+        use(group, received[2 * group - 2:2 * group])
     for copy in sends:
         copy.wait_send()
 
 
-def gather_dots_kernel(chips, layer, forward, n_outs, tile, loc_ref, *refs):
+def gather_dots_kernel(chips, layer, forward, with_hidden, attn_group, tile, n_inputs, n_outs, loc_ref, *refs):
     n_weights = 3 if forward else 2
-    n_inputs = 3 if forward else 4
     inputs, outs = refs[:n_inputs], refs[n_inputs:n_inputs + n_outs]
     full, scratch = refs[n_inputs + n_outs], refs[n_inputs + n_outs + 1:]
-    held, staged = scratch[:n_inputs], scratch[n_inputs:-4]
-    load_sem, store_sem, send, recv = scratch[-4:]
-    half = loc_ref.shape[0] // 2
+    held, staged = scratch[:n_inputs], scratch[n_inputs:-5]
+    load_sem, store_sem, attn_sem, send, recv = scratch[-5:]
     loads = [pltpu.make_async_copy(src.at[layer] if idx < n_weights else src, dst, load_sem.at[idx]) for idx, (src, dst) in enumerate(zip(inputs, held))]
-    for load in loads:
+    n_dots = n_weights + (1 if with_hidden else 0) if forward else 4
+    attn_loads = loads[4:] if attn_group else []
+    dot_loads = loads[:len(loads) - len(attn_loads)]
+    for load in attn_loads + dot_loads:
         load.start()
     stores = []
 
-    def consume(group, first_rows):
-        pieces = [pl.ds(first, half) for first in first_rows]
+    def attention():
+        for load in attn_loads:
+            load.wait()
+        attn_fwd_kernel(attn_group, *held[4:], *staged[n_dots:])
+        for idx, (src, dst) in enumerate(zip(staged[n_dots:], outs[-3:])):
+            copy = pltpu.make_async_copy(src, dst, attn_sem.at[idx])
+            copy.start()
+            stores.append(copy)
+
+    def consume(group, first_rows, count):
+        pieces = [pl.ds(first, count) for first in first_rows]
 
         def rows_of(ref, cols=slice(None)):
             return jnp.concatenate([ref[rows, cols] for rows in pieces], axis=0)
 
         def put(ref, cols, value):
             for idx, rows in enumerate(pieces):
-                ref[rows, cols] = value[idx * half:(idx + 1) * half]
+                ref[rows, cols] = value[idx * count:(idx + 1) * count]
 
         if not group:
-            loads[0].wait()
+            dot_loads[0].wait()
         put(staged[0], slice(None), dot(rows_of(full), held[0][...], MATMUL if forward else CONTRACT_LAST).astype(BF16))
         if not group:
-            for load in loads[1:]:
+            for load in dot_loads[1:]:
                 load.wait()
 
         def one_tile(idx, carry):
@@ -364,7 +371,7 @@
                 up = dot(rows_of(full), held[2][:, cols], MATMUL).astype(BF16)
                 put(staged[1], cols, gate)
                 put(staged[2], cols, up)
-                if n_outs > 3:
+                if with_hidden:
                     put(staged[3], cols, gated(gate.astype(F32), up.astype(F32)).astype(BF16))
             else:
                 d_hidden = dot(rows_of(full), held[1][cols, :], CONTRACT_LAST).astype(BF16).astype(F32)
@@ -376,47 +383,55 @@
             return carry
 
         lax.fori_loop(0, staged[1].shape[1] // tile, one_tile, 0)
-        for idx, out in enumerate(outs):
-            source = full if idx == len(staged) else staged[idx]
+        sources = list(staged[:n_dots]) + ([] if forward else [full])
+        for idx, source in enumerate(sources):
             for place, rows in enumerate(pieces):
-                copy = pltpu.make_async_copy(source.at[rows], out.at[rows], store_sem.at[group, place, idx])
+                copy = pltpu.make_async_copy(source.at[rows], outs[idx].at[rows], store_sem.at[group, place, idx])
                 copy.start()
                 stores.append(copy)
 
-    ring_gather(chips, loc_ref, full, send, recv, consume)
+    ring_gather(chips, loc_ref, full, send, recv, consume, attention if attn_group else None)
     for copy in stores:
         copy.wait()
 
 
-def gather_dots(loc, inputs, layer, forward, with_hidden, tp_size, collective_id, name, tile=256):
+def gather_dots(loc, inputs, layer, forward, with_hidden, tp_size, collective_id, name, attn_inputs=(), tile=256):
     n_rows, depth = loc.shape
     seq_len, chips = n_rows * tp_size, tp_size // CORES
     n_weights = 3 if forward else 2
-    weights, saved = inputs[:n_weights], inputs[n_weights:]
+    weights, saved = inputs[:n_weights], tuple(inputs[n_weights:]) + tuple(attn_inputs)
     if forward:
         widths = [weight.shape[2] for weight in weights] + ([weights[1].shape[2]] if with_hidden else [])
     else:
         widths = [weights[0].shape[1]] + [weights[1].shape[1]] * 3
-    staged = [pltpu.VMEM((seq_len, width), BF16) for width in widths]
-    outs = [jax.ShapeDtypeStruct((seq_len, width), BF16) for width in widths + ([] if forward else [depth])]
+    staged = [((seq_len, width), BF16) for width in widths]
+    attn_group = weights[0].shape[1] // HEAD_DIM if attn_inputs else 0
+    attn_outs = []
+    if attn_inputs:
+        attn_outs = [(attn_inputs[0].shape, BF16), ((seq_len, weights[0].shape[1]), BF16), ((seq_len, weights[0].shape[1]), F32)]
+    outs = staged + ([] if forward else [((seq_len, depth), BF16)]) + attn_outs
     n_cols = sum(weight.size // (weight.shape[0] * depth) for weight in weights)
+    all_inputs = tuple(inputs) + tuple(attn_inputs)
     return pl.pallas_call(
-        functools.partial(gather_dots_kernel, chips, layer, forward, len(outs), tile),
-        out_shape=outs,
-        in_specs=[pl.BlockSpec(memory_space=pltpu.VMEM)] + [pl.BlockSpec(memory_space=pl.ANY)] * len(inputs),
+        functools.partial(gather_dots_kernel, chips, layer, forward, with_hidden, attn_group, tile, len(all_inputs), len(outs)),
+        out_shape=[jax.ShapeDtypeStruct(*item) for item in outs],
+        in_specs=[pl.BlockSpec(memory_space=pltpu.VMEM)] + [pl.BlockSpec(memory_space=pl.ANY)] * len(all_inputs),
         out_specs=[pl.BlockSpec(memory_space=pl.ANY)] * len(outs),
         scratch_shapes=[pltpu.VMEM((seq_len, depth), BF16)]
         + [pltpu.VMEM(weight.shape[1:], BF16) for weight in weights]
-        + [pltpu.VMEM(item.shape, BF16) for item in saved]
-        + staged
-        + [pltpu.SemaphoreType.DMA((len(inputs),)), pltpu.SemaphoreType.DMA((4, 2 * CORES, len(outs))), pltpu.SemaphoreType.DMA((14,)), pltpu.SemaphoreType.DMA((14,))],
+        + [pltpu.VMEM(item.shape, item.dtype) for item in saved]
+        + [pltpu.VMEM(*item) for item in staged + attn_outs]
+        + [
+            pltpu.SemaphoreType.DMA((len(all_inputs),)),
+            pltpu.SemaphoreType.DMA((5, 2 * CORES, len(outs))),
+            pltpu.SemaphoreType.DMA((3,)),
+            pltpu.SemaphoreType.DMA((17,)),
+            pltpu.SemaphoreType.DMA((17,)),
+        ],
         compiler_params=pltpu.CompilerParams(vmem_limit_bytes=VMEM_LIMIT, collective_id=collective_id, has_side_effects=True),
         cost_estimate=cost(2 * seq_len * depth * n_cols, 2 * (seq_len * depth + depth * n_cols + seq_len * n_cols)),
         name=name,
-    )(loc, *inputs)
-
-
-SCATTER_ORDER = ((0, 0), (0, 1), (1, 0), (2, 1), (1, 1), (2, 0), (3, 0), (3, 1))
+    )(loc, *all_inputs)
 
 
 def weight_grads(u_ref, rhs_refs, grad_refs, u_held, grads_held, u_sem, grad_sem):
@@ -463,100 +478,133 @@
 
 
 def dots_scatter_kernel(chips, layer, dims, n_terms, tile, with_grads, *refs):
-    lhs_refs, rhs_refs, refs = refs[:n_terms], refs[n_terms:2 * n_terms], refs[2 * n_terms:]
+    lhs_hbm, rhs_refs, refs = refs[:n_terms], refs[n_terms:2 * n_terms], refs[2 * n_terms:]
     if with_grads:
         u_ref, refs = refs[0], refs[1:]
     out_ref, refs = refs[0], refs[1:]
     if with_grads:
         grad_refs, refs = refs[:n_terms], refs[n_terms:]
-    held, scratch = refs[:n_terms], refs[n_terms:]
-    part, acc, from_far, from_side, load_sem, core_send, core_recv, send, recv = scratch[:9]
+    lhs_refs, held, scratch = refs[:n_terms], refs[n_terms:2 * n_terms], refs[2 * n_terms:]
+    part, acc, from_far, from_side, lhs_sem, load_sem, core_send, core_recv, send, recv = scratch[:10]
     n_rows, n_cols = out_ref.shape
     half = n_cols // 2
+    n_tiles = half // tile
     chip, core, (partner, left, right) = ring_place(chips)
     dest_chips = [lax.rem(chip + offset, chips) for offset in (2, chips - 1, 1, 0)]
 
-    def half_of(ref, which):
-        cols = pl.ds(which * half, half)
-        return ref.at[:, cols] if dims is MATMUL else ref.at[cols, :]
-
-    loads = [
-        [pltpu.make_async_copy(half_of(src.at[layer], which), half_of(dst, which), load_sem.at[idx, which]) for idx, (src, dst) in enumerate(zip(rhs_refs, held))]
-        for which in range(2)
-    ]
-    for group in loads:
-        for load in group:
+    chip_rows = CORES * n_rows
+
+    def rows_of(step):
+        return pl.ds(pl.multiple_of(dest_chips[step] * chip_rows, chip_rows), chip_rows)
+
+    def cols_of(which, idx):
+        return pl.ds(pl.multiple_of(which * half + idx * tile, tile), tile)
+
+    def lhs_loads(step):
+        return [pltpu.make_async_copy(src.at[rows_of(step)], dst.at[rows_of(step)], lhs_sem.at[step, place]) for place, (src, dst) in enumerate(zip(lhs_hbm, lhs_refs))]
+
+    def rhs_loads(which, idx):
+        cols = cols_of(which, idx)
+        if dims is MATMUL:
+            pairs = [(src.at[layer, :, cols], dst.at[:, cols]) for src, dst in zip(rhs_refs, held)]
+        else:
+            pairs = [(src.at[layer, cols, :], dst.at[cols, :]) for src, dst in zip(rhs_refs, held)]
+        return [pltpu.make_async_copy(src, dst, load_sem.at[which * n_tiles + idx, place]) for place, (src, dst) in enumerate(pairs)]
+
+    for load in lhs_loads(0):
+        load.start()
+    for idx in range(n_tiles):
+        for which in range(2):
+            for load in rhs_loads(which, idx):
+                load.start()
+    for step in range(1, 4):
+        for load in lhs_loads(step):
             load.start()
     enter_ring((partner, left, right))
-    to_core = [
-        remote(part.at[item % 2, 1 - core], acc.at[step, which], core_send, core_recv, item, partner) for item, (step, which) in enumerate(SCATTER_ORDER)
-    ]
-    hops = {
-        (0, 0): remote(acc.at[0, 0], from_far.at[0], send, recv, 0, right),
-        (0, 1): remote(acc.at[0, 1], from_far.at[1], send, recv, 1, left),
-        (1, 0): remote(acc.at[1, 0], from_side.at[1, 0], send, recv, 2, left),
-        (2, 1): remote(acc.at[2, 1], from_side.at[0, 1], send, recv, 3, right),
-        (1, 1): remote(acc.at[1, 1], from_side.at[1, 1], send, recv, 4, left),
-        (2, 0): remote(acc.at[2, 0], from_side.at[0, 0], send, recv, 5, right),
-    }
-
-    def compute(item):
-        step, which = SCATTER_ORDER[item]
-        rows = pl.ds(pl.multiple_of(dest_chips[step] * (CORES * n_rows), CORES * n_rows), CORES * n_rows)
-        if item < 2:
-            for load in loads[which]:
+
+    def to_core(step, which, idx):
+        slot = which * n_tiles + idx
+        return remote(part.at[which, 1 - core], acc.at[step, slot], core_send, core_recv, step * 2 * n_tiles + slot, partner)
+
+    def hop(step, which, idx):
+        slot = which * n_tiles + idx
+        if not step:
+            return remote(acc.at[0, slot], from_far.at[slot], send, recv, slot, left if which else right)
+        side = 1 if step == 1 else 0
+        return remote(acc.at[step, slot], from_side.at[side, slot], send, recv, step * 2 * n_tiles + slot, left if side else right)
+
+    def compute(step, which, idx):
+        rows, rhs_cols = rows_of(step), cols_of(which, idx)
+        if not step:
+            for load in rhs_loads(which, idx):
                 load.wait()
-        if item >= 2:
-            to_core[item - 2].wait_send()
-
-        def one_tile(idx, carry):
-            first = pl.multiple_of(idx * tile, tile)
-            rhs_cols = pl.ds(which * half + first, tile)
-            total = None
-            for lhs_ref, rhs_ref in zip(lhs_refs, held):
-                rhs = rhs_ref[:, rhs_cols] if dims is MATMUL else rhs_ref[rhs_cols, :]
-                product = dot(lhs_ref[rows, :], rhs, dims)
-                total = product if total is None else total + product
-            for idx_core in range(CORES):
-                part[item % 2, idx_core, :, pl.ds(first, tile)] = total[idx_core * n_rows:(idx_core + 1) * n_rows]
+        total = None
+        for lhs_ref, rhs_ref in zip(lhs_refs, held):
+            rhs = rhs_ref[:, rhs_cols] if dims is MATMUL else rhs_ref[rhs_cols, :]
+            product = dot(lhs_ref[rows, :], rhs, dims)
+            total = product if total is None else total + product
+        for idx_core in range(CORES):
+            part[which, idx_core] = total[idx_core * n_rows:(idx_core + 1) * n_rows]
+        to_core(step, which, idx).start()
+
+    def add_core(step, which, idx, hop_now):
+        copy = to_core(step, which, idx)
+        copy.wait_recv()
+        slot = which * n_tiles + idx
+        acc[step, slot] = acc[step, slot] + part[which, core]
+        copy.wait_send()
+        if hop_now:
+            hop(step, which, idx).start()
+
+    for first, second, hop_now in (((0, 0), (0, 1), True), ((1, 0), (2, 1), True), ((2, 0), (1, 1), False), ((3, 0), (3, 1), False)):
+        for step in {first[0]: 0, second[0]: 0} if hop_now else ():
+            for load in lhs_loads(step):
+                load.wait()
+        if first[0] == 3:
+            for load in lhs_loads(3):
+                load.wait()
+
+        def one_pair(idx, carry):
+            compute(*first, idx)
+
+            @pl.when(idx > 0)
+            def _():
+                add_core(*second, idx - 1, hop_now)
+
+            compute(*second, idx)
+            add_core(*first, idx, hop_now)
             return carry
 
-        lax.fori_loop(0, half // tile, one_tile, 0)
-        to_core[item].start()
-
-    def add_core(item):
-        step, which = SCATTER_ORDER[item]
-        to_core[item].wait_recv()
-        acc[step, which] = acc[step, which] + part[item % 2, core]
-        if item < 4:
-            hops[step, which].start()
-
-    n_items = len(SCATTER_ORDER)
-    for item in range(n_items):
-        compute(item)
-        if item:
-            add_core(item - 1)
-    add_core(n_items - 1)
-    for which, step in ((0, 2), (1, 1)):
-        hops[0, which].wait_recv()
-        acc[step, which] = acc[step, which] + from_far[which]
-        hops[step, which].start()
+        lax.fori_loop(0, n_tiles, one_pair, 0)
+        add_core(*second, n_tiles - 1, hop_now)
+
+    def pass_on(idx, carry):
+        for step, which in ((2, 0), (1, 1)):
+            slot = which * n_tiles + idx
+            hop(0, which, idx).wait_recv()
+            acc[step, slot] = acc[step, slot] + from_far[slot]
+            hop(step, which, idx).start()
+        return carry
+
+    lax.fori_loop(0, n_tiles, pass_on, 0)
     if with_grads:
-        weight_grads(u_ref, lhs_refs, grad_refs, *scratch[9:])
-    for key in ((1, 0), (2, 1), (1, 1), (2, 0)):
-        hops[key].wait_recv()
+        weight_grads(u_ref, lhs_refs, grad_refs, *scratch[10:])
     for which in range(2):
-        out_ref[:, pl.ds(which * half, half)] = acc[3, which] + from_side[0, which] + from_side[1, which]
-    for copy in to_core[-2:]:
-        copy.wait_send()
-    for copy in hops.values():
-        copy.wait_send()
+        for idx in range(n_tiles):
+            slot = which * n_tiles + idx
+            hop(1, which, idx).wait_recv()
+            hop(2, which, idx).wait_recv()
+            out_ref[:, pl.ds(slot * tile, tile)] = acc[3, slot] + from_side[0, slot] + from_side[1, slot]
+    for step in range(3):
+        for which in range(2):
+            for idx in range(n_tiles):
+                hop(step, which, idx).wait_send()
 
 
 def dots_scatter(terms, layer, dims, tp_size, collective_id, name, u_full=None, tile=512, grad_tile=512):
     seq_len = terms[0][0].shape[0]
     n_cols = terms[0][1].shape[2] if dims is MATMUL else terms[0][1].shape[1]
-    n_rows, half = seq_len // tp_size, n_cols // 2
+    n_rows = seq_len // tp_size
     depth = sum(lhs.shape[1] for lhs, _ in terms)
     with_grads = u_full is not None
     n_terms = len(terms)
@@ -574,19 +622,21 @@
     results = pl.pallas_call(
         functools.partial(dots_scatter_kernel, tp_size // CORES, layer, dims, n_terms, tile, with_grads),
         out_shape=outs,
-        in_specs=[vmem_spec] * n_terms + [any_spec] * (n_terms + len(extra_inputs)),
+        in_specs=[any_spec] * (2 * n_terms + len(extra_inputs)),
         out_specs=[vmem_spec] + [any_spec] * (len(outs) - 1),
-        scratch_shapes=[pltpu.VMEM(rhs.shape[1:], BF16) for _, rhs in terms]
+        scratch_shapes=[pltpu.VMEM(lhs.shape, BF16) for lhs, _ in terms]
+        + [pltpu.VMEM(rhs.shape[1:], BF16) for _, rhs in terms]
         + [
-            pltpu.VMEM((2, CORES, n_rows, half), F32),
-            pltpu.VMEM((4, 2, n_rows, half), F32),
-            pltpu.VMEM((2, n_rows, half), F32),
-            pltpu.VMEM((2, 2, n_rows, half), F32),
-            pltpu.SemaphoreType.DMA((n_terms, 2)),
-            pltpu.SemaphoreType.DMA((len(SCATTER_ORDER),)),
-            pltpu.SemaphoreType.DMA((len(SCATTER_ORDER),)),
-            pltpu.SemaphoreType.DMA((6,)),
-            pltpu.SemaphoreType.DMA((6,)),
+            pltpu.VMEM((2, CORES, n_rows, tile), F32),
+            pltpu.VMEM((4, n_cols // tile, n_rows, tile), F32),
+            pltpu.VMEM((n_cols // tile, n_rows, tile), F32),
+            pltpu.VMEM((2, n_cols // tile, n_rows, tile), F32),
+            pltpu.SemaphoreType.DMA((4, n_terms)),
+            pltpu.SemaphoreType.DMA((n_cols // tile, n_terms)),
+            pltpu.SemaphoreType.DMA((4 * n_cols // tile,)),
+            pltpu.SemaphoreType.DMA((4 * n_cols // tile,)),
+            pltpu.SemaphoreType.DMA((3 * n_cols // tile,)),
+            pltpu.SemaphoreType.DMA((3 * n_cols // tile,)),
         ]
         + extra_scratch,
         compiler_params=pltpu.CompilerParams(vmem_limit_bytes=VMEM_LIMIT, collective_id=collective_id, has_side_effects=True),
@@ -630,7 +680,7 @@
             u_loc = rms_scale(x_f32, norm_gain[layer]).astype(BF16)
             outs = gather_dots(u_loc, (w_qkv, w_gate, w_up), layer, True, not last, tp_size, layer, "gather_in")
             qkv, gate, up = outs[:3]
-            rot, attn_out, lse = attn_fwd(qkv, cos_tab, sin_tab, group)
+            rot, attn_out, lse = (qkv, None, None) if last else attn_fwd(qkv, cos_tab, sin_tab, group)
             saved_all.append((x_cur, u_loc, rot, attn_out, lse, gate, up))
             if not last:
                 block_sum = dots_scatter([(attn_out, w_out), (outs[3], w_down)], layer, MATMUL, tp_size, n_layers + layer, "scatter_out")
@@ -639,8 +689,12 @@
         out_grads, gain_grads, done_grads = (), [], []
         for layer in reversed(range(n_layers)):
             x_in, u_loc, rot, attn_out, lse, gate, up = saved_all[layer]
-            dy_send, rot = lax.optimization_barrier((dy_loc, rot))
-            d_attn, hidden, d_gate, d_up, dy_full = gather_dots(dy_send, (w_out, w_down, gate, up), layer, False, True, tp_size, 2 * n_layers + layer, "gather_back")
+            last = layer == n_layers - 1
+            attn_inputs = (rot, cos_tab, sin_tab) if last else ()
+            outs = gather_dots(dy_loc, (w_out, w_down, gate, up), layer, False, True, tp_size, 2 * n_layers + layer, "gather_back", attn_inputs)
+            d_attn, hidden, d_gate, d_up, dy_full = outs[:5]
+            if last:
+                rot, attn_out, lse = outs[5:]
             u_full = gather_rows(after(u_loc, attn_out, d_attn))
             d_qkv = attn_bwd(rot, lse, d_attn, cos_tab, sin_tab, group)
             out_grads = grad_out(attn_out, hidden, dy_full, layer, n_layers, out_grads)

time: 733 us -> 686 us (0.936)
  Pallas kernels: 678 us -> 631 us
    pallas_call x3, Pallas kernels: 291 us -> 264 us  [dots_scatter(): pl.pallas_call(functools.partial(dots_scatter_kernel, tp_size // CORES, l...]
    pallas_call x2 -> x1, Pallas kernels: 38.2 us -> 19 us  [attn_fwd(): pl.pallas_call(functools.partial(attn_fwd_kernel, group), out_shape=(jax....]
  transfers between devices with their start and end apart: 5 -> 5, of which waited for: 3 -> 3; matrix products, arithmetic and copies ran while one was open for 1% -> 1% of each run, Pallas kernels for 18% -> 19%
where the time goes in v4:
time: 686 us; the launch traced here: 682 us
  Pallas kernels  631 us (92%)
  other arithmetic  22.5 us (3%)
  between operations  14.4 us (2%)
  waiting for transfers between devices  8.34 us (1%)
    pallas_call x3, Pallas kernels, dots_scatter(): pl.pallas_call(functools.partial(dots_scatter_kernel, tp_size // CORES, l...  264 us
    pallas_call x4, Pallas kernels, gather_dots(): pl.pallas_call(functools.partial(gather_dots_kernel, chips, layer, forwar...  215 us
    pallas_call x2, Pallas kernels, attn_bwd(): pl.pallas_call(functools.partial(attn_bwd_kernel, group), out_shape=jax.S...  54.3 us
    pallas_call x2, Pallas kernels, grad_out(): pl.pallas_call(grad_out_kernel, out_shape=(jax.ShapeDtypeStruct((n_layers...  41 us
    pallas_call x1, Pallas kernels, grad_in(): pl.pallas_call(functools.partial(grad_in_kernel, n_rhs), out_shape=[jax.S...  36.8 us
    pallas_call x1, Pallas kernels, attn_fwd(): pl.pallas_call(functools.partial(attn_fwd_kernel, group), out_shape=(jax....  19 us
  transfers between devices with their start and end apart: 5, of which 3 were waited for; matrix products, arithmetic and copies ran while one was open for 1% of the time, Pallas kernels for 19%

profile of v4, /device:TPU:112, one launch (start us, length us, event | category | flops | bytes accessed | tf_op | source)
XLA Modules:
  0.0 682.5 jit_solution(1652995144490579059)
XLA Ops:
  8.1 1.6 fusion.14
  10.9 2.7 fusion.4.loc_ref
  13.5 55.8 %gather_in.2 = (bf16[1536,640]{1,0:T(8,128)(2,1)}, bf16[1536,1024]{1,0:T(8,128)(2,1)}, bf16[1536,1024]{1,0:T(8,128)(2,1)}, bf16[1536,1024]{1,0:T(8,128)(2,1)}) custom-call(bf16[192,3072]{1,0:T(8,128)(2,1)} %fusion.4.loc_ref, bf16[2,3072,640]{2,1,0:T(8,128)(2,1)} %refs_3_.5, bf16[2,3072,1024]{2,1,0:T(8,128)(2,1)} %refs_4_.3, bf16[2,3072,1024]{2,1,0:T(8,128)(2,1)} %refs_5_.4), custom_call_target="tpu_custom_call" | custom-call | flops 25367150592 | bytes 34209792 | tf_op jit(solution)/shard_map/gather_in/pallas_call | solution.py:415
  69.3 19.0 %attn_fwd.1 = (bf16[1536,640]{1,0:T(8,128)(2,1)}, bf16[1536,384]{1,0:T(8,128)(2,1)}, f32[1536,384]{1,0:T(8,128)}) custom-call(bf16[1536,640]{1,0:T(8,128)(2,1)} %get-tuple-element.56.qkv_ref, f32[1536,128]{1,0:T(8,128)} %constant.16.clone.cos_ref.refs_5_, f32[1536,128]{1,0:T(8,128)} %constant.17.clone.sin_ref.refs_6_), custom_call_target="tpu_custom_call" | custom-call | flops 3623878656 | bytes 7864320 | tf_op jit(solution)/shard_map/attn_fwd/pallas_call | solution.py:103
  88.3 87.7 %scatter_out.1 = f32[192,3072]{1,0:T(8,128)} custom-call(bf16[1536,384]{1,0:T(8,128)(2,1)} %get-tuple-element.57.refs_0_.attn_ref, bf16[1536,1024]{1,0:T(8,128)(2,1)} %get-tuple-element.58.refs_1_, bf16[2,384,3072]{2,1,0:T(8,128)(2,1)} %refs_0_.7, bf16[2,1024,3072]{2,1,0:T(8,128)(2,1)} %refs_1_.7), custom_call_target="tpu_custom_call" | custom-call | flops 13287555072 | bytes 15335424 | tf_op jit(solution)/shard_map/scatter_out/pallas_call | solution.py:622
  176.0 2.5 fusion.12
  180.9 54.0 %gather_in.3 = (bf16[1536,640]{1,0:T(8,128)(2,1)}, bf16[1536,1024]{1,0:T(8,128)(2,1)}, bf16[1536,1024]{1,0:T(8,128)(2,1)}) custom-call(bf16[192,3072]{1,0:T(8,128)(2,1)} %fusion.5.loc_ref, bf16[2,3072,640]{2,1,0:T(8,128)(2,1)} %refs_3_.5, bf16[2,3072,1024]{2,1,0:T(8,128)(2,1)} %refs_4_.3, bf16[2,3072,1024]{2,1,0:T(8,128)(2,1)} %refs_5_.4), custom_call_target="tpu_custom_call" | custom-call | flops 25367150592 | bytes 34209792 | tf_op jit(solution)/shard_map/gather_in/pallas_call | solution.py:415
  235.0 54.2 %gather_back.2 = (bf16[1536,384]{1,0:T(8,128)(2,1)}, bf16[1536,1024]{1,0:T(8,128)(2,1)}, bf16[1536,1024]{1,0:T(8,128)(2,1)}, bf16[1536,1024]{1,0:T(8,128)(2,1)},...) custom-call(bf16[192,3072]{1,0:T(8,128)(2,1)} %loc_ref.1, ...), custom_call_target="tpu_custom_call" | custom-call | flops 13287555072 | bytes 22413312 | tf_op jit(solution)/shard_map/gather_back/pallas_call | solution.py:415
  289.4 27.1 %attn_bwd.2.refs_0_ = bf16[1536,640]{1,0:T(8,128)(2,1)} custom-call(bf16[1536,640]{1,0:T(8,128)(2,1)} %get-tuple-element.62.rot_ref, f32[1536,384]{1,0:T(8,128)} %get-tuple-element.63.lse_ref, bf16[1536,384]{1,0:T(8,128)(2,1)} %get-tuple-element.64.dout_ref, f32[1536,128]{1,0:T(8,128)} %constant.16.clone.cos_ref.refs_5_, ...), custom_call_target="tpu_custom_call" | custom-call | flops 9059696640 | bytes 7864320 | tf_op jit(solution)/shard_map/attn_bwd/pallas_call | solution.py:169
  316.5 20.5 %grad_out.2 = (bf16[2,384,3072]{2,1,0:T(8,128)(2,1)}, bf16[2,1024,3072]{2,1,0:T(8,128)(2,1)}) custom-call(bf16[1536,384]{1,0:T(8,128)(2,1)} %get-tuple-element.65.attn_ref, bf16[1536,1024]{1,0:T(8,128)(2,1)} %get-tuple-element.67.hidden_ref, bf16[1536,3072]{1,0:T(8,128)(2,1)} %get-tuple-element.68.dy_ref), custom_call_target="tpu_custom_call" | custom-call | flops 13287555072 | bytes 22413312 | tf_op jit(solution)/shard_map/grad_out/pallas_call | solution.py:219
  337.0 2.0 all-gather.3.cloned.1.call-done.refs_6_
  339.0 88.2 %scatter_back.2 = (f32[192,3072]{1,0:T(8,128)}, bf16[3072,640]{1,0:T(8,128)(2,1)}, bf16[3072,1024]{1,0:T(8,128)(2,1)}, bf16[3072,1024]{1,0:T(8,128)(2,1)}) custom-call(bf16[1536,640]{1,0:T(8,128)(2,1)} %attn_bwd.2.refs_0_, bf16[1536,1024]{1,0:T(8,128)(2,1)} %get-tuple-element.72.refs_1_, bf16[1536,1024]{1,0:T(8,128)(2,1)} %get-tuple-element.73.refs_2_, ...), custom_call_target="tpu_custom_call" | custom-call | flops 50734301184 | bytes 27131904 | tf_op jit(solution)/shard_map/scatter_back/pallas_call | solution.py:622
  427.2 3.3 fusion.6
  430.5 3.1 fusion.9.loc_ref
  433.6 51.3 %gather_back.3 = (bf16[1536,384]{1,0:T(8,128)(2,1)}, bf16[1536,1024]{1,0:T(8,128)(2,1)}, bf16[1536,1024]{1,0:T(8,128)(2,1)}, bf16[1536,1024]{1,0:T(8,128)(2,1)}, bf16[1536,3072]{1,0:T(8,128)(2,1)}) custom-call(bf16[192,3072]{1,0:T(8,128)(2,1)} %fusion.9.loc_ref, bf16[2,384,3072]{2,1,0:T(8,128)(2,1)} %refs_0_.7, bf16[2,1024,3072]{2,1,0:T(8,128)(2,1)} %refs_1_.7, ...), custom_call_target="tpu_custom_call" | custom-call | flops 13287555072 | bytes 22413312 | tf_op jit(solution)/shard_map/gather_back/pallas_call | solution.py:415
  485.1 27.1 %attn_bwd.3.refs_0_.refs_1_ = bf16[1536,640]{1,0:T(8,128)(2,1)} custom-call(bf16[1536,640]{1,0:T(8,128)(2,1)} %get-tuple-element.76.rot_ref, f32[1536,384]{1,0:T(8,128)} %get-tuple-element.77.lse_ref, bf16[1536,384]{1,0:T(8,128)(2,1)} %get-tuple-element.80.dout_ref, f32[1536,128]{1,0:T(8,128)} %constant.16.clone.cos_ref.refs_5_, ...), custom_call_target="tpu_custom_call" | custom-call | flops 9059696640 | bytes 7864320 | tf_op jit(solution)/shard_map/attn_bwd/pallas_call | solution.py:169
  512.2 20.5 %grad_out.3 = (bf16[2,384,3072]{2,1,0:T(8,128)(2,1)}, bf16[2,1024,3072]{2,1,0:T(8,128)(2,1)}) custom-call(bf16[1536,384]{1,0:T(8,128)(2,1)} %get-tuple-element.57.refs_0_.attn_ref, bf16[1536,1024]{1,0:T(8,128)(2,1)} %get-tuple-element.82.hidden_ref, bf16[1536,3072]{1,0:T(8,128)(2,1)} %get-tuple-element.83.dy_ref, ...), custom_call_target="tpu_custom_call", output_to_operand_aliasing={{0}: (3, {}), {1}: (4, {})} | custom-call | flops 13287555072 | bytes 22413312 | tf_op jit(solution)/shard_map/grad_out/pallas_call | solution.py:219
  532.7 3.6 all-gather.5.cloned.1.call-done.refs_0_
  536.3 88.2 %scatter_back.3 = f32[192,3072]{1,0:T(8,128)} custom-call(bf16[1536,640]{1,0:T(8,128)(2,1)} %attn_bwd.3.refs_0_.refs_1_, bf16[1536,1024]{1,0:T(8,128)(2,1)} %get-tuple-element.95.refs_1_.refs_2_, bf16[1536,1024]{1,0:T(8,128)(2,1)} %get-tuple-element.96.refs_2_.refs_3_, bf16[2,3072,640]{2,1,0:T(8,128)(2,1)} %refs_3_.5, bf16[2,3072,1024]{2,1,0:T(8,128)(2,1)} %refs_4_.3, ...), custom_call_target="tpu_custom_call" | custom-call | flops 25367150592 | bytes 27131904 | tf_op jit(solution)/shard_map/scatter_back/pallas_call | solution.py:622
  624.6 3.1 fusion.7
  627.8 36.8 %grad_in.1 = (bf16[2,3072,640]{2,1,0:T(8,128)(2,1)}, bf16[2,3072,1024]{2,1,0:T(8,128)(2,1)}, bf16[2,3072,1024]{2,1,0:T(8,128)(2,1)}) custom-call(bf16[1536,3072]{1,0:T(8,128)(2,1)} %all-gather.5.cloned.1.call-done.refs_0_, bf16[1536,640]{1,0:T(8,128)(2,1)} %attn_bwd.3.refs_0_.refs_1_, bf16[1536,1024]{1,0:T(8,128)(2,1)} %get-tuple-element.95.refs_1_.refs_2_, ...), custom_call_target="tpu_custom_call" | custom-call | flops 25367150592 | bytes 67239936 | tf_op jit(solution)/shard_map/grad_in/pallas_call | solution.py:192
  666.0 2.7 collective-permute-done.1
  668.7 2.0 collective-permute-start.2
  670.6 4.2 fusion.11
  (36 shorter events, 6.8 us)
Async XLA Ops:
  7.2 331.8 %all-gather.3.cloned.1.call-start = ((), (), s32[]{:S(2)}) async-start(), calls=%async_computation | async-start | bytes 10616832 | tf_op jit(solution)/shard_map/all_gather | solution.py:650
  8.1 2.2 copy-start.3
  9.7 0.6 copy-start.7
  10.3 0.6 copy-start.5
  178.5 1.1 copy-start
  289.3 247.0 %all-gather.5.cloned.1.call-start = ((), (), s32[]{:S(2)}) async-start(), calls=%async_computation.1 | async-start | bytes 10616832 | tf_op jit(solution)/shard_map/all_gather | solution.py:650
  427.2 3.3 copy-start.1
  427.2 3.3 copy-start.2
  536.3 88.3 %copy-start.4 = (f32[1,3072]{1,0:T(1,128)S(1)}, f32[1,3072]{1,0:T(1,128)}, u32[]{:S(2)}) copy-start(f32[1,3072]{1,0:T(1,128)} %copy-done.3) | copy-start | bytes 36868
  536.3 88.3 %copy-start.6 = (f32[192]{0:T(256)S(1)}, f32[192]{0:T(256)}, u32[]{:S(2)}) copy-start(f32[192]{0:T(256)} %copy-done.5) | copy-start | bytes 2308
  627.7 37.0 %collective-permute-start = (f32[2,3072]{1,0:T(2,128)S(1)}, f32[2,3072]{1,0:T(2,128)S(1)}, u32[]{:S(2)}, u32[]{:S(2)}) collective-permute-start(f32[2,3072]{1,0:T(2,128)S(1)} %pad_maximum_fusion), channel_id=1, source_target_pairs={{0,1},{1,0},{2,3},{3,2},{4,5},{5,4},{6,7},{7,6},{8,9},{9,8},{10,11... | collective-permute-start | bytes 73736 | tf_op jit(solution)/shard_map/ppermute | solution.py:666
  627.8 38.1 %copy-start.8 = (f32[192]{0:T(256)S(1)}, f32[192]{0:T(256)}, u32[]{:S(2)}) copy-start(f32[192]{0:T(256)} %copy-done.7) | copy-start | bytes 2308
  664.7 3.9 collective-permute-start.1
  668.7 6.1 collective-permute-start.2
Sparse Core Ops, SparseCore 0:
  289.4 49.5 all-gather.2
  485.2 51.0 all-gather.4

commit v5 on v4

--- a/solution.py
+++ b/solution.py
@@ -12,6 +12,7 @@
 NORM_EPS = 1e-5
 ROPE_BASE = 10000.0
 Q_BLOCK = 256
+FINISH_ROWS = 32
 VMEM_LIMIT = 63 * 1024 * 1024
 F32 = jnp.float32
 BF16 = jnp.bfloat16
@@ -330,12 +331,26 @@
     full, scratch = refs[n_inputs + n_outs], refs[n_inputs + n_outs + 1:]
     held, staged = scratch[:n_inputs], scratch[n_inputs:-5]
     load_sem, store_sem, attn_sem, send, recv = scratch[-5:]
-    loads = [pltpu.make_async_copy(src.at[layer] if idx < n_weights else src, dst, load_sem.at[idx]) for idx, (src, dst) in enumerate(zip(inputs, held))]
+    n_tiles = staged[1].shape[1] // tile
+    n_whole = 1 if forward else n_inputs
+    loads = [
+        pltpu.make_async_copy(src.at[layer] if idx < n_weights else src, dst, load_sem.at[idx, 0])
+        for idx, (src, dst) in enumerate(zip(inputs[:n_whole], held[:n_whole]))
+    ]
+
+    def tile_loads(idx):
+        cols = pl.ds(pl.multiple_of(idx * tile, tile), tile)
+        return [pltpu.make_async_copy(inputs[place].at[layer, :, cols], held[place].at[:, cols], load_sem.at[place, idx]) for place in range(1, n_weights)]
+
     n_dots = n_weights + (1 if with_hidden else 0) if forward else 4
     attn_loads = loads[4:] if attn_group else []
     dot_loads = loads[:len(loads) - len(attn_loads)]
     for load in attn_loads + dot_loads:
         load.start()
+    if forward:
+        for idx in range(n_tiles):
+            for load in tile_loads(idx):
+                load.start()
     stores = []
 
     def attention():
@@ -366,6 +381,9 @@
 
         def one_tile(idx, carry):
             cols = pl.ds(pl.multiple_of(idx * tile, tile), tile)
+            if forward and not group:
+                for load in tile_loads(idx):
+                    load.wait()
             if forward:
                 gate = dot(rows_of(full), held[1][:, cols], MATMUL).astype(BF16)
                 up = dot(rows_of(full), held[2][:, cols], MATMUL).astype(BF16)
@@ -382,7 +400,7 @@
                 put(staged[3], cols, d_up.astype(BF16))
             return carry
 
-        lax.fori_loop(0, staged[1].shape[1] // tile, one_tile, 0)
+        lax.fori_loop(0, n_tiles, one_tile, 0)
         sources = list(staged[:n_dots]) + ([] if forward else [full])
         for idx, source in enumerate(sources):
             for place, rows in enumerate(pieces):
@@ -422,7 +440,7 @@
         + [pltpu.VMEM(item.shape, item.dtype) for item in saved]
         + [pltpu.VMEM(*item) for item in staged + attn_outs]
         + [
-            pltpu.SemaphoreType.DMA((len(all_inputs),)),
+            pltpu.SemaphoreType.DMA((len(all_inputs), widths[1] // tile)),
             pltpu.SemaphoreType.DMA((5, 2 * CORES, len(outs))),
             pltpu.SemaphoreType.DMA((3,)),
             pltpu.SemaphoreType.DMA((17,)),
@@ -477,14 +495,15 @@
             store.wait()
 
 
-def dots_scatter_kernel(chips, layer, dims, n_terms, tile, with_grads, *refs):
+def dots_scatter_kernel(chips, layer, dims, n_terms, n_rows_in, tile, with_grads, *refs):
     lhs_hbm, rhs_refs, refs = refs[:n_terms], refs[n_terms:2 * n_terms], refs[2 * n_terms:]
+    rows_hbm, gain_ref, refs = refs[:n_rows_in], refs[n_rows_in], refs[n_rows_in + 1:]
     if with_grads:
         u_ref, refs = refs[0], refs[1:]
-    out_ref, refs = refs[0], refs[1:]
+    out_ref, side_out_ref, refs = refs[0], refs[1], refs[2:]
     if with_grads:
         grad_refs, refs = refs[:n_terms], refs[n_terms:]
-    lhs_refs, held, scratch = refs[:n_terms], refs[n_terms:2 * n_terms], refs[2 * n_terms:]
+    lhs_refs, held, rows_in, row_sem, scratch = refs[:n_terms], refs[n_terms:2 * n_terms], refs[2 * n_terms:2 * n_terms + n_rows_in], refs[2 * n_terms + n_rows_in], refs[2 * n_terms + n_rows_in + 1:]
     part, acc, from_far, from_side, lhs_sem, load_sem, core_send, core_recv, send, recv = scratch[:10]
     n_rows, n_cols = out_ref.shape
     half = n_cols // 2
@@ -520,6 +539,9 @@
     for step in range(1, 4):
         for load in lhs_loads(step):
             load.start()
+    row_loads = [pltpu.make_async_copy(src, dst, row_sem.at[idx]) for idx, (src, dst) in enumerate(zip(rows_hbm, rows_in))]
+    for load in row_loads:
+        load.start()
     enter_ring((partner, left, right))
 
     def to_core(step, which, idx):
@@ -589,19 +611,37 @@
     lax.fori_loop(0, n_tiles, pass_on, 0)
     if with_grads:
         weight_grads(u_ref, lhs_refs, grad_refs, *scratch[10:])
+    for load in row_loads:
+        load.wait()
     for which in range(2):
         for idx in range(n_tiles):
-            slot = which * n_tiles + idx
             hop(1, which, idx).wait_recv()
             hop(2, which, idx).wait_recv()
-            out_ref[:, pl.ds(slot * tile, tile)] = acc[3, slot] + from_side[0, slot] + from_side[1, slot]
+    if n_rows_in > 1:
+        side_out_ref[...] = jnp.zeros_like(side_out_ref)
+
+    def finish(idx, carry):
+        rows = pl.ds(pl.multiple_of(idx * FINISH_ROWS, FINISH_ROWS), FINISH_ROWS)
+        total = jnp.concatenate([acc[3, slot, rows, :] + from_side[0, slot, rows, :] + from_side[1, slot, rows, :] for slot in range(2 * n_tiles)], axis=1)
+        x_rows = rows_in[0][rows, :].astype(F32)
+        if n_rows_in == 1:
+            x_next = (x_rows + total).astype(BF16)
+            out_ref[rows, :] = x_next
+            side_out_ref[rows, :] = rms_scale(x_next.astype(F32), gain_ref[...]).astype(BF16)
+        else:
+            d_x, gain_grad = jax.vjp(rms_scale, x_rows, gain_ref[...])[1](total.astype(BF16).astype(F32))
+            out_ref[rows, :] = (rows_in[1][rows, :].astype(F32) + d_x).astype(BF16)
+            side_out_ref[...] += gain_grad
+        return carry
+
+    lax.fori_loop(0, n_rows // FINISH_ROWS, finish, 0)
     for step in range(3):
         for which in range(2):
             for idx in range(n_tiles):
                 hop(step, which, idx).wait_send()
 
 
-def dots_scatter(terms, layer, dims, tp_size, collective_id, name, u_full=None, tile=512, grad_tile=512):
+def dots_scatter(terms, layer, dims, rows_in, gain_row, tp_size, collective_id, name, u_full=None, tile=512, grad_tile=512):
     seq_len = terms[0][0].shape[0]
     n_cols = terms[0][1].shape[2] if dims is MATMUL else terms[0][1].shape[1]
     n_rows = seq_len // tp_size
@@ -609,7 +649,8 @@
     with_grads = u_full is not None
     n_terms = len(terms)
     any_spec, vmem_spec = pl.BlockSpec(memory_space=pl.ANY), pl.BlockSpec(memory_space=pltpu.VMEM)
-    outs, extra_inputs, extra_scratch = [jax.ShapeDtypeStruct((n_rows, n_cols), F32)], (), []
+    side_out = jax.ShapeDtypeStruct((n_rows, n_cols), BF16) if len(rows_in) == 1 else jax.ShapeDtypeStruct((1, n_cols), F32)
+    outs, extra_inputs, extra_scratch = [jax.ShapeDtypeStruct((n_rows, n_cols), BF16), side_out], (), []
     if with_grads:
         outs += [jax.ShapeDtypeStruct((n_cols, lhs.shape[1]), BF16) for lhs, _ in terms]
         extra_inputs = (u_full,)
@@ -620,13 +661,15 @@
             pltpu.SemaphoreType.DMA((2, n_terms)),
         ]
     results = pl.pallas_call(
-        functools.partial(dots_scatter_kernel, tp_size // CORES, layer, dims, n_terms, tile, with_grads),
+        functools.partial(dots_scatter_kernel, tp_size // CORES, layer, dims, n_terms, len(rows_in), tile, with_grads),
         out_shape=outs,
-        in_specs=[any_spec] * (2 * n_terms + len(extra_inputs)),
-        out_specs=[vmem_spec] + [any_spec] * (len(outs) - 1),
+        in_specs=[any_spec] * (2 * n_terms + len(rows_in)) + [vmem_spec] + [any_spec] * len(extra_inputs),
+        out_specs=[vmem_spec] * 2 + [any_spec] * (len(outs) - 2),
         scratch_shapes=[pltpu.VMEM(lhs.shape, BF16) for lhs, _ in terms]
         + [pltpu.VMEM(rhs.shape[1:], BF16) for _, rhs in terms]
+        + [pltpu.VMEM((n_rows, n_cols), BF16)] * len(rows_in)
         + [
+            pltpu.SemaphoreType.DMA((len(rows_in),)),
             pltpu.VMEM((2, CORES, n_rows, tile), F32),
             pltpu.VMEM((4, n_cols // tile, n_rows, tile), F32),
             pltpu.VMEM((n_cols // tile, n_rows, tile), F32),
@@ -642,8 +685,8 @@
         compiler_params=pltpu.CompilerParams(vmem_limit_bytes=VMEM_LIMIT, collective_id=collective_id, has_side_effects=True),
         cost_estimate=cost(2 * seq_len * depth * n_cols * (2 if with_grads else 1), 2 * depth * (seq_len + n_cols) + 4 * n_rows * n_cols),
         name=name,
-    )(*[lhs for lhs, _ in terms], *[rhs for _, rhs in terms], *extra_inputs)
-    return (results[0], tuple(results[1:])) if with_grads else results[0]
+    )(*[lhs for lhs, _ in terms], *[rhs for _, rhs in terms], *rows_in, gain_row, *extra_inputs)
+    return results[0], results[1], tuple(results[2:])
 
 
 def gather_rows(rows_loc):
@@ -674,17 +717,16 @@
         cos_tab, sin_tab = rope_tables(seq_len)
         saved_all = []
         x_cur = x_loc
+        u_loc = rms_scale(x_loc.astype(F32), norm_gain[0]).astype(BF16)
         for layer in range(n_layers):
             last = layer == n_layers - 1
-            x_f32 = x_cur.astype(F32)
-            u_loc = rms_scale(x_f32, norm_gain[layer]).astype(BF16)
             outs = gather_dots(u_loc, (w_qkv, w_gate, w_up), layer, True, not last, tp_size, layer, "gather_in")
             qkv, gate, up = outs[:3]
             rot, attn_out, lse = (qkv, None, None) if last else attn_fwd(qkv, cos_tab, sin_tab, group)
             saved_all.append((x_cur, u_loc, rot, attn_out, lse, gate, up))
             if not last:
-                block_sum = dots_scatter([(attn_out, w_out), (outs[3], w_down)], layer, MATMUL, tp_size, n_layers + layer, "scatter_out")
-                x_cur = (x_f32 + block_sum).astype(BF16)
+                terms = [(attn_out, w_out), (outs[3], w_down)]
+                x_cur, u_loc, _ = dots_scatter(terms, layer, MATMUL, (x_cur,), norm_gain[layer + 1:layer + 2], tp_size, n_layers + layer, "scatter_out")
 
         out_grads, gain_grads, done_grads = (), [], []
         for layer in reversed(range(n_layers)):
@@ -700,19 +742,16 @@
             out_grads = grad_out(attn_out, hidden, dy_full, layer, n_layers, out_grads)
             d_qkv, u_full, out_grads = lax.optimization_barrier((d_qkv, u_full, out_grads))
             terms = [(d_qkv, w_qkv), (d_gate, w_gate), (d_up, w_up)]
+            dy_loc, gain_grad, done = dots_scatter(
+                terms, layer, CONTRACT_LAST, (x_in, dy_loc), norm_gain[layer:layer + 1], tp_size, 3 * n_layers + layer, "scatter_back", u_full if layer else None
+            )
+            gain_grads.insert(0, gain_grad)
             if layer:
-                d_normed, done = dots_scatter(terms, layer, CONTRACT_LAST, tp_size, 3 * n_layers + layer, "scatter_back", u_full)
                 done_grads.insert(0, done)
             else:
-                d_normed = dots_scatter(terms, layer, CONTRACT_LAST, tp_size, 3 * n_layers + layer, "scatter_back")
-                d_normed, u_full, d_qkv, d_gate, d_up = lax.optimization_barrier((d_normed, u_full, d_qkv, d_gate, d_up))
+                gain_grads[0], u_full, d_qkv, d_gate, d_up = lax.optimization_barrier((gain_grad, u_full, d_qkv, d_gate, d_up))
                 in_grads = grad_in(u_full, (d_qkv, d_gate, d_up), done_grads)
-            d_normed = d_normed.astype(BF16)
-            norm_pull = jax.vjp(rms_scale, x_in.astype(F32), norm_gain[layer])[1]
-            d_x_norm, gain_grad = norm_pull(d_normed.astype(F32))
-            dy_loc = (dy_loc.astype(F32) + d_x_norm).astype(BF16)
-            gain_grads.insert(0, gain_grad)
-        grad_gain = sum_over_tp(jnp.stack(gain_grads))
+        grad_gain = sum_over_tp(jnp.concatenate(gain_grads))
         return (dy_loc, grad_gain, in_grads[0], out_grads[0], in_grads[1], in_grads[2], out_grads[1])
 
     return jax.shard_map(device_program, mesh=mesh, in_specs=(row_spec, row_spec, P(None, None), col_spec, inner_spec, col_spec, col_spec, inner_spec), out_specs=(row_spec, P('dp', None), P('dp', None, 'tp'), P('dp', 'tp', None), P('dp', None, 'tp'), P('dp', None, 'tp'), P('dp', 'tp', None)), check_vma=False)

time: 686 us -> 681 us (level)
  other arithmetic: 22.5 us -> 7.09 us
  Pallas kernels: 631 us -> 639 us
    convert_element_type x4 -> x1, other arithmetic: 11.3 us -> 2.66 us  [device_program(): u_loc = rms_scale(x_loc.astype(F32), norm_gain[0]).astype(BF16)]
    pallas_call x3, Pallas kernels: 264 us -> 271 us  [dots_scatter(): pl.pallas_call(functools.partial(dots_scatter_kernel, tp_size // CORES, l...]
  transfers between devices with their start and end apart: 5 -> 5, of which waited for: 3 -> 4; matrix products, arithmetic and copies ran while one was open for 1% -> 0% of each run, Pallas kernels for 19% -> 20%
where the time goes in v5:
time: 681 us; the launch traced here: 678 us
  Pallas kernels  639 us (94%)
  between operations  14.3 us (2%)
  waiting for transfers between devices  9.52 us (1%)
  other arithmetic  7.09 us (1%)
    pallas_call x3, Pallas kernels, dots_scatter(): pl.pallas_call(functools.partial(dots_scatter_kernel, tp_size // CORES, l...  271 us
    pallas_call x4, Pallas kernels, gather_dots(): pl.pallas_call(functools.partial(gather_dots_kernel, chips, layer, forwar...  216 us
    pallas_call x2, Pallas kernels, attn_bwd(): pl.pallas_call(functools.partial(attn_bwd_kernel, group), out_shape=jax.S...  54.3 us
    pallas_call x2, Pallas kernels, grad_out(): pl.pallas_call(grad_out_kernel, out_shape=(jax.ShapeDtypeStruct((n_layers...  41 us
    pallas_call x1, Pallas kernels, grad_in(): pl.pallas_call(functools.partial(grad_in_kernel, n_rhs), out_shape=[jax.S...  36.8 us
    pallas_call x1, Pallas kernels, attn_fwd(): pl.pallas_call(functools.partial(attn_fwd_kernel, group), out_shape=(jax....  19.4 us
  transfers between devices with their start and end apart: 5, of which 4 were waited for; matrix products, arithmetic and copies ran while one was open for 0% of the time, Pallas kernels for 20%

profile of v5, /device:TPU:112, one launch (start us, length us, event | category | flops | bytes accessed | tf_op | source)
XLA Modules:
  0.0 677.7 jit_solution(16809796825680178960)
XLA Ops:
  7.2 1.6 fusion
  8.8 1.4 fusion.4
  10.9 2.7 fusion.2.loc_ref
  13.5 55.8 %gather_in.2 = (bf16[1536,640]{1,0:T(8,128)(2,1)}, bf16[1536,1024]{1,0:T(8,128)(2,1)}, bf16[1536,1024]{1,0:T(8,128)(2,1)}, bf16[1536,1024]{1,0:T(8,128)(2,1)}) custom-call(bf16[192,3072]{1,0:T(8,128)(2,1)} %fusion.2.loc_ref, bf16[2,3072,640]{2,1,0:T(8,128)(2,1)} %refs_3_.5, bf16[2,3072,1024]{2,1,0:T(8,128)(2,1)} %refs_4_.5, bf16[2,3072,1024]{2,1,0:T(8,128)(2,1)} %refs_5_.4), custom_call_target="tpu_custom_call" | custom-call | flops 25367150592 | bytes 34209792 | tf_op jit(solution)/shard_map/gather_in/pallas_call | solution.py:433
  69.4 19.4 %attn_fwd.1 = (bf16[1536,640]{1,0:T(8,128)(2,1)}, bf16[1536,384]{1,0:T(8,128)(2,1)}, f32[1536,384]{1,0:T(8,128)}) custom-call(bf16[1536,640]{1,0:T(8,128)(2,1)} %get-tuple-element.61.qkv_ref, f32[1536,128]{1,0:T(8,128)} %constant.11.clone.cos_ref.refs_5_, f32[1536,128]{1,0:T(8,128)} %constant.12.clone.sin_ref.refs_6_), custom_call_target="tpu_custom_call" | custom-call | flops 3623878656 | bytes 7864320 | tf_op jit(solution)/shard_map/attn_fwd/pallas_call | solution.py:104
  88.7 89.6 %scatter_out.1 = (bf16[192,3072]{1,0:T(8,128)(2,1)}, bf16[192,3072]{1,0:T(8,128)(2,1)}) custom-call(bf16[1536,384]{1,0:T(8,128)(2,1)} %get-tuple-element.64.refs_0_.attn_ref, bf16[1536,1024]{1,0:T(8,128)(2,1)} %get-tuple-element.65.refs_1_, bf16[2,384,3072]{2,1,0:T(8,128)(2,1)} %refs_0_.7, bf16[2,1024,3072]{2,1,0:T(8,128)(2,1)} %refs_1_.7, ...), custom_call_target="tpu_custom_call" | custom-call | flops 13287555072 | bytes 15335424 | tf_op jit(solution)/shard_map/scatter_out/pallas_call | solution.py:663
  178.3 54.2 %gather_in.3 = (bf16[1536,640]{1,0:T(8,128)(2,1)}, bf16[1536,1024]{1,0:T(8,128)(2,1)}, bf16[1536,1024]{1,0:T(8,128)(2,1)}) custom-call(bf16[192,3072]{1,0:T(8,128)(2,1)} %get-tuple-element.74.loc_ref, bf16[2,3072,640]{2,1,0:T(8,128)(2,1)} %refs_3_.5, bf16[2,3072,1024]{2,1,0:T(8,128)(2,1)} %refs_4_.5, bf16[2,3072,1024]{2,1,0:T(8,128)(2,1)} %refs_5_.4), custom_call_target="tpu_custom_call" | custom-call | flops 25367150592 | bytes 34209792 | tf_op jit(solution)/shard_map/gather_in/pallas_call | solution.py:433
  232.5 54.4 %gather_back.2 = (bf16[1536,384]{1,0:T(8,128)(2,1)}, bf16[1536,1024]{1,0:T(8,128)(2,1)}, bf16[1536,1024]{1,0:T(8,128)(2,1)}, bf16[1536,1024]{1,0:T(8,128)(2,1)},...) custom-call(bf16[192,3072]{1,0:T(8,128)(2,1)} %refs_7_.1, ...), custom_call_target="tpu_custom_call" | custom-call | flops 13287555072 | bytes 22413312 | tf_op jit(solution)/shard_map/gather_back/pallas_call | solution.py:433
  287.1 27.1 %attn_bwd.2.refs_0_ = bf16[1536,640]{1,0:T(8,128)(2,1)} custom-call(bf16[1536,640]{1,0:T(8,128)(2,1)} %get-tuple-element.70.rot_ref, f32[1536,384]{1,0:T(8,128)} %get-tuple-element.71.lse_ref, bf16[1536,384]{1,0:T(8,128)(2,1)} %get-tuple-element.72.dout_ref, f32[1536,128]{1,0:T(8,128)} %constant.11.clone.cos_ref.refs_5_, ...), custom_call_target="tpu_custom_call" | custom-call | flops 9059696640 | bytes 7864320 | tf_op jit(solution)/shard_map/attn_bwd/pallas_call | solution.py:170
  314.2 20.5 %grad_out.2 = (bf16[2,384,3072]{2,1,0:T(8,128)(2,1)}, bf16[2,1024,3072]{2,1,0:T(8,128)(2,1)}) custom-call(bf16[1536,384]{1,0:T(8,128)(2,1)} %get-tuple-element.73.attn_ref, bf16[1536,1024]{1,0:T(8,128)(2,1)} %get-tuple-element.75.hidden_ref, bf16[1536,3072]{1,0:T(8,128)(2,1)} %get-tuple-element.76.dy_ref), custom_call_target="tpu_custom_call" | custom-call | flops 13287555072 | bytes 22413312 | tf_op jit(solution)/shard_map/grad_out/pallas_call | solution.py:220
  334.7 2.1 all-gather.3.cloned.1.call-done.refs_9_
  336.8 90.9 %scatter_back.2 = (bf16[192,3072]{1,0:T(8,128)(2,1)}, f32[1,3072]{1,0:T(1,128)}, bf16[3072,640]{1,0:T(8,128)(2,1)}, bf16[3072,1024]{1,0:T(8,128)(2,1)}, bf16[3072,1024]{1,0:T(8,128)(2,1)}) custom-call(bf16[1536,640]{1,0:T(8,128)(2,1)} %attn_bwd.2.refs_0_, bf16[1536,1024]{1,0:T(8,128)(2,1)} %get-tuple-element.80.refs_1_, ...), custom_call_target="tpu_custom_call" | custom-call | flops 50734301184 | bytes 27131904 | tf_op jit(solution)/shard_map/scatter_back/pallas_call | solution.py:663
  427.7 51.6 %gather_back.3 = (bf16[1536,384]{1,0:T(8,128)(2,1)}, bf16[1536,1024]{1,0:T(8,128)(2,1)}, bf16[1536,1024]{1,0:T(8,128)(2,1)}, bf16[1536,1024]{1,0:T(8,128)(2,1)}, bf16[1536,3072]{1,0:T(8,128)(2,1)}) custom-call(bf16[192,3072]{1,0:T(8,128)(2,1)} %get-tuple-element.84.loc_ref.refs_7_, bf16[2,384,3072]{2,1,0:T(8,128)(2,1)} %refs_0_.7, ...), custom_call_target="tpu_custom_call" | custom-call | flops 13287555072 | bytes 22413312 | tf_op jit(solution)/shard_map/gather_back/pallas_call | solution.py:433
  479.5 27.2 %attn_bwd.3.refs_0_.refs_1_ = bf16[1536,640]{1,0:T(8,128)(2,1)} custom-call(bf16[1536,640]{1,0:T(8,128)(2,1)} %get-tuple-element.62.rot_ref, f32[1536,384]{1,0:T(8,128)} %get-tuple-element.63.lse_ref, bf16[1536,384]{1,0:T(8,128)(2,1)} %get-tuple-element.87.dout_ref, f32[1536,128]{1,0:T(8,128)} %constant.11.clone.cos_ref.refs_5_, ...), custom_call_target="tpu_custom_call" | custom-call | flops 9059696640 | bytes 7864320 | tf_op jit(solution)/shard_map/attn_bwd/pallas_call | solution.py:170
  506.7 20.5 %grad_out.3 = (bf16[2,384,3072]{2,1,0:T(8,128)(2,1)}, bf16[2,1024,3072]{2,1,0:T(8,128)(2,1)}) custom-call(bf16[1536,384]{1,0:T(8,128)(2,1)} %get-tuple-element.64.refs_0_.attn_ref, bf16[1536,1024]{1,0:T(8,128)(2,1)} %get-tuple-element.89.hidden_ref, bf16[1536,3072]{1,0:T(8,128)(2,1)} %get-tuple-element.90.dy_ref, ...), custom_call_target="tpu_custom_call", output_to_operand_aliasing={{0}: (3, {}), {1}: (4, {})} | custom-call | flops 13287555072 | bytes 22413312 | tf_op jit(solution)/shard_map/grad_out/pallas_call | solution.py:220
  527.2 3.5 all-gather.5.cloned.1.call-done.refs_0_
  530.7 90.8 %scatter_back.3 = (bf16[192,3072]{1,0:T(8,128)(2,1)}, f32[1,3072]{1,0:T(1,128)}) custom-call(bf16[1536,640]{1,0:T(8,128)(2,1)} %attn_bwd.3.refs_0_.refs_1_, bf16[1536,1024]{1,0:T(8,128)(2,1)} %get-tuple-element.105.refs_1_.refs_2_, bf16[1536,1024]{1,0:T(8,128)(2,1)} %get-tuple-element.106.refs_2_.refs_3_, bf16[2,3072,640]{2,1,0:T(8,128)(2,1)} %refs_3_.5, ...), custom_call_target="tpu_custom_call" | custom-call | flops 25367150592 | bytes 27131904 | tf_op jit(solution)/shard_map/scatter_back/pallas_call | solution.py:663
  622.3 1.2 collective-permute-done
  624.2 1.3 collective-permute-start.1
  625.5 2.6 collective-permute-done.1
  628.1 0.7 fusion.5
  628.9 1.9 collective-permute-start.2
  630.8 36.8 %grad_in.1 = (bf16[2,3072,640]{2,1,0:T(8,128)(2,1)}, bf16[2,3072,1024]{2,1,0:T(8,128)(2,1)}, bf16[2,3072,1024]{2,1,0:T(8,128)(2,1)}) custom-call(bf16[1536,3072]{1,0:T(8,128)(2,1)} %all-gather.5.cloned.1.call-done.refs_0_, bf16[1536,640]{1,0:T(8,128)(2,1)} %attn_bwd.3.refs_0_.refs_1_, bf16[1536,1024]{1,0:T(8,128)(2,1)} %get-tuple-element.105.refs_1_.refs_2_, ...), custom_call_target="tpu_custom_call" | custom-call | flops 25367150592 | bytes 67239936 | tf_op jit(solution)/shard_map/grad_in/pallas_call | solution.py:193
  668.3 2.4 copy.22
  (14 shorter events, 3.0 us)
Async XLA Ops:
  7.2 329.7 %all-gather.3.cloned.1.call-start = ((), (), s32[]{:S(2)}) async-start(), calls=%async_computation | async-start | bytes 10616832 | tf_op jit(solution)/shard_map/all_gather | solution.py:693
  10.3 0.6 copy-start.1
  287.0 243.6 %all-gather.5.cloned.1.call-start = ((), (), s32[]{:S(2)}) async-start(), calls=%async_computation.1 | async-start | bytes 10616832 | tf_op jit(solution)/shard_map/all_gather | solution.py:693
  530.7 90.8 %copy-start = (f32[1,3072]{1,0:T(1,128)S(1)}, f32[1,3072]{1,0:T(1,128)}, u32[]{:S(2)}) copy-start(f32[1,3072]{1,0:T(1,128)} %get-tuple-element.102) | copy-start | bytes 36868
  622.2 1.3 collective-permute-start
  624.2 3.9 collective-permute-start.1
  628.9 38.8 %collective-permute-start.2 = (f32[2,3072]{1,0:T(2,128)S(1)}, f32[2,3072]{1,0:T(2,128)S(1)}, u32[]{:S(2)}, u32[]{:S(2)}) collective-permute-start(f32[2,3072]{1,0:T(2,128)S(1)} %fusion.5), channel_id=1, source_target_pairs={{0,4},{1,5},{2,6},{3,7},{4,0},{5,1},{6,2},{7,3},{8,12},{9,13},{10,... | collective-permute-start | bytes 73736 | tf_op jit(solution)/shard_map/ppermute | solution.py:709
Sparse Core Ops, SparseCore 0:
  287.1 49.6 all-gather.2
  479.6 51.0 all-gather.4

commit v6 on v5

--- a/solution.py
+++ b/solution.py
@@ -413,7 +413,7 @@
         copy.wait()
 
 
-def gather_dots(loc, inputs, layer, forward, with_hidden, tp_size, collective_id, name, attn_inputs=(), tile=256):
+def gather_dots(loc, inputs, layer, forward, with_hidden, tp_size, collective_id, name, attn_inputs=(), tile=512):
     n_rows, depth = loc.shape
     seq_len, chips = n_rows * tp_size, tp_size // CORES
     n_weights = 3 if forward else 2

time: 681 us -> 677 us (level)
  no operation moved by 1% of the time
where the time goes in v6:
time: 677 us; the launch traced here: 673 us
  Pallas kernels  634 us (94%)
  between operations  14.4 us (2%)
  waiting for transfers between devices  9.71 us (1%)
  other arithmetic  7.09 us (1%)
    pallas_call x3, Pallas kernels, dots_scatter(): pl.pallas_call(functools.partial(dots_scatter_kernel, tp_size // CORES, l...  271 us
    pallas_call x4, Pallas kernels, gather_dots(): pl.pallas_call(functools.partial(gather_dots_kernel, chips, layer, forwar...  212 us
    pallas_call x2, Pallas kernels, attn_bwd(): pl.pallas_call(functools.partial(attn_bwd_kernel, group), out_shape=jax.S...  54.5 us
    pallas_call x2, Pallas kernels, grad_out(): pl.pallas_call(grad_out_kernel, out_shape=(jax.ShapeDtypeStruct((n_layers...  40.4 us
    pallas_call x1, Pallas kernels, grad_in(): pl.pallas_call(functools.partial(grad_in_kernel, n_rhs), out_shape=[jax.S...  36.8 us
    pallas_call x1, Pallas kernels, attn_fwd(): pl.pallas_call(functools.partial(attn_fwd_kernel, group), out_shape=(jax....  18.8 us
  transfers between devices with their start and end apart: 5, of which 4 were waited for; matrix products, arithmetic and copies ran while one was open for 0% of the time, Pallas kernels for 20%

profile of v6, /device:TPU:112, one launch (start us, length us, event | category | flops | bytes accessed | tf_op | source)
XLA Modules:
  0.0 673.4 jit_solution(2318315958262475889)
XLA Ops:
  7.2 1.6 fusion
  8.8 1.4 fusion.4
  10.9 2.7 fusion.2.loc_ref
  13.5 54.5 %gather_in.2 = (bf16[1536,640]{1,0:T(8,128)(2,1)}, bf16[1536,1024]{1,0:T(8,128)(2,1)}, bf16[1536,1024]{1,0:T(8,128)(2,1)}, bf16[1536,1024]{1,0:T(8,128)(2,1)}) custom-call(bf16[192,3072]{1,0:T(8,128)(2,1)} %fusion.2.loc_ref, bf16[2,3072,640]{2,1,0:T(8,128)(2,1)} %refs_3_.5, bf16[2,3072,1024]{2,1,0:T(8,128)(2,1)} %refs_4_.5, bf16[2,3072,1024]{2,1,0:T(8,128)(2,1)} %refs_5_.4), custom_call_target="tpu_custom_call" | custom-call | flops 25367150592 | bytes 34209792 | tf_op jit(solution)/shard_map/gather_in/pallas_call | solution.py:433
  68.1 18.8 %attn_fwd.1 = (bf16[1536,640]{1,0:T(8,128)(2,1)}, bf16[1536,384]{1,0:T(8,128)(2,1)}, f32[1536,384]{1,0:T(8,128)}) custom-call(bf16[1536,640]{1,0:T(8,128)(2,1)} %get-tuple-element.61.qkv_ref, f32[1536,128]{1,0:T(8,128)} %constant.11.clone.cos_ref.refs_5_, f32[1536,128]{1,0:T(8,128)} %constant.12.clone.sin_ref.refs_6_), custom_call_target="tpu_custom_call" | custom-call | flops 3623878656 | bytes 7864320 | tf_op jit(solution)/shard_map/attn_fwd/pallas_call | solution.py:104
  86.9 89.6 %scatter_out.1 = (bf16[192,3072]{1,0:T(8,128)(2,1)}, bf16[192,3072]{1,0:T(8,128)(2,1)}) custom-call(bf16[1536,384]{1,0:T(8,128)(2,1)} %get-tuple-element.64.refs_0_.attn_ref, bf16[1536,1024]{1,0:T(8,128)(2,1)} %get-tuple-element.65.refs_1_, bf16[2,384,3072]{2,1,0:T(8,128)(2,1)} %refs_0_.7, bf16[2,1024,3072]{2,1,0:T(8,128)(2,1)} %refs_1_.7, ...), custom_call_target="tpu_custom_call" | custom-call | flops 13287555072 | bytes 15335424 | tf_op jit(solution)/shard_map/scatter_out/pallas_call | solution.py:663
  176.5 52.7 %gather_in.3 = (bf16[1536,640]{1,0:T(8,128)(2,1)}, bf16[1536,1024]{1,0:T(8,128)(2,1)}, bf16[1536,1024]{1,0:T(8,128)(2,1)}) custom-call(bf16[192,3072]{1,0:T(8,128)(2,1)} %get-tuple-element.74.loc_ref, bf16[2,3072,640]{2,1,0:T(8,128)(2,1)} %refs_3_.5, bf16[2,3072,1024]{2,1,0:T(8,128)(2,1)} %refs_4_.5, bf16[2,3072,1024]{2,1,0:T(8,128)(2,1)} %refs_5_.4), custom_call_target="tpu_custom_call" | custom-call | flops 25367150592 | bytes 34209792 | tf_op jit(solution)/shard_map/gather_in/pallas_call | solution.py:433
  229.2 54.0 %gather_back.2 = (bf16[1536,384]{1,0:T(8,128)(2,1)}, bf16[1536,1024]{1,0:T(8,128)(2,1)}, bf16[1536,1024]{1,0:T(8,128)(2,1)}, bf16[1536,1024]{1,0:T(8,128)(2,1)},...) custom-call(bf16[192,3072]{1,0:T(8,128)(2,1)} %refs_7_.1, ...), custom_call_target="tpu_custom_call" | custom-call | flops 13287555072 | bytes 22413312 | tf_op jit(solution)/shard_map/gather_back/pallas_call | solution.py:433
  283.4 27.2 %attn_bwd.2.refs_0_ = bf16[1536,640]{1,0:T(8,128)(2,1)} custom-call(bf16[1536,640]{1,0:T(8,128)(2,1)} %get-tuple-element.70.rot_ref, f32[1536,384]{1,0:T(8,128)} %get-tuple-element.71.lse_ref, bf16[1536,384]{1,0:T(8,128)(2,1)} %get-tuple-element.72.dout_ref, f32[1536,128]{1,0:T(8,128)} %constant.11.clone.cos_ref.refs_5_, ...), custom_call_target="tpu_custom_call" | custom-call | flops 9059696640 | bytes 7864320 | tf_op jit(solution)/shard_map/attn_bwd/pallas_call | solution.py:170
  310.6 20.3 %grad_out.2 = (bf16[2,384,3072]{2,1,0:T(8,128)(2,1)}, bf16[2,1024,3072]{2,1,0:T(8,128)(2,1)}) custom-call(bf16[1536,384]{1,0:T(8,128)(2,1)} %get-tuple-element.73.attn_ref, bf16[1536,1024]{1,0:T(8,128)(2,1)} %get-tuple-element.75.hidden_ref, bf16[1536,3072]{1,0:T(8,128)(2,1)} %get-tuple-element.76.dy_ref), custom_call_target="tpu_custom_call" | custom-call | flops 13287555072 | bytes 22413312 | tf_op jit(solution)/shard_map/grad_out/pallas_call | solution.py:220
  330.9 2.2 all-gather.3.cloned.1.call-done.refs_9_
  333.1 90.9 %scatter_back.2 = (bf16[192,3072]{1,0:T(8,128)(2,1)}, f32[1,3072]{1,0:T(1,128)}, bf16[3072,640]{1,0:T(8,128)(2,1)}, bf16[3072,1024]{1,0:T(8,128)(2,1)}, bf16[3072,1024]{1,0:T(8,128)(2,1)}) custom-call(bf16[1536,640]{1,0:T(8,128)(2,1)} %attn_bwd.2.refs_0_, bf16[1536,1024]{1,0:T(8,128)(2,1)} %get-tuple-element.80.refs_1_, ...), custom_call_target="tpu_custom_call" | custom-call | flops 50734301184 | bytes 27131904 | tf_op jit(solution)/shard_map/scatter_back/pallas_call | solution.py:663
  424.0 51.1 %gather_back.3 = (bf16[1536,384]{1,0:T(8,128)(2,1)}, bf16[1536,1024]{1,0:T(8,128)(2,1)}, bf16[1536,1024]{1,0:T(8,128)(2,1)}, bf16[1536,1024]{1,0:T(8,128)(2,1)}, bf16[1536,3072]{1,0:T(8,128)(2,1)}) custom-call(bf16[192,3072]{1,0:T(8,128)(2,1)} %get-tuple-element.84.loc_ref.refs_7_, bf16[2,384,3072]{2,1,0:T(8,128)(2,1)} %refs_0_.7, ...), custom_call_target="tpu_custom_call" | custom-call | flops 13287555072 | bytes 22413312 | tf_op jit(solution)/shard_map/gather_back/pallas_call | solution.py:433
  475.2 27.4 %attn_bwd.3.refs_0_.refs_1_ = bf16[1536,640]{1,0:T(8,128)(2,1)} custom-call(bf16[1536,640]{1,0:T(8,128)(2,1)} %get-tuple-element.62.rot_ref, f32[1536,384]{1,0:T(8,128)} %get-tuple-element.63.lse_ref, bf16[1536,384]{1,0:T(8,128)(2,1)} %get-tuple-element.87.dout_ref, f32[1536,128]{1,0:T(8,128)} %constant.11.clone.cos_ref.refs_5_, ...), custom_call_target="tpu_custom_call" | custom-call | flops 9059696640 | bytes 7864320 | tf_op jit(solution)/shard_map/attn_bwd/pallas_call | solution.py:170
  502.6 20.1 %grad_out.3 = (bf16[2,384,3072]{2,1,0:T(8,128)(2,1)}, bf16[2,1024,3072]{2,1,0:T(8,128)(2,1)}) custom-call(bf16[1536,384]{1,0:T(8,128)(2,1)} %get-tuple-element.64.refs_0_.attn_ref, bf16[1536,1024]{1,0:T(8,128)(2,1)} %get-tuple-element.89.hidden_ref, bf16[1536,3072]{1,0:T(8,128)(2,1)} %get-tuple-element.90.dy_ref, ...), custom_call_target="tpu_custom_call", output_to_operand_aliasing={{0}: (3, {}), {1}: (4, {})} | custom-call | flops 13287555072 | bytes 22413312 | tf_op jit(solution)/shard_map/grad_out/pallas_call | solution.py:220
  522.7 3.5 all-gather.5.cloned.1.call-done.refs_0_
  526.3 90.8 %scatter_back.3 = (bf16[192,3072]{1,0:T(8,128)(2,1)}, f32[1,3072]{1,0:T(1,128)}) custom-call(bf16[1536,640]{1,0:T(8,128)(2,1)} %attn_bwd.3.refs_0_.refs_1_, bf16[1536,1024]{1,0:T(8,128)(2,1)} %get-tuple-element.105.refs_1_.refs_2_, bf16[1536,1024]{1,0:T(8,128)(2,1)} %get-tuple-element.106.refs_2_.refs_3_, bf16[2,3072,640]{2,1,0:T(8,128)(2,1)} %refs_3_.5, ...), custom_call_target="tpu_custom_call" | custom-call | flops 25367150592 | bytes 27131904 | tf_op jit(solution)/shard_map/scatter_back/pallas_call | solution.py:663
  617.9 1.2 collective-permute-done
  619.8 1.2 collective-permute-start.1
  621.1 2.7 collective-permute-done.1
  623.7 0.7 fusion.5
  624.5 1.9 collective-permute-start.2
  626.4 36.8 %grad_in.1 = (bf16[2,3072,640]{2,1,0:T(8,128)(2,1)}, bf16[2,3072,1024]{2,1,0:T(8,128)(2,1)}, bf16[2,3072,1024]{2,1,0:T(8,128)(2,1)}) custom-call(bf16[1536,3072]{1,0:T(8,128)(2,1)} %all-gather.5.cloned.1.call-done.refs_0_, bf16[1536,640]{1,0:T(8,128)(2,1)} %attn_bwd.3.refs_0_.refs_1_, bf16[1536,1024]{1,0:T(8,128)(2,1)} %get-tuple-element.105.refs_1_.refs_2_, ...), custom_call_target="tpu_custom_call" | custom-call | flops 25367150592 | bytes 67239936 | tf_op jit(solution)/shard_map/grad_in/pallas_call | solution.py:193
  663.9 2.4 copy.22
  (14 shorter events, 3.0 us)
Async XLA Ops:
  7.2 325.9 %all-gather.3.cloned.1.call-start = ((), (), s32[]{:S(2)}) async-start(), calls=%async_computation | async-start | bytes 10616832 | tf_op jit(solution)/shard_map/all_gather | solution.py:693
  10.3 0.6 copy-start.1
  283.3 242.9 %all-gather.5.cloned.1.call-start = ((), (), s32[]{:S(2)}) async-start(), calls=%async_computation.1 | async-start | bytes 10616832 | tf_op jit(solution)/shard_map/all_gather | solution.py:693
  526.3 90.8 %copy-start = (f32[1,3072]{1,0:T(1,128)S(1)}, f32[1,3072]{1,0:T(1,128)}, u32[]{:S(2)}) copy-start(f32[1,3072]{1,0:T(1,128)} %get-tuple-element.102) | copy-start | bytes 36868
  617.8 1.3 collective-permute-start
  619.8 3.9 collective-permute-start.1
  624.5 38.8 %collective-permute-start.2 = (f32[2,3072]{1,0:T(2,128)S(1)}, f32[2,3072]{1,0:T(2,128)S(1)}, u32[]{:S(2)}, u32[]{:S(2)}) collective-permute-start(f32[2,3072]{1,0:T(2,128)S(1)} %fusion.5), channel_id=1, source_target_pairs={{0,4},{1,5},{2,6},{3,7},{4,0},{5,1},{6,2},{7,3},{8,12},{9,13},{10,... | collective-permute-start | bytes 73736 | tf_op jit(solution)/shard_map/ppermute | solution.py:709
Sparse Core Ops, SparseCore 0:
  283.5 49.6 all-gather.2
  475.3 50.8 all-gather.4
